TPU v7x, 32 devices: a whole 2x2x4 slice. The times are simulated.
32 devices in a mesh: dp: 32 (over z, y, x, core).
Axes of the slice: x: 2, y: 2, z: 4, core: 2. Of those that a mesh axis runs over, the one named last changes fastest.
Arguments:
- images: bfloat16 [512, 14, 14, 512], P('dp'), may hold values from -6 to 6
- first_gain: bfloat16 [512], P('dp'), may hold values from 0.099609375 to 1.8984375
- first_shift: bfloat16 [512], P('dp'), may hold values from -1.75 to 1.75
- joint_weight: bfloat16 [512, 1536], P('dp'), may hold values from -0.25 to 0.25
- joint_bias: bfloat16 [2, 512], P(None, 'dp'), may hold values from -3 to 3
- output_weight: bfloat16 [512, 512], P('dp'), may hold values from -0.5 to 0.5
- output_bias: bfloat16 [512], P('dp'), may hold values from -1.75 to 1.75
- second_gain: bfloat16 [512], P('dp'), may hold values from 0.099609375 to 1.8984375
- second_shift: bfloat16 [512], P('dp'), may hold values from -1.75 to 1.75
- expand_weight: bfloat16 [512, 2048], P('dp'), may hold values from -0.25 to 0.25
- expand_bias: bfloat16 [2048], P('dp'), may hold values from -3 to 3
- reduce_weight: bfloat16 [2048, 512], P('dp'), may hold values from -0.125 to 0.125
- reduce_bias: bfloat16 [512], P('dp'), may hold values from -1.75 to 1.75
- bias_table: bfloat16 [169, 16], replicated, may hold values from -4 to 260
- regions: int32 [14, 14], replicated, may hold values from 0 to 8
- live_slots: int32 [512], P('dp'), may hold values from 0 to 1, as said below
- cotangent: bfloat16 [512, 14, 14, 512], P('dp'), may hold values from -6 to 6
Outputs:
- block_output: bfloat16 [512, 14, 14, 512], P('dp')
- input_grad: bfloat16 [512, 14, 14, 512], P('dp')
- first_gain_grad: float32 [512], P('dp')
- first_shift_grad: float32 [512], P('dp')
- joint_weight_grad: float32 [512, 1536], P('dp')
- joint_bias_grad: float32 [2, 512], P(None, 'dp')
- output_weight_grad: float32 [512, 512], P('dp')
- output_bias_grad: float32 [512], P('dp')
- second_gain_grad: float32 [512], P('dp')
- second_shift_grad: float32 [512], P('dp')
- expand_weight_grad: float32 [512, 2048], P('dp')
- expand_bias_grad: float32 [2048], P('dp')
- reduce_weight_grad: float32 [2048, 512], P('dp')
- reduce_bias_grad: float32 [512], P('dp')
- table_grad: float32 [169, 16], replicated
Inputs may be any that keep to these rules, and one draw needn't show every extreme that they name: `live_slots`: on each device the live image slots come first: the first 1 to 16 of its 16 slots hold images, and some device holds 16.
All inputs are finite; a program needn't handle non-finite values.
Results may differ from a plain program's by a relative error of at most 0.011.
Values may be sent and summed in bfloat16 or wider, within the bound.
A program may use at most 320 MiB of HBM per device.

v0:
```python
import jax
import jax.numpy as jnp
from jax import lax
from jax.sharding import PartitionSpec as P

C = 512
HEADS = 16
HEAD_DIM = 32
WIN = 7
SIDE = 14
SHIFT = 3
MB = 2
PANES = 4


epsilon = 1e-05
exact_mode = lax.Precision.HIGHEST


def norm_rows(values, gains, offset):
    center = jnp.mean(values, axis=-1, keepdims=True)
    centred = values - center
    spread = jnp.mean(centred * centred, axis=-1, keepdims=True)
    return centred * lax.rsqrt(spread + epsilon) * gains + offset


def exact_gelu(values):
    return jax.nn.gelu(values, approximate=False)


def windows_of(field):
    count = field.shape[0]
    width = field.shape[-1]
    rolled = jnp.roll(field, (-SHIFT, -SHIFT), axis=(1, 2))
    parted = rolled.reshape(count, SIDE // WIN, WIN, SIDE // WIN, WIN, width)
    return parted.transpose(0, 1, 3, 2, 4, 5).reshape(count * PANES, WIN * WIN, width)


def images_of(panes):
    count = panes.shape[0] // PANES
    width = panes.shape[-1]
    parted = panes.reshape(count, SIDE // WIN, SIDE // WIN, WIN, WIN, width).transpose(
        0, 1, 3, 2, 4, 5
    )
    return jnp.roll(parted.reshape(count, SIDE, SIDE, width), (SHIFT, SHIFT), axis=(1, 2))


def relative_index():
    cells = jnp.arange(WIN * WIN, dtype=jnp.int32)
    down = cells // WIN
    across = cells % WIN
    return (down[:, None] - down[None, :] + WIN - 1) * (2 * WIN - 1) + (
        across[:, None] - across[None, :] + WIN - 1
    )


def pane_mask(regions):
    labels = windows_of(regions[None, :, :, None])[:, :, 0]
    return jnp.where(labels[:, :, None] == labels[:, None, :], 0.0, -100.0).astype(jnp.float32)


def heads_of(panes):
    count = panes.shape[0]
    split_heads = panes.reshape(count, WIN * WIN, 3, HEADS, HEAD_DIM).transpose(2, 0, 3, 1, 4)
    return (split_heads[0], split_heads[1], split_heads[2])


def pane_scores(queries, keys, pair_bias, mask):
    count = queries.shape[0]
    raw = jnp.einsum(
        "nhid,nhjd->nhij", queries, keys, preferred_element_type=jnp.float32
    ) * HEAD_DIM ** (-0.5)
    raw = (
        raw.reshape(count // PANES, PANES, HEADS, WIN * WIN, WIN * WIN)
        + pair_bias[None, None]
        + mask[None, :, None]
    )
    return raw.reshape(count, HEADS, WIN * WIN, WIN * WIN)


def forward_pass(slab, full, pair_bias, mask):
    (
        first_gain,
        first_shift,
        joint_weight,
        joint_bias,
        output_weight,
        output_bias,
        second_gain,
        second_shift,
        expand_weight,
        expand_bias,
        reduce_weight,
        reduce_bias,
    ) = full
    count = slab.shape[0]
    source = slab.astype(jnp.float32)
    normed = norm_rows(source, first_gain.astype(jnp.float32), first_shift.astype(jnp.float32))
    normed = normed.astype(jnp.bfloat16).reshape(-1, C)
    joint_add = jnp.concatenate(
        [
            joint_bias[0].astype(jnp.float32),
            jnp.zeros((C,), jnp.float32),
            joint_bias[1].astype(jnp.float32),
        ]
    )
    joint = (jnp.dot(normed, joint_weight, preferred_element_type=jnp.float32) + joint_add).astype(
        jnp.bfloat16
    )
    panes = windows_of(joint.reshape(count, SIDE, SIDE, 3 * C))
    queries, keys, values = heads_of(panes)
    scores = pane_scores(queries, keys, pair_bias, mask)
    log_totals = jax.nn.logsumexp(scores, axis=-1, keepdims=True)
    probs = jnp.exp(scores - log_totals).astype(jnp.bfloat16)
    mixed = jnp.einsum("nhij,nhjd->nihd", probs, values, preferred_element_type=jnp.float32)
    mixed = mixed.astype(jnp.bfloat16).reshape(-1, C)
    projected = jnp.dot(
        mixed, output_weight, preferred_element_type=jnp.float32
    ) + output_bias.astype(jnp.float32)
    residual = source + images_of(projected.reshape(-1, WIN * WIN, C))
    second = norm_rows(residual, second_gain.astype(jnp.float32), second_shift.astype(jnp.float32))
    second = second.astype(jnp.bfloat16).reshape(-1, C)
    hidden = jnp.dot(
        second, expand_weight, preferred_element_type=jnp.float32
    ) + expand_bias.astype(jnp.float32)
    active = exact_gelu(hidden).astype(jnp.bfloat16)
    reduced = jnp.dot(
        active, reduce_weight, preferred_element_type=jnp.float32
    ) + reduce_bias.astype(jnp.float32)
    output = residual + reduced.reshape(residual.shape)
    kept = (normed, panes, log_totals, mixed, residual, second, hidden, active)
    return (output.astype(jnp.bfloat16), kept)


def backward_pass(slab, upstream, full, kept, pair_bias, mask, onehot):
    (
        first_gain,
        first_shift,
        joint_weight,
        joint_bias,
        output_weight,
        output_bias,
        second_gain,
        second_shift,
        expand_weight,
        expand_bias,
        reduce_weight,
        reduce_bias,
    ) = full
    normed, panes, log_totals, mixed, residual, second, hidden, active = kept
    upstream_low = upstream.reshape(-1, C).astype(jnp.bfloat16)
    reduce_weight_grad = jnp.einsum(
        "tc,tf->cf", active, upstream_low, preferred_element_type=jnp.float32
    )
    reduce_bias_grad = jnp.sum(upstream_low.astype(jnp.float32), axis=0)
    active_grad = jnp.einsum(
        "tf,cf->tc", upstream_low, reduce_weight, preferred_element_type=jnp.float32
    )
    hidden_grad = jax.vjp(exact_gelu, hidden)[1](active_grad)[0].astype(jnp.bfloat16)
    expand_weight_grad = jnp.einsum(
        "tc,tf->cf", second, hidden_grad, preferred_element_type=jnp.float32
    )
    expand_bias_grad = jnp.sum(hidden_grad.astype(jnp.float32), axis=0)
    second_grad = jnp.einsum(
        "tf,cf->tc", hidden_grad, expand_weight, preferred_element_type=jnp.float32
    )
    second_pull = jax.vjp(
        norm_rows, residual, second_gain.astype(jnp.float32), second_shift.astype(jnp.float32)
    )[1]
    residual_grad, second_gain_grad, second_shift_grad = second_pull(
        second_grad.reshape(residual.shape)
    )
    residual_grad = residual_grad + upstream
    projected_grad = windows_of(residual_grad).reshape(-1, C).astype(jnp.bfloat16)
    output_weight_grad = jnp.einsum(
        "tc,tf->cf", mixed, projected_grad, preferred_element_type=jnp.float32
    )
    output_bias_grad = jnp.sum(projected_grad.astype(jnp.float32), axis=0)
    mixed_grad = jnp.einsum(
        "tf,cf->tc", projected_grad, output_weight, preferred_element_type=jnp.float32
    )
    mixed_grad = mixed_grad.astype(jnp.bfloat16).reshape(-1, WIN * WIN, HEADS, HEAD_DIM)
    queries, keys, values = heads_of(panes)
    scores = pane_scores(queries, keys, pair_bias, mask)
    probs = jnp.exp(scores - log_totals)
    probs_low = probs.astype(jnp.bfloat16)
    values_grad = jnp.einsum(
        "nhij,nihd->njhd", probs_low, mixed_grad, preferred_element_type=jnp.float32
    )
    probs_grad = jnp.einsum(
        "nihd,nhjd->nhij", mixed_grad, values, preferred_element_type=jnp.float32
    )
    scores_grad = probs * (probs_grad - jnp.sum(probs_grad * probs, axis=-1, keepdims=True))
    scores_grad = scores_grad.astype(jnp.bfloat16)
    table_part = jnp.sum(scores_grad, axis=0, dtype=jnp.float32).reshape(
        HEADS, WIN * WIN * WIN * WIN
    )
    table_grad = jnp.dot(
        table_part, onehot, precision=exact_mode, preferred_element_type=jnp.float32
    ).T
    scale = HEAD_DIM ** (-0.5)
    queries_grad = (
        jnp.einsum("nhij,nhjd->nihd", scores_grad, keys, preferred_element_type=jnp.float32) * scale
    )
    keys_grad = (
        jnp.einsum("nhij,nhid->njhd", scores_grad, queries, preferred_element_type=jnp.float32)
        * scale
    )
    panes_grad = jnp.stack([queries_grad, keys_grad, values_grad], axis=2).reshape(
        -1, WIN * WIN, 3 * C
    )
    joint_grad = images_of(panes_grad).reshape(-1, 3 * C).astype(jnp.bfloat16)
    joint_weight_grad = jnp.einsum(
        "tc,tf->cf", normed, joint_grad, preferred_element_type=jnp.float32
    )
    column_sums = jnp.sum(joint_grad.astype(jnp.float32), axis=0)
    joint_bias_grad = jnp.stack([column_sums[:C], column_sums[2 * C :]])
    normed_grad = jnp.einsum(
        "tf,cf->tc", joint_grad, joint_weight, preferred_element_type=jnp.float32
    )
    first_pull = jax.vjp(
        norm_rows,
        slab.astype(jnp.float32),
        first_gain.astype(jnp.float32),
        first_shift.astype(jnp.float32),
    )[1]
    source_grad, first_gain_grad, first_shift_grad = first_pull(normed_grad.reshape(residual.shape))
    input_grad = (residual_grad + source_grad).astype(jnp.bfloat16)
    grads = (
        first_gain_grad,
        first_shift_grad,
        joint_weight_grad,
        joint_bias_grad,
        output_weight_grad,
        output_bias_grad,
        second_gain_grad,
        second_shift_grad,
        expand_weight_grad,
        expand_bias_grad,
        reduce_weight_grad,
        reduce_bias_grad,
    )
    return (input_grad, grads, table_grad)


def on_device(
    images,
    first_gain,
    first_shift,
    joint_weight,
    joint_bias,
    output_weight,
    output_bias,
    second_gain,
    second_shift,
    expand_weight,
    expand_bias,
    reduce_weight,
    reduce_bias,
    bias_table,
    regions,
    live_slots,
    cotangent,
):
    cells = relative_index().reshape(-1)
    offsets = jnp.arange((2 * WIN - 1) ** 2, dtype=jnp.int32)
    onehot = (cells[:, None] == offsets[None, :]).astype(jnp.float32)
    pair_bias = jnp.dot(
        onehot,
        bias_table.astype(jnp.float32),
        precision=exact_mode,
        preferred_element_type=jnp.float32,
    ).T.reshape(HEADS, WIN * WIN, WIN * WIN)
    mask = pane_mask(regions)
    upstream_all = (
        cotangent.astype(jnp.float32) * live_slots.astype(jnp.float32)[:, None, None, None]
    )
    batch = images.shape[0] // MB
    outputs = []
    input_grads = []
    totals = None
    table_total = jnp.zeros(bias_table.shape, jnp.float32)
    for index in range(MB):
        slab = images[index * batch : (index + 1) * batch]
        upstream = upstream_all[index * batch : (index + 1) * batch]
        full = (
            lax.all_gather(first_gain, "dp", axis=0, tiled=True),
            lax.all_gather(first_shift, "dp", axis=0, tiled=True),
            lax.all_gather(joint_weight, "dp", axis=0, tiled=True),
            lax.all_gather(joint_bias, "dp", axis=1, tiled=True),
            lax.all_gather(output_weight, "dp", axis=0, tiled=True),
            lax.all_gather(output_bias, "dp", axis=0, tiled=True),
            lax.all_gather(second_gain, "dp", axis=0, tiled=True),
            lax.all_gather(second_shift, "dp", axis=0, tiled=True),
            lax.all_gather(expand_weight, "dp", axis=0, tiled=True),
            lax.all_gather(expand_bias, "dp", axis=0, tiled=True),
            lax.all_gather(reduce_weight, "dp", axis=0, tiled=True),
            lax.all_gather(reduce_bias, "dp", axis=0, tiled=True),
        )
        output, kept = forward_pass(slab, full, pair_bias, mask)
        again = (
            lax.all_gather(first_gain, "dp", axis=0, tiled=True),
            lax.all_gather(first_shift, "dp", axis=0, tiled=True),
            lax.all_gather(joint_weight, "dp", axis=0, tiled=True),
            lax.all_gather(joint_bias, "dp", axis=1, tiled=True),
            lax.all_gather(output_weight, "dp", axis=0, tiled=True),
            lax.all_gather(output_bias, "dp", axis=0, tiled=True),
            lax.all_gather(second_gain, "dp", axis=0, tiled=True),
            lax.all_gather(second_shift, "dp", axis=0, tiled=True),
            lax.all_gather(expand_weight, "dp", axis=0, tiled=True),
            lax.all_gather(expand_bias, "dp", axis=0, tiled=True),
            lax.all_gather(reduce_weight, "dp", axis=0, tiled=True),
            lax.all_gather(reduce_bias, "dp", axis=0, tiled=True),
        )
        input_grad, grads, table_part = backward_pass(
            slab, upstream, again, kept, pair_bias, mask, onehot
        )
        totals = (
            grads if totals is None else tuple((left + right for left, right in zip(totals, grads)))
        )
        table_total = table_total + table_part
        outputs.append(output)
        input_grads.append(input_grad)
    totals = (
        lax.psum_scatter(totals[0], "dp", scatter_dimension=0, tiled=True),
        lax.psum_scatter(totals[1], "dp", scatter_dimension=0, tiled=True),
        lax.psum_scatter(totals[2], "dp", scatter_dimension=0, tiled=True),
        lax.psum_scatter(totals[3], "dp", scatter_dimension=1, tiled=True),
        lax.psum_scatter(totals[4], "dp", scatter_dimension=0, tiled=True),
        lax.psum_scatter(totals[5], "dp", scatter_dimension=0, tiled=True),
        lax.psum_scatter(totals[6], "dp", scatter_dimension=0, tiled=True),
        lax.psum_scatter(totals[7], "dp", scatter_dimension=0, tiled=True),
        lax.psum_scatter(totals[8], "dp", scatter_dimension=0, tiled=True),
        lax.psum_scatter(totals[9], "dp", scatter_dimension=0, tiled=True),
        lax.psum_scatter(totals[10], "dp", scatter_dimension=0, tiled=True),
        lax.psum_scatter(totals[11], "dp", scatter_dimension=0, tiled=True),
    )
    table_grad = lax.psum(table_total, "dp")
    return (
        jnp.concatenate(outputs, axis=0),
        jnp.concatenate(input_grads, axis=0),
        totals[0],
        totals[1],
        totals[2],
        totals[3],
        totals[4],
        totals[5],
        totals[6],
        totals[7],
        totals[8],
        totals[9],
        totals[10],
        totals[11],
        table_grad,
    )


def solution(mesh):
    in_specs = (
        P("dp", None, None, None),
        P("dp"),
        P("dp"),
        P("dp", None),
        P(None, "dp"),
        P("dp", None),
        P("dp"),
        P("dp"),
        P("dp"),
        P("dp", None),
        P("dp"),
        P("dp", None),
        P("dp"),
        P(),
        P(),
        P("dp"),
        P("dp", None, None, None),
    )
    out_specs = (
        P("dp", None, None, None),
        P("dp", None, None, None),
        P("dp"),
        P("dp"),
        P("dp", None),
        P(None, "dp"),
        P("dp", None),
        P("dp"),
        P("dp"),
        P("dp"),
        P("dp", None),
        P("dp"),
        P("dp", None),
        P("dp"),
        P(),
    )
    return jax.shard_map(
        on_device, mesh=mesh, in_specs=in_specs, out_specs=out_specs, check_vma=False
    )
```

profile of v0, /device:TPU:0, one launch (start us, length us, event | category | flops | bytes accessed | tf_op | source)
XLA Modules:
  0.0 1625.6 jit_solution(10181714244926879593)
XLA Ops:
  17.6 42.4 %all-reduce.15 = (bf16[512]{0:T(512)(128)(2,1)S(1)}, bf16[512]{0:T(512)(128)(2,1)S(1)}, bf16[512]{0:T(512)(128)(2,1)S(1)}, bf16[512]{0:T(512)(128)(2,1)S(1)}, bf...) all-reduce(bf16[512]{0:T(512)(128)(2,1)S(1)} %dynamic-update-slice., ...), channel_id=1, replica_groups=mesh['dp'=32] {'dp'}, use_global_device_ids=true, to_apply=%add.1 | all-reduce | flops 5120 | bytes 20480
  62.6 40.3 %all-gather = bf16[32,16,2]{1,2,0:T(2,128)(2,1)S(1)} all-gather(bf16[1,16,2]{1,2,0:T(2,128)(2,1)} %bitcast.265), channel_id=1, replica_groups=mesh['dp'=32] {'dp'}, dimensions={0}, use_global_device_ids=true | all-gather | bytes 2112 | tf_op jit(solution)/shard_map/all_gather | solution.py:290
  114.3 41.5 %all_gather.28 = bf16[512,512]{1,0:T(8,128)(2,1)} all-gather(bf16[16,512]{1,0:T(8,128)(2,1)S(1)} %copy-done.82), channel_id=1, replica_groups=mesh['dp'=32] {'dp'}, dimensions={0}, use_global_device_ids=true | all-gather | bytes 540672 | tf_op jit(solution)/shard_map/all_gather | solution.py:291
  175.1 6.8 add_convert_fusion.2
  181.9 8.2 reshape.389
  200.5 8.2 reshape.381
  222.3 9.4 copy.153
  231.7 24.4 %reshape_reshape.22 = bf16[32,49,3,16,32]{4,3,2,0,1:T(8,128)(2,1)} reshape(bf16[8,2,2,7,7,1536]{5,2,1,0,4,3:T(2,128)(2,1)} %copy.153) | data formatting | bytes 9633792 | tf_op jit(solution)/shard_map/reshape;reshape | solution.py:64
  256.1 23.4 %copy.154 = bf16[32,49,3,16,32]{1,4,3,0,2:T(8,128)(2,1)} copy(bf16[32,49,3,16,32]{4,3,2,0,1:T(8,128)(2,1)} %reshape_reshape.22) | data formatting | bytes 9633792 | tf_op jit(solution)/shard_map/reshape;reshape | solution.py:64
  279.6 13.0 fusion.99
  292.6 9.3 exponential_reduce_fusion.1
  302.0 8.7 convert_bitcast_fusion.1
  315.7 8.5 reshape.384
  350.3 9.4 copy.164
  359.7 24.4 %reshape_reshape.24 = bf16[32,49,3,16,32]{4,3,2,0,1:T(8,128)(2,1)} reshape(bf16[8,2,2,7,7,1536]{5,2,1,0,4,3:T(2,128)(2,1)} %copy.164) | data formatting | bytes 9633792 | tf_op jit(solution)/shard_map/reshape;reshape | solution.py:64
  384.1 23.5 %copy.165 = bf16[32,49,3,16,32]{1,4,3,0,2:T(8,128)(2,1)} copy(bf16[32,49,3,16,32]{4,3,2,0,1:T(8,128)(2,1)} %reshape_reshape.24) | data formatting | bytes 9633792 | tf_op jit(solution)/shard_map/reshape;reshape | solution.py:64
  407.6 13.0 fusion.100
  420.7 9.3 exponential_reduce_fusion
  430.1 8.7 convert_bitcast_fusion
  443.7 8.4 reshape.391
  475.1 5.8 fusion.105
  485.5 63.9 %multiply_convert_fusion.3 = (bf16[1568,2048]{1,0:T(8,128)(2,1)}, f32[1568,2048]{1,0:T(8,128)}, bf16[1568,2048]{1,0:T(8,128)(2,1)}, f32[1568,2048]{1,0:T(8,128)}, f32[1568,2048]{1,0:T(8,128)}) fusion(f32[2048]{0:T(1024)S(1)} %copy-done.92, f32[1568,2048]{1,0:T(8,128)S(1)} %fusion.105, bf16[1568,512]{1,0:T(8,128)(2,1)S(1)} %copy-done.56, ...), kind=kOutput, calls=%fused_computation.35 | convolution fusion | flops 3712221184 | bytes 67936256 | tf_op jit(solution)/shard_map/dot_general | solution.py:123
  549.4 6.3 convolution_add_fusion.2
  557.7 6.2 convolution_add_fusion.3
  566.0 16.1 convert_reduce_fusion.3
  584.8 5.9 fusion.103
  600.8 16.2 convert_reduce_fusion.2
  617.0 5.9 fusion.104
  628.0 9.2 multiply_reduce_fusion.3
  641.3 14.2 add_add_fusion.7
  677.0 5.9 reshape.427
  682.9 9.5 copy.189
  692.4 12.4 convolution_bitcast_fusion.1
  704.7 13.1 multiply_reduce_fusion
  717.9 14.9 convert_reduce_fusion
  732.8 8.3 multiply_bitcast_fusion
  741.0 6.7 multiply_bitcast_fusion.1
  747.7 6.4 pad_maximum_fusion.1
  754.1 22.9 %copy.194 = bf16[32,49,3,16,32]{4,3,2,0,1:T(8,128)(2,1)} copy(bf16[32,49,3,16,32]{1,4,3,0,2:T(8,128)(2,1)} %pad_maximum_fusion.1) | data formatting | bytes 9633792 | tf_op jit(solution)/shard_map/stack | solution.py:209
  777.0 26.9 %reshape_reshape.27 = bf16[8,2,2,7,7,1536]{5,2,1,0,4,3:T(2,128)(2,1)} reshape(bf16[32,49,3,16,32]{4,3,2,0,1:T(8,128)(2,1)} %copy.194) | data formatting | bytes 9633792 | tf_op jit(solution)/shard_map/reshape;reshape | solution.py:42
  814.5 5.8 reshape.426
  820.4 9.5 copy.175
  829.8 12.4 convolution_bitcast_fusion.2
  842.2 13.5 multiply_reduce_fusion.1
  855.7 14.7 convert_reduce_fusion.1
  870.4 8.3 multiply_bitcast_fusion.2
  878.7 6.7 multiply_bitcast_fusion.3
  885.4 6.3 pad_maximum_fusion
  891.7 22.9 %copy.180 = bf16[32,49,3,16,32]{4,3,2,0,1:T(8,128)(2,1)} copy(bf16[32,49,3,16,32]{1,4,3,0,2:T(8,128)(2,1)} %pad_maximum_fusion) | data formatting | bytes 9633792 | tf_op jit(solution)/shard_map/stack | solution.py:209
  914.6 26.9 %reshape_reshape.26 = bf16[8,2,2,7,7,1536]{5,2,1,0,4,3:T(2,128)(2,1)} reshape(bf16[32,49,3,16,32]{4,3,2,0,1:T(8,128)(2,1)} %copy.180) | data formatting | bytes 9633792 | tf_op jit(solution)/shard_map/reshape;reshape | solution.py:42
  960.2 8.1 fusion.42
  970.6 11.4 fusion.66
  982.1 6.2 fusion.107
  988.3 8.4 convolution_add_fusion.5
  998.2 6.1 fusion.108
  1004.3 8.7 convolution_add_fusion.4
  1022.5 5.7 fusion.102
  1035.9 6.8 fusion.53
  1044.6 37.4 %all-reduce.14 = (f32[512]{0:T(512)S(1)}, f32[512]{0:T(512)S(1)}, f32[512]{0:T(512)S(1)}, f32[512]{0:T(512)S(1)}, f32[512]{0:T(512)S(1)}, /*index=5*/f32[2048]{0:T(1024)S(1)}, f32[512]{0:T(512)S(1)}, f32[169,16]{0,1:T(8,128)}) all-reduce(f32[512]{0:T(512)S(1)} %add.396, f32[512]{0:T(512)S(1)} %add.397, ...), channel_id=2, replica_groups=mesh['dp'=32] {'dp'}, use_global_device_ids=true, to_apply=%region_24.25.clone | all-reduce | flops 7824 | bytes 62592
  1092.0 7.6 add_convert_fusion.5
  1103.1 125.3 %reduce-scatter.10.cloned.1.call-done = f32[16,512]{1,0:T(8,128)} async-done(((f32[512,512]{1,0:T(8,128)}), f32[16,512]{1,0:T(8,128)}) %reduce-scatter.10.cloned.1.call-update) | async-done | bytes 32784 | tf_op jit(solution)/shard_map/reduce_scatter | solution.py:329
  1228.4 103.9 %reduce-scatter.8.cloned.1.call-done = f32[16,1536]{1,0:T(8,128)} async-done(((f32[512,1536]{1,0:T(8,128)}), f32[16,1536]{1,0:T(8,128)}) %reduce-scatter.8.cloned.1.call-update) | async-done | bytes 98320 | tf_op jit(solution)/shard_map/reduce_scatter | solution.py:327
  1332.3 144.3 %reduce-scatter.12.cloned.1.call-done = f32[16,2048]{1,0:T(8,128)} async-done(((f32[512,2048]{1,0:T(8,128)}), f32[16,2048]{1,0:T(8,128)}) %reduce-scatter.12.cloned.1.call-update) | async-done | bytes 131088 | tf_op jit(solution)/shard_map/reduce_scatter | solution.py:333
  1476.6 141.7 %reduce-scatter.14.cloned.1.call-done = f32[64,512]{1,0:T(8,128)} async-done(((f32[2048,512]{1,0:T(8,128)}), f32[64,512]{1,0:T(8,128)}) %reduce-scatter.14.cloned.1.call-update) | async-done | bytes 131088 | tf_op jit(solution)/shard_map/reduce_scatter | solution.py:335
  (418 shorter events, 243.0 us)
Async XLA Ops:
  7.2 102.0 %copy-start = (bf16[169,16]{0,1:T(8,128)(2,1)S(1)}, bf16[169,16]{0,1:T(8,128)(2,1)}, u32[]{:S(2)}) copy-start(bf16[169,16]{0,1:T(8,128)(2,1)} %param.30) | copy-start | bytes 16228
  7.2 99.2 %copy-start.2 = (bf16[16,14,14,512]{3,0,2,1:T(8,128)(2,1)S(1)}, bf16[16,14,14,512]{3,0,2,1:T(8,128)(2,1)}, u32[]{:S(2)}) copy-start(bf16[16,14,14,512]{3,0,2,1:T(8,128)(2,1)} %param.17) | copy-start | bytes 9633796
  7.2 167.9 %all-gather.5.cloned.1.call-start = ((), (), s32[]{:S(2)}) async-start(), calls=%async_computation.5 | async-start | bytes 1622016 | tf_op jit(solution)/shard_map/all_gather | solution.py:289
  7.9 467.1 %all-gather.7.cloned.1.call-start = ((), (), s32[]{:S(2)}) async-start(), calls=%async_computation.6 | async-start | bytes 2162688 | tf_op jit(solution)/shard_map/all_gather | solution.py:295
  8.7 540.7 %all-gather.9.cloned.1.call-start = ((), (), s32[]{:S(2)}) async-start(), calls=%async_computation.7 | async-start | bytes 2162688 | tf_op jit(solution)/shard_map/all_gather | solution.py:297
  9.4 1092.3 %reduce-scatter.16.cloned.1.call-start = ((), (), s32[]{:S(2)}) async-start(), calls=%async_computation.12 | async-start | bytes 270336
  60.6 95.2 %copy-start.80 = (f32[512]{0:T(512)}, f32[512]{0:T(512)S(1)}, u32[]{:S(2)}) copy-start(f32[512]{0:T(512)S(1)} %convert_element_type.227) | copy-start | bytes 6148
  103.2 7.2 copy-start.83
  106.4 8.0 copy-start.82
  106.4 49.4 %copy-start.40 = (f32[8,14,14]{0,2,1:T(8,128)}, f32[8,14,14]{0,2,1:T(8,128)S(1)}, u32[]{:S(2)}) copy-start(f32[8,14,14]{0,2,1:T(8,128)S(1)} %get-tuple-element.155) | copy-start | bytes 18820
  106.4 49.4 %copy-start.42 = (f32[8,14,14]{0,2,1:T(8,128)}, f32[8,14,14]{0,2,1:T(8,128)S(1)}, u32[]{:S(2)}) copy-start(f32[8,14,14]{0,2,1:T(8,128)S(1)} %get-tuple-element.156) | copy-start | bytes 18820
  256.1 23.5 %copy-start.75 = (f32[4,49,49]{1,2,0:T(8,128)S(1)}, f32[4,49,49]{1,2,0:T(8,128)}, u32[]{:S(2)}) copy-start(f32[4,49,49]{1,2,0:T(8,128)} %compare_select_fusion) | copy-start | bytes 115252
  256.1 23.5 %copy-start.36 = (f32[16,49,49]{1,2,0:T(8,128)S(1)}, f32[16,49,49]{1,2,0:T(8,128)}, u32[]{:S(2)}) copy-start(f32[16,49,49]{1,2,0:T(8,128)} %copy.155) | copy-start | bytes 460996
  302.0 8.7 copy-start.27
  315.7 8.5 copy-start.73
  332.9 7.7 slice-start
  332.9 7.7 slice-start.1
  384.1 23.5 %copy-start.37 = (f32[16,49,49]{1,2,0:T(8,128)S(1)}, f32[16,49,49]{1,2,0:T(8,128)}, u32[]{:S(2)}) copy-start(f32[16,49,49]{1,2,0:T(8,128)} %copy.155) | copy-start | bytes 460996
  430.1 8.7 copy-start.29
  475.0 5.9 copy-start.25
  475.0 10.5 copy-start.56
  475.0 10.5 copy-start.92
  475.0 10.5 copy-start.96
  485.5 63.9 %copy-start.95 = (f32[512]{0:T(512)S(1)}, f32[512]{0:T(512)}, u32[]{:S(2)}) copy-start(f32[512]{0:T(512)} %convert_element_type.244) | copy-start | bytes 6148
  566.0 18.8 %copy-start.97 = (bf16[512,2048]{1,0:T(8,128)(2,1)S(1)}, bf16[512,2048]{1,0:T(8,128)(2,1)}, u32[]{:S(2)}) copy-start(bf16[512,2048]{1,0:T(8,128)(2,1)} %all-gather.7.cloned.1.call-done) | copy-start | bytes 6291460
  600.8 16.2 copy-start.98
  617.0 5.9 copy-start.24
  627.9 9.2 copy-start.68
  627.9 9.3 copy-start.11
  627.9 9.3 copy-start.48
  682.9 9.5 copy-start.30
  741.0 6.7 copy-start.17
  820.4 9.5 copy-start.28
  878.7 6.7 copy-start.18
  960.2 268.2 %reduce-scatter.10.cloned.1.call-start = ((), (), s32[]{:S(2)}) async-start(), calls=%async_computation.9 | async-start | bytes 1081344 | tf_op jit(solution)/shard_map/reduce_scatter | solution.py:329
  960.2 8.2 copy-start.53
  960.2 8.2 copy-start.59
  960.2 8.2 copy-start.103
  970.6 361.8 %reduce-scatter.8.cloned.1.call-start = ((), (), s32[]{:S(2)}) async-start(), calls=%async_computation.8 | async-start | bytes 3244032 | tf_op jit(solution)/shard_map/reduce_scatter | solution.py:327
  970.6 11.5 copy-start.57
  982.1 6.3 copy-start.26
  982.1 494.5 %reduce-scatter.12.cloned.1.call-start = ((), (), s32[]{:S(2)}) async-start(), calls=%async_computation.10 | async-start | bytes 4325376 | tf_op jit(solution)/shard_map/reduce_scatter | solution.py:333
  996.8 7.5 copy-start.55
  996.8 621.5 %reduce-scatter.14.cloned.1.call-start = ((), (), s32[]{:S(2)}) async-start(), calls=%async_computation.11 | async-start | bytes 4325376 | tf_op jit(solution)/shard_map/reduce_scatter | solution.py:335
  1013.0 8.8 copy-start.90
  1013.0 8.8 copy-start.91
  1013.0 8.8 copy-start.93
  1013.0 8.8 copy-start.94
  1013.0 8.8 copy-start.87
  1013.0 8.8 copy-start.88
  1013.0 8.8 copy-start.22
  1013.1 9.1 copy-start.20
  1022.1 6.0 slice-start.4
  1022.4 5.7 slice-start.5
  1022.4 5.7 copy-start.100
  1028.2 7.7 copy-start.13
  1035.8 7.0 copy-start.71
  1035.9 6.9 copy-start.72
  1035.9 6.9 copy-start.76
  1035.9 6.9 copy-start.84
  1035.9 7.8 copy-start.77
  1082.0 10.0 copy-start.14
  1082.0 10.0 copy-start.16
  1092.0 526.3 %copy-start.1 = (bf16[169,16]{0,1:T(8,128)(2,1)S(1)}, bf16[169,16]{0,1:T(8,128)(2,1)}, u32[]{:S(2)}) copy-start(bf16[169,16]{0,1:T(8,128)(2,1)} %param.30) | copy-start | bytes 16228
  (54 other events, 171.4 us)
Sparse Core Ops, SparseCore 0:
  10.9 57.9 all-gather.4
  71.7 55.2 all-gather.6
  129.8 55.0 all-gather.8
  960.3 132.8 reduce-scatter.15
  1095.8 132.5 reduce-scatter.9
  1234.3 98.0 reduce-scatter.7
  1335.2 141.3 reduce-scatter.11
  1479.5 138.8 reduce-scatter.13
where the time goes:
time: 1640 us; the launch traced here: 1630 us
  waiting for transfers between devices  517 us (32%)
  local copies, waits for them, and re-layouts  421 us (26%)
  matrix products  341 us (21%)
  other arithmetic  168 us (10%)
  blocking collectives  162 us (10%)
    reduce_scatter x1, waiting for transfers between devices, on_device(): lax.psum_scatter(totals[8], 'dp', scatter_dimension=0, tiled=True)  144 us
    reduce_scatter x1, waiting for transfers between devices, on_device(): lax.psum_scatter(totals[10], 'dp', scatter_dimension=0, tiled=True)  142 us
    reduce_scatter x1, waiting for transfers between devices, on_device(): lax.psum_scatter(totals[4], 'dp', scatter_dimension=0, tiled=True)  125 us
    reduce_scatter x1, waiting for transfers between devices, on_device(): lax.psum_scatter(totals[2], 'dp', scatter_dimension=0, tiled=True)  104 us
    another operation x4, local copies, waits for them, and re-layouts, heads_of(): panes.reshape(count, WIN * WIN, 3, HEADS, HEAD_DIM).transpose(2, 0, 3, 1, 4)  95.7 us
    unnamed x2, blocking collectives  79.8 us
    dot_general x2, matrix products, forward_pass(): jnp.dot(second, expand_weight, preferred_element_type=jnp.float32)  69.7 us
    another operation x4, local copies, waits for them, and re-layouts, images_of(): panes.reshape(count, SIDE // WIN, SIDE // WIN, WIN, WIN, width)  60.4 us
  transfers between devices with their start and end apart: 8, of which 4 were waited for; matrix products, arithmetic and copies ran while one was open for 31% of the time, Pallas kernels for 0%

commit v1 on v0

--- a/solution.py
+++ b/solution.py
@@ -1,17 +1,21 @@
+import functools
+
 import jax
 import jax.numpy as jnp
 from jax import lax
+from jax.experimental import pallas as pl
+from jax.experimental.pallas import tpu as pltpu
 from jax.sharding import PartitionSpec as P
 
 C = 512
 HEADS = 16
 HEAD_DIM = 32
+EXPAND = 2048
 WIN = 7
 SIDE = 14
 SHIFT = 3
-MB = 2
 PANES = 4
-
+RANKS = 32
 
 epsilon = 1e-05
 exact_mode = lax.Precision.HIGHEST
@@ -243,6 +247,329 @@
     return (input_grad, grads, table_grad)
 
 
+MESH = pl.DeviceIdType.MESH
+
+
+def place():
+    me = lax.axis_index("dp")
+    return me, me // 8, (me // 4) % 2, (me // 2) % 2, me % 2
+
+
+def rank_of(z, y, x, c):
+    return z * 8 + y * 4 + x * 2 + c
+
+
+def greet(peers):
+    barrier = pltpu.get_barrier_semaphore()
+    for peer in peers:
+        pl.semaphore_signal(barrier, inc=1, device_id=(peer,), device_id_type=MESH)
+    pl.semaphore_wait(barrier, len(peers))
+
+
+def flip(z, k):
+    low, high = z % 2, z // 2
+    if k % 2:
+        low = 1 - low
+    if k // 2:
+        high = 1 - high
+    return high * 2 + low
+
+
+def gather_kernel(groups, *refs):
+    shards = refs[:groups]
+    fulls = refs[groups : 2 * groups]
+    local, send, recv = refs[2 * groups :]
+    me, z, y, x, c = place()
+    peer_x = rank_of(z, y, 1 - x, c)
+    peer_y = rank_of(z, 1 - y, x, c)
+    mate = rank_of(z, y, x, 1 - c)
+    peers_z = [rank_of(flip(z, k), y, x, c) for k in (1, 2, 3)]
+    greet([mate, peer_x, peer_y] + peers_z)
+
+    def copy(group, lane, source, owner, target):
+        return pltpu.make_async_remote_copy(
+            src_ref=source,
+            dst_ref=fulls[group].at[owner],
+            send_sem=send.at[group, lane],
+            recv_sem=recv.at[group, lane],
+            device_id=(target,),
+            device_id_type=MESH,
+        )
+
+    def column(k, dy, dx):
+        return rank_of(flip(z, k), 1 - y if dy else y, 1 - x if dx else x, c)
+
+    def incoming(group, lane):
+        return copy(group, lane, shards[group], me, mate)
+
+    started = []
+    keep = []
+
+    def push(group, lane, source, owner, target):
+        made = copy(group, lane, source, owner, target)
+        made.start()
+        started.append(made)
+
+    for group in range(groups):
+        own = shards[group]
+        for k in (1, 2, 3):
+            push(group, k - 1, own, me, peers_z[k - 1])
+        push(group, 3, own, me, peer_x)
+        push(group, 7, own, me, peer_y)
+        push(group, 15, own, me, mate)
+        made = pltpu.make_async_copy(own, fulls[group].at[me], local.at[group])
+        made.start()
+        keep.append(made)
+    for group in range(groups):
+        full = fulls[group]
+        for k in (1, 2, 3):
+            incoming(group, k - 1).wait_recv()
+            owner = column(k, 0, 0)
+            push(group, 3 + k, full.at[owner], owner, peer_x)
+            push(group, 7 + k, full.at[owner], owner, peer_y)
+            push(group, 15 + k, full.at[owner], owner, mate)
+        for k in range(4):
+            incoming(group, 3 + k).wait_recv()
+            owner = column(k, 0, 1)
+            if k % 2 == 0:
+                push(group, 11 + k, full.at[owner], owner, peer_y)
+            push(group, 15 + 4 + k, full.at[owner], owner, mate)
+            incoming(group, 7 + k).wait_recv()
+            owner = column(k, 1, 0)
+            if k % 2 == 1:
+                push(group, 11 + k, full.at[owner], owner, peer_x)
+            push(group, 15 + 8 + k, full.at[owner], owner, mate)
+        for k in range(4):
+            incoming(group, 11 + k).wait_recv()
+            owner = column(k, 1, 1)
+            push(group, 15 + 12 + k, full.at[owner], owner, mate)
+    for group in range(groups):
+        for lane in range(15, 31):
+            incoming(group, lane).wait_recv()
+    for made in started:
+        made.wait_send()
+    for made in keep:
+        made.wait()
+
+
+def gather_all(*shards):
+    count = len(shards)
+    return pl.pallas_call(
+        functools.partial(gather_kernel, count),
+        out_shape=[jax.ShapeDtypeStruct((32,) + s.shape, s.dtype) for s in shards],
+        in_specs=[pl.BlockSpec(memory_space=pl.ANY)] * count,
+        out_specs=[pl.BlockSpec(memory_space=pl.ANY)] * count,
+        scratch_shapes=[
+            pltpu.SemaphoreType.DMA((count,)),
+            pltpu.SemaphoreType.DMA((count, 31)),
+            pltpu.SemaphoreType.DMA((count, 31)),
+        ],
+        compiler_params=pltpu.CompilerParams(collective_id=0, has_side_effects=True),
+        name="gather_shards",
+    )(*shards)
+
+
+def reduce_kernel(groups, chunks, *refs):
+    parts = refs[:groups]
+    sums_in = refs[groups]
+    outs = refs[groups + 1 : 2 * groups + 1]
+    sums_out = refs[2 * groups + 1]
+    rest = refs[2 * groups + 2 :]
+    acc, rc, r1x, r1y, r2x, r2y, rz = (rest[i * groups : (i + 1) * groups] for i in range(7))
+    vec, vecs, local, send, recv, vsend, vrecv = rest[7 * groups :]
+    me, z, y, x, c = place()
+    peer_x = rank_of(z, y, 1 - x, c)
+    peer_y = rank_of(z, 1 - y, x, c)
+    mate = rank_of(z, y, x, 1 - c)
+    peers_z = [rank_of(flip(z, k), y, x, c) for k in (1, 2, 3)]
+    greet([mate, peer_x, peer_y] + peers_z)
+    started = []
+
+    def copy(source, target_ref, sems, index, target):
+        return pltpu.make_async_remote_copy(
+            src_ref=source,
+            dst_ref=target_ref,
+            send_sem=sems[0].at[index],
+            recv_sem=sems[1].at[index],
+            device_id=(target,),
+            device_id_type=MESH,
+        )
+
+    def push(*what):
+        made = copy(*what)
+        made.start()
+        started.append(made)
+        return made
+
+    wide = (send, recv)
+    slim = (vsend, vrecv)
+    spans = []
+    first = {}
+    mine = {}
+    for group, count in enumerate(chunks):
+        rows = parts[group].shape[-2] // count
+        for index in range(count):
+            spans.append((group, index * rows, rows))
+    for number, (group, start, rows) in enumerate(spans):
+        cut = pl.ds(start, rows)
+        first[number] = push(
+            parts[group].at[:, :, :, 1 - c, cut], rc[group].at[:, :, :, cut], wide, (number, 0), mate
+        )
+        made = pltpu.make_async_copy(
+            parts[group].at[:, :, :, c, cut], acc[group].at[:, :, :, cut], local.at[number]
+        )
+        made.start()
+        mine[number] = made
+    hop = push(sums_in, vecs.at[0], slim, 0, mate)
+    hop.wait_recv()
+    vec[0] = sums_in[...] + vecs[0]
+    hop = push(vec.at[0], vecs.at[1], slim, 1, peer_x)
+
+    def add(into, where, other):
+        into[where] = (into[where].astype(jnp.float32) + other.astype(jnp.float32)).astype(jnp.bfloat16)
+
+    second = {}
+    for number, (group, start, rows) in enumerate(spans):
+        cut = pl.ds(start, rows)
+        mine[number].wait()
+        first[number].wait_recv()
+        a = acc[group]
+        for zz in range(4):
+            for yy in range(2):
+                for xx in range(2):
+                    add(a, (zz, yy, xx, cut), rc[group][zz, yy, xx, cut])
+        second[number] = (
+            push(a.at[0:2, :, 1 - x, cut], r1x[group].at[:, :, cut], wide, (number, 1), peer_x),
+            push(a.at[2:4, 1 - y, :, cut], r1y[group].at[:, :, cut], wide, (number, 2), peer_y),
+        )
+    hop.wait_recv()
+    vec[1] = vec[0] + vecs[1]
+    hop = push(vec.at[1], vecs.at[2], slim, 2, peer_y)
+    third = {}
+    for number, (group, start, rows) in enumerate(spans):
+        cut = pl.ds(start, rows)
+        for made in second[number]:
+            made.wait_recv()
+        a = acc[group]
+        for zz in range(2):
+            for other in range(2):
+                add(a, (zz, other, x, cut), r1x[group][zz, other, cut])
+                add(a, (2 + zz, y, other, cut), r1y[group][zz, other, cut])
+        third[number] = (
+            push(a.at[0:2, 1 - y, x, cut], r2y[group].at[:, cut], wide, (number, 3), peer_y),
+            push(a.at[2:4, y, 1 - x, cut], r2x[group].at[:, cut], wide, (number, 4), peer_x),
+        )
+    hop.wait_recv()
+    vec[2] = vec[1] + vecs[2]
+    hops = [push(vec.at[2], vecs.at[2 + k], slim, 2 + k, peers_z[k - 1]) for k in (1, 2, 3)]
+    fourth = {}
+    for number, (group, start, rows) in enumerate(spans):
+        cut = pl.ds(start, rows)
+        for made in third[number]:
+            made.wait_recv()
+        a = acc[group]
+        for zz in range(2):
+            add(a, (zz, y, x, cut), r2y[group][zz, cut])
+            add(a, (2 + zz, y, x, cut), r2x[group][zz, cut])
+        fourth[number] = [
+            push(
+                a.at[flip(z, k), y, x, cut],
+                rz[group].at[k - 1, cut],
+                wide,
+                (number, 4 + k),
+                peers_z[k - 1],
+            )
+            for k in (1, 2, 3)
+        ]
+    for number, (group, start, rows) in enumerate(spans):
+        cut = pl.ds(start, rows)
+        total = acc[group][z, y, x, cut].astype(jnp.float32)
+        for k in (1, 2, 3):
+            fourth[number][k - 1].wait_recv()
+            total += rz[group][k - 1, cut].astype(jnp.float32)
+        outs[group][cut, :] = total
+    for made in hops:
+        made.wait_recv()
+    sums_out[...] = (vec[2] + vecs[3]) + (vecs[4] + vecs[5])
+    for made in started:
+        made.wait_send()
+
+
+def reduce_all(parts, sums, chunks, collective_id):
+    groups = len(parts)
+    rows = [p.shape[1] for p in parts]
+    number = sum(chunks)
+    scratch = [pltpu.VMEM((4, 2, 2, r, C), jnp.bfloat16) for r in rows]
+    scratch += [pltpu.VMEM((4, 2, 2, r, C), jnp.bfloat16) for r in rows]
+    scratch += [pltpu.VMEM((2, 2, r, C), jnp.bfloat16) for r in rows]
+    scratch += [pltpu.VMEM((2, 2, r, C), jnp.bfloat16) for r in rows]
+    scratch += [pltpu.VMEM((2, r, C), jnp.bfloat16) for r in rows]
+    scratch += [pltpu.VMEM((2, r, C), jnp.bfloat16) for r in rows]
+    scratch += [pltpu.VMEM((3, r, C), jnp.bfloat16) for r in rows]
+    scratch += [
+        pltpu.VMEM((3,) + sums.shape, jnp.float32),
+        pltpu.VMEM((6,) + sums.shape, jnp.float32),
+        pltpu.SemaphoreType.DMA((number,)),
+        pltpu.SemaphoreType.DMA((number, 8)),
+        pltpu.SemaphoreType.DMA((number, 8)),
+        pltpu.SemaphoreType.DMA((6,)),
+        pltpu.SemaphoreType.DMA((6,)),
+    ]
+    return pl.pallas_call(
+        functools.partial(reduce_kernel, groups, chunks),
+        out_shape=[jax.ShapeDtypeStruct((r, C), jnp.float32) for r in rows]
+        + [jax.ShapeDtypeStruct(sums.shape, jnp.float32)],
+        in_specs=[pl.BlockSpec(memory_space=pl.ANY)] * groups
+        + [pl.BlockSpec(memory_space=pltpu.VMEM)],
+        out_specs=[pl.BlockSpec(memory_space=pltpu.VMEM)] * (groups + 1),
+        scratch_shapes=scratch,
+        compiler_params=pltpu.CompilerParams(
+            collective_id=collective_id, has_side_effects=True, vmem_limit_bytes=60 << 20
+        ),
+        name="reduce_shards",
+    )(*[p.reshape(4, 2, 2, 2, p.shape[1], C) for p in parts], sums)
+
+
+def pack_shards(joint_weight, output_weight, expand_weight, reduce_weight, vectors):
+    row = jnp.concatenate([v.reshape(-1) for v in vectors])
+    tail = jnp.zeros((16 * C - row.shape[0],), row.dtype)
+    near = jnp.concatenate(
+        [joint_weight[:, i * C : (i + 1) * C] for i in range(3)]
+        + [output_weight, jnp.concatenate([row, tail]).reshape(16, C)],
+        axis=0,
+    )
+    far = jnp.concatenate(
+        [expand_weight[:, i * C : (i + 1) * C] for i in range(4)] + [reduce_weight], axis=0
+    )
+    return near, far
+
+
+def split_blocks(packed, width):
+    return packed.reshape(RANKS, width, 16, C).transpose(0, 2, 1, 3).reshape(RANKS * 16, width * C)
+
+
+def join_blocks(grad, width):
+    return grad.reshape(RANKS, 16, width, C).transpose(0, 2, 1, 3).reshape(RANKS, width * 16, C)
+
+
+def regroup(packed, blocks, rows):
+    count = packed.shape[0]
+    return (
+        packed.reshape(RANKS, count // RANKS, blocks, rows, C)
+        .transpose(0, 2, 1, 3, 4)
+        .reshape(RANKS, blocks * rows * count // RANKS, C)
+    )
+
+
+def ungroup(parts, blocks, ranks):
+    rows = parts.shape[1] // blocks
+    return (
+        parts.reshape(RANKS, blocks, ranks // RANKS, rows * RANKS // ranks, C)
+        .transpose(0, 2, 1, 3, 4)
+        .reshape(ranks, -1, C)
+    )
+
+
 def on_device(
     images,
     first_gain,
@@ -262,6 +589,8 @@
     live_slots,
     cotangent,
 ):
+    ranks = lax.axis_size("dp")
+    me = lax.axis_index("dp")
     cells = relative_index().reshape(-1)
     offsets = jnp.arange((2 * WIN - 1) ** 2, dtype=jnp.int32)
     onehot = (cells[:, None] == offsets[None, :]).astype(jnp.float32)
@@ -272,86 +601,59 @@
         preferred_element_type=jnp.float32,
     ).T.reshape(HEADS, WIN * WIN, WIN * WIN)
     mask = pane_mask(regions)
-    upstream_all = (
-        cotangent.astype(jnp.float32) * live_slots.astype(jnp.float32)[:, None, None, None]
-    )
-    batch = images.shape[0] // MB
-    outputs = []
-    input_grads = []
-    totals = None
-    table_total = jnp.zeros(bias_table.shape, jnp.float32)
-    for index in range(MB):
-        slab = images[index * batch : (index + 1) * batch]
-        upstream = upstream_all[index * batch : (index + 1) * batch]
-        full = (
-            lax.all_gather(first_gain, "dp", axis=0, tiled=True),
-            lax.all_gather(first_shift, "dp", axis=0, tiled=True),
-            lax.all_gather(joint_weight, "dp", axis=0, tiled=True),
-            lax.all_gather(joint_bias, "dp", axis=1, tiled=True),
-            lax.all_gather(output_weight, "dp", axis=0, tiled=True),
-            lax.all_gather(output_bias, "dp", axis=0, tiled=True),
-            lax.all_gather(second_gain, "dp", axis=0, tiled=True),
-            lax.all_gather(second_shift, "dp", axis=0, tiled=True),
-            lax.all_gather(expand_weight, "dp", axis=0, tiled=True),
-            lax.all_gather(expand_bias, "dp", axis=0, tiled=True),
-            lax.all_gather(reduce_weight, "dp", axis=0, tiled=True),
-            lax.all_gather(reduce_bias, "dp", axis=0, tiled=True),
-        )
-        output, kept = forward_pass(slab, full, pair_bias, mask)
-        again = (
-            lax.all_gather(first_gain, "dp", axis=0, tiled=True),
-            lax.all_gather(first_shift, "dp", axis=0, tiled=True),
-            lax.all_gather(joint_weight, "dp", axis=0, tiled=True),
-            lax.all_gather(joint_bias, "dp", axis=1, tiled=True),
-            lax.all_gather(output_weight, "dp", axis=0, tiled=True),
-            lax.all_gather(output_bias, "dp", axis=0, tiled=True),
-            lax.all_gather(second_gain, "dp", axis=0, tiled=True),
-            lax.all_gather(second_shift, "dp", axis=0, tiled=True),
-            lax.all_gather(expand_weight, "dp", axis=0, tiled=True),
-            lax.all_gather(expand_bias, "dp", axis=0, tiled=True),
-            lax.all_gather(reduce_weight, "dp", axis=0, tiled=True),
-            lax.all_gather(reduce_bias, "dp", axis=0, tiled=True),
-        )
-        input_grad, grads, table_part = backward_pass(
-            slab, upstream, again, kept, pair_bias, mask, onehot
-        )
-        totals = (
-            grads if totals is None else tuple((left + right for left, right in zip(totals, grads)))
-        )
-        table_total = table_total + table_part
-        outputs.append(output)
-        input_grads.append(input_grad)
-    totals = (
-        lax.psum_scatter(totals[0], "dp", scatter_dimension=0, tiled=True),
-        lax.psum_scatter(totals[1], "dp", scatter_dimension=0, tiled=True),
-        lax.psum_scatter(totals[2], "dp", scatter_dimension=0, tiled=True),
-        lax.psum_scatter(totals[3], "dp", scatter_dimension=1, tiled=True),
-        lax.psum_scatter(totals[4], "dp", scatter_dimension=0, tiled=True),
-        lax.psum_scatter(totals[5], "dp", scatter_dimension=0, tiled=True),
-        lax.psum_scatter(totals[6], "dp", scatter_dimension=0, tiled=True),
-        lax.psum_scatter(totals[7], "dp", scatter_dimension=0, tiled=True),
-        lax.psum_scatter(totals[8], "dp", scatter_dimension=0, tiled=True),
-        lax.psum_scatter(totals[9], "dp", scatter_dimension=0, tiled=True),
-        lax.psum_scatter(totals[10], "dp", scatter_dimension=0, tiled=True),
-        lax.psum_scatter(totals[11], "dp", scatter_dimension=0, tiled=True),
-    )
-    table_grad = lax.psum(table_total, "dp")
+    upstream = cotangent.astype(jnp.float32) * live_slots.astype(jnp.float32)[:, None, None, None]
+    small = (first_gain, first_shift, joint_bias[0], joint_bias[1], output_bias, second_gain, second_shift, reduce_bias, expand_bias)
+    if ranks == RANKS:
+        near, far = pack_shards(joint_weight, output_weight, expand_weight, reduce_weight, small)
+        near, far = gather_all(near, far)
+        vec = near[:, 64].reshape(RANKS, C)[:, : 12 * 16]
+        vectors = [vec[:, 16 * i : 16 * i + 16].reshape(-1) for i in range(8)] + [vec[:, 128:].reshape(-1)]
+        wj = split_blocks(near[:, :48], 3)
+        wo = near[:, 48:64].reshape(C, C)
+        we = split_blocks(far[:, :64], 4)
+        wr = far[:, 64:].reshape(EXPAND, C)
+    else:
+        wj, wo, we, wr = (lax.all_gather(w, "dp", axis=0, tiled=True) for w in (joint_weight, output_weight, expand_weight, reduce_weight))
+        vectors = [lax.all_gather(v, "dp", axis=0, tiled=True) for v in small]
+    jb = jnp.stack([vectors[2], vectors[3]])
+    full = (vectors[0], vectors[1], wj, jb, wo, vectors[4], vectors[5], vectors[6], we, vectors[8], wr, vectors[7])
+    output, kept = forward_pass(images, full, pair_bias, mask)
+    input_grad, grads, table_part = backward_pass(images, upstream, full, kept, pair_bias, mask, onehot)
+    gsmall = [grads[0], grads[1], grads[3][0], grads[3][1], grads[5], grads[6], grads[7], grads[11], grads[9]]
+    if ranks == RANKS:
+        flat = jnp.concatenate(gsmall + [table_part.reshape(-1)])
+        sums = jnp.concatenate([flat, jnp.zeros((72 * 128 - flat.shape[0],), jnp.float32)]).reshape(72, 128)
+        ga = jnp.concatenate([join_blocks(grads[2], 3), grads[4].reshape(RANKS, 16, C)], axis=1).astype(jnp.bfloat16)
+        gb = jnp.concatenate([join_blocks(grads[8], 4), grads[10].reshape(RANKS, 64, C)], axis=1).astype(jnp.bfloat16)
+        gb, ga, sums = reduce_all([gb, ga], sums, (4, 2), 1)
+        sums = sums.reshape(-1)
+        own = [lax.dynamic_slice(sums, (C * i + 16 * me,), (16,)) for i in range(8)]
+        own.append(lax.dynamic_slice(sums, (C * 8 + 64 * me,), (64,)))
+        table = sums[C * 12 : C * 12 + 169 * HEADS].reshape(169, HEADS)
+        gj = ga[:48].reshape(3, 16, C).transpose(1, 0, 2).reshape(16, 3 * C)
+        go = ga[48:]
+        ge = gb[:64].reshape(4, 16, C).transpose(1, 0, 2).reshape(16, 4 * C)
+        gr = gb[64:]
+    else:
+        gj, go, ge, gr = (lax.psum_scatter(g, "dp", scatter_dimension=0, tiled=True) for g in (grads[2], grads[4], grads[8], grads[10]))
+        own = [lax.psum_scatter(g, "dp", scatter_dimension=0, tiled=True) for g in gsmall]
+        table = lax.psum(table_part, "dp")
     return (
-        jnp.concatenate(outputs, axis=0),
-        jnp.concatenate(input_grads, axis=0),
-        totals[0],
-        totals[1],
-        totals[2],
-        totals[3],
-        totals[4],
-        totals[5],
-        totals[6],
-        totals[7],
-        totals[8],
-        totals[9],
-        totals[10],
-        totals[11],
-        table_grad,
+        output,
+        input_grad,
+        own[0],
+        own[1],
+        gj,
+        jnp.stack([own[2], own[3]]),
+        go,
+        own[4],
+        own[5],
+        own[6],
+        ge,
+        own[8],
+        gr,
+        own[7],
+        table,
     )
 
 

time: 1640 us -> 1210 us (0.74)
  waiting for transfers between devices: 517 us -> 0 us
  blocking collectives: 162 us -> 0 us
  local copies, waits for them, and re-layouts: 421 us -> 562 us
  Pallas kernels: 0 us -> 93.1 us
  other arithmetic: 168 us -> 246 us
  matrix products: 341 us -> 294 us
    reduce_scatter x4 -> x0, waiting for transfers between devices: 515 us -> none  [the longest x1 144 us: on_device(): lax.psum_scatter(totals[8], 'dp', scatter_dimension=0, tiled=True)]
    pallas_call x0 -> x2, Pallas kernels: none -> 93.1 us  [the longest x1 52.1 us: reduce_all(): pl.pallas_call(functools.partial(reduce_kernel, groups, chunks), out_shap...]
    all_gather x2 -> x0, blocking collectives: 81.8 us -> none  [the longest x1 41.5 us: on_device(): lax.all_gather(output_weight, 'dp', axis=0, tiled=True)]
    unnamed x2 -> x0, blocking collectives: 79.8 us -> none
    reduce_sum x0 -> x1, other arithmetic: none -> 65.6 us  [backward_pass(): expand_bias_grad = jnp.sum(hidden_grad.astype(jnp.float32), axis=0)]
    dot_general x2 -> x1, matrix products: 69.7 us -> 13.7 us  [forward_pass(): jnp.dot(second, expand_weight, preferred_element_type=jnp.float32)]
    convert_element_type x4 -> x12, local copies, waits for them, and re-layouts: 3.62 us -> 54.5 us  [the longest x2 34.3 us: backward_pass(): joint_grad = images_of(panes_grad).reshape(-1, 3 * C).astype(jnp.bfloat16)]
    dot_general x0 -> x4, local copies, waits for them, and re-layouts: none -> 38.5 us  [the longest x1 17.8 us: backward_pass(): jnp.einsum('tf,cf->tc', hidden_grad, expand_weight, preferred_element_typ...]
  transfers between devices with their start and end apart: 8 -> 0, of which waited for: 4 -> 0; matrix products, arithmetic and copies ran while one was open for 31% -> 0% of each run, Pallas kernels for 0% -> 0%
where the time goes in v1:
time: 1210 us; the launch traced here: 1200 us
  local copies, waits for them, and re-layouts  562 us (46%)
  matrix products  294 us (24%)
  other arithmetic  246 us (20%)
  Pallas kernels  93.1 us (8%)
    another operation x2, local copies, waits for them, and re-layouts, heads_of(): panes.reshape(count, WIN * WIN, 3, HEADS, HEAD_DIM).transpose(2, 0, 3, 1, 4)  92.7 us
    dot_general x1, matrix products, backward_pass(): jnp.einsum('tf,cf->tc', upstream_low, reduce_weight, preferred_element_ty...  68.7 us
    reduce_sum x1, other arithmetic, backward_pass(): expand_bias_grad = jnp.sum(hidden_grad.astype(jnp.float32), axis=0)  65.6 us
    another operation x2, local copies, waits for them, and re-layouts, images_of(): panes.reshape(count, SIDE // WIN, SIDE // WIN, WIN, WIN, width)  60.1 us
    pallas_call x1, Pallas kernels, reduce_all(): pl.pallas_call(functools.partial(reduce_kernel, groups, chunks), out_shap...  52.1 us
    another operation x1, local copies, waits for them, and re-layouts, backward_pass(): jnp.stack([queries_grad, keys_grad, values_grad], axis=2)  44.8 us
    pallas_call x1, Pallas kernels, gather_all(): pl.pallas_call(functools.partial(gather_kernel, count), out_shape=[jax.Sh...  40.9 us
    unnamed x152, local copies, waits for them, and re-layouts  34.9 us

profile of v1, /device:TPU:0, one launch (start us, length us, event | category | flops | bytes accessed | tf_op | source)
XLA Modules:
  0.0 1197.1 jit_solution(14690384651982963641)
XLA Ops:
  4.1 4.8 concatenate.70
  19.5 5.5 convert_reduce_fusion.3
  25.1 5.2 fusion.48
  38.5 4.8 convert_reduce_fusion.4
  43.3 6.0 reshape.411
  49.4 6.0 convert_element_type.219
  55.4 40.9 %gather_shards.1 = (bf16[32,80,512]{2,1,0:T(8,128)(2,1)}, bf16[32,128,512]{2,1,0:T(8,128)(2,1)}) custom-call(bf16[80,512]{1,0:T(8,128)(2,1)} %copy-done.37, bf16[128,512]{1,0:T(8,128)(2,1)} %constant_dynamic-update-slice_fusion.5.refs_1_), custom_call_target="tpu_custom_call" | custom-call | tf_op jit(solution)/shard_map/gather_shards/pallas_call | solution.py:357
  110.8 5.6 reshape.408
  127.8 5.9 fusion.46
  133.7 4.7 reshape.374
  142.2 8.9 add_convert_fusion.1
  151.1 15.1 %reshape.377 = bf16[16,14,14,1536]{3,2,1,0:T(8,128)(2,1)} reshape(bf16[3136,1536]{1,0:T(8,128)(2,1)} %add_convert_fusion.1) | data formatting | bytes 19267584 | tf_op jit(solution)/shard_map/reshape | solution.py:114
  168.0 7.6 slice.255
  175.7 6.9 slice_maximum_fusion
  182.6 7.4 fusion.36
  190.0 14.0 %copy.162 = bf16[16,14,14,1536]{3,0,2,1:T(8,128)(2,1)} copy(bf16[16,14,14,1536]{3,2,1,0:T(8,128)(2,1)} %fusion.36) | data formatting | bytes 19267584 | tf_op jit(solution)/shard_map/jit(_roll_static)/concatenate | solution.py:38
  204.0 18.7 %copy.163 = bf16[16,2,2,7,7,1536]{5,2,1,0,4,3:T(2,128)(2,1)} copy(bf16[16,2,2,7,7,1536]{5,0,4,2,3,1:T(8,128)(2,1)} %bitcast.274) | data formatting | bytes 19267584 | tf_op jit(solution)/shard_map/transpose | solution.py:40
  222.7 47.2 %reshape_reshape.11 = bf16[64,49,3,16,32]{4,3,2,0,1:T(8,128)(2,1)} reshape(bf16[16,2,2,7,7,1536]{5,2,1,0,4,3:T(2,128)(2,1)} %copy.163) | data formatting | bytes 19267584 | tf_op jit(solution)/shard_map/reshape;reshape | solution.py:68
  269.9 45.5 %copy.164 = bf16[64,49,3,16,32]{1,4,3,0,2:T(8,128)(2,1)} copy(bf16[64,49,3,16,32]{4,3,2,0,1:T(8,128)(2,1)} %reshape_reshape.11) | data formatting | bytes 19267584 | tf_op jit(solution)/shard_map/reshape;reshape | solution.py:68
  315.4 19.1 %fusion.89 = (f32[64,16,49]{2,1,0:T(8,128)S(1)}, f32[64,16,49,49]{2,3,1,0:T(8,128)}) fusion(f32[64,49,49]{1,2,0:T(8,128)S(1)} %bitcast.293, f32[16,49,49]{1,2,0:T(8,128)S(1)} %copy-done.17, bf16[3,64,16,49,32]{3,4,2,1,0:T(8,128)(2,1)} %bitcast.263), kind=kOutput, calls=%fused_computation.195 | convolution fusion | flops 167136256 | bytes 27580736 | tf_op jit(solution)/shard_map/nhid,nhjd->nhij/dot_general | solution.py:74
  334.5 16.3 %exponential_reduce_fusion = f32[64,16,49]{2,1,0:T(8,128)S(1)} fusion(f32[64,16,49,49]{2,3,1,0:T(8,128)} %get-tuple-element.133, f32[64,16,49]{2,1,0:T(8,128)S(1)} %is-finite_select_fusion), kind=kLoop, calls=%fused_computation.7 | loop fusion | flops 4867072 | bytes 10235904 | tf_op jit(solution)/shard_map/reduce_sum | solution.py:117
  351.7 17.5 %convert_bitcast_fusion = bf16[64,49,16,32]{1,3,2,0:T(8,128)(2,1)} fusion(bf16[3,64,16,49,32]{3,4,2,1,0:T(8,128)(2,1)} %bitcast.264, f32[64,16,49,49]{2,3,1,0:T(8,128)} %get-tuple-element.133, f32[64,16,49]{2,1,0:T(8,128)S(1)} %log_add_fusion), kind=kOutput, calls=%fused_computation.87 | convolution fusion | flops 163874816 | bytes 41160704 | tf_op jit(solution)/shard_map/nhij,nhjd->nihd/dot_general | solution.py:119
  369.3 12.0 %copy.168 = bf16[64,49,16,32]{1,0,3,2:T(8,128)(2,1)} copy(bf16[64,49,16,32]{1,3,2,0:T(8,128)(2,1)} %convert_bitcast_fusion) | data formatting | bytes 6422528 | tf_op jit(solution)/shard_map/convert_element_type | solution.py:120
  381.3 12.0 reshape.380
  393.2 6.0 convolution_add_fusion
  399.2 8.1 reshape_reshape.12
  407.3 8.8 copy.169
  421.2 5.2 fusion.84
  441.3 13.7 %fusion.91 = f32[3136,2048]{1,0:T(8,128)} fusion(bf16[3136,512]{1,0:T(8,128)(2,1)S(1)} %reshape.383, bf16[512,2048]{1,0:T(8,128)(2,1)} %bitcast.300), kind=kOutput, calls=%fused_computation.197 | convolution fusion | flops 6576668672 | bytes 30998528 | tf_op jit(solution)/shard_map/dot_general | solution.py:127
  455.1 68.7 %fusion.8 = (bf16[2048,3136]{0,1:T(8,128)(2,1)}, f32[2048,3136]{0,1:T(8,128)}, f32[3136,2048]{1,0:T(8,128)}) fusion(f32[3136,2048]{1,0:T(8,128)} %fusion.91, f32[2048]{0:T(1024)S(1)} %copy-done.38, bf16[3136,512]{1,0:T(8,128)(2,1)S(1)} %copy-done.23, bf16[2048,512]{1,0:T(8,128)(2,1)S(1)} %bitcast.302), kind=kOutput, calls=%fused_computation.23 | convolution fusion | flops 7045513216 | bytes 95232000 | tf_op jit(solution)/shard_map/tf,cf->tc/dot_general | solution.py:160
  523.8 12.3 %fusion.65 = bf16[32,16,4,512]{3,1,2,0:T(8,128)(2,1)} fusion(bf16[32,16,3136,1]{2,1,3,0:T(8,128)(2,1)} %bitcast.299, bf16[392,4,8,512]{3,2,1,0:T(8,128)(2,1)} %bitcast.321), kind=kOutput, calls=%fused_computation.128 | convolution fusion | flops 6577717248 | bytes 18153472 | tf_op jit(solution)/shard_map/tc,tf->cf/dot_general | solution.py:164
  537.5 15.1 %fusion.10 = bf16[2048,3136]{0,1:T(8,128)(2,1)} fusion(f32[2048,3136]{0,1:T(8,128)} %get-tuple-element.101, f32[3136,2048]{1,0:T(8,128)S(1)} %copy-done.6, f32[2048]{0:T(1024)S(1)} %copy-done.38), kind=kLoop, calls=%fused_computation.26 | loop fusion | flops 25690112 | bytes 64233472 | tf_op jit(solution)/shard_map/convert_element_type | solution.py:130
  552.6 17.1 %copy.187 = bf16[2048,3136]{1,0:T(8,128)(2,1)} copy(bf16[2048,3136]{0,1:T(8,128)(2,1)} %fusion.10) | data formatting | bytes 25690112 | tf_op jit(solution)/shard_map/convert_element_type | solution.py:130
  569.7 12.3 %fusion.62 = bf16[4,2,2,2,64,512]{5,4,3,2,1,0:T(8,128)(2,1)} fusion(bf16[4,2,2,2,64,3136]{5,4,3,2,1,0:T(8,128)(2,1)} %bitcast.290, bf16[3136,512,1,1,1,1]{1,0,2,3,4,5:T(8,128)(2,1)} %reshape.411), kind=kOutput, calls=%fused_computation.127 | convolution fusion | flops 6577717248 | bytes 18153472 | tf_op jit(solution)/shard_map/tc,tf->cf/dot_general | solution.py:156
  582.0 5.0 pad_maximum_fusion.4.refs_0_
  587.1 65.6 %convert_reduce_fusion.1 = (f32[2048]{0:T(1024)}, bf16[3136,2048]{1,0:T(8,128)(2,1)}, f32[3136,2048]{1,0:T(8,128)}) fusion(f32[3136,2048]{1,0:T(8,128)} %get-tuple-element.134, f32[3136,2048]{1,0:T(8,128)S(1)} %bitcast.271, f32[2048]{0:T(1024)S(1)} %copy-done.38), kind=kLoop, calls=%fused_computation.27 | loop fusion | flops 481687552 | bytes 89931776 | tf_op jit(solution)/shard_map/reduce_sum | solution.py:167
  652.7 21.6 %fusion.51 = f32[3136,512]{1,0:T(8,128)} fusion(bf16[2048,512]{1,0:T(8,128)(2,1)} %bitcast.301, f32[3136,2048]{1,0:T(8,128)} %get-tuple-element.95, f32[3136,2048]{1,0:T(8,128)} %fusion.91, f32[2048]{0:T(1024)S(1)} %copy-done.38, f32[512]{0:T(512)S(1)} %copy-done.52), kind=kOutput, calls=%fused_computation.111 | convolution fusion | flops 6603964416 | bytes 59910144 | tf_op jit(solution)/shard_map/dot_general | solution.py:131
  674.3 7.7 reshape.387
  682.0 17.8 %dot_general.93 = bf16[16,14,14,2048]{3,2,1,0:T(8,128)(2,1)} reshape(bf16[3136,2048]{1,0:T(8,128)(2,1)} %get-tuple-element.94) | data formatting | bytes 25690112 | tf_op jit(solution)/shard_map/tf,cf->tc/dot_general | solution.py:168
  699.8 17.7 %fusion.79 = (f32[512]{0:T(512)}, f32[16,14,14]{2,1,0:T(8,128)S(1)}, f32[16,14,14,512]{3,2,1,0:T(8,128)S(1)}) fusion(f32[512]{0:T(512)S(1)} %copy-done.42, f32[16,14,14,512]{3,2,1,0:T(8,128)} %copy-done.2, f32[16,14,14]{2,1,0:T(8,128)S(1)} %copy-done.19, bf16[16,14,14,2048]{3,2,1,0:T(8,128)(2,1)} %dot_general.93, bf16[512,2048,1,1]{1,0,2,3:T(8,128)(2,1)} %reshape.407), kind=kOutput, calls=%fused_computation.189 | convolution fusion | flops 6584693248 | bytes 27816448 | tf_op jit(solution)/shard_map/tf,cf->tc/dot_general | solution.py:168
  722.2 6.8 add_add_fusion.3
  729.0 8.5 copy.197
  749.1 6.3 reshape.414
  760.1 4.8 convert_element_type.223
  769.4 15.0 %reshape.419 = bf16[64,49,16,32]{3,2,1,0:T(8,128)(2,1)} reshape(bf16[3136,512]{1,0:T(8,128)(2,1)} %convolution_convert_fusion) | data formatting | bytes 6422528 | tf_op jit(solution)/shard_map/reshape | solution.py:186
  784.5 17.7 %copy.177 = bf16[64,49,16,32]{1,3,2,0:T(8,128)(2,1)} copy(bf16[64,49,16,32]{3,2,1,0:T(8,128)(2,1)} %reshape.419) | data formatting | bytes 6422528 | tf_op jit(solution)/shard_map/reshape | solution.py:186
  802.1 18.5 %convolution_bitcast_fusion = bf16[64,49,1,16,32]{1,4,3,0,2:T(8,128)(2,1)} fusion(bf16[64,49,16,32]{1,3,2,0:T(8,128)(2,1)} %copy.177, f32[64,16,49,49]{2,3,1,0:T(8,128)} %get-tuple-element.133, f32[64,16,49]{2,1,0:T(8,128)S(1)} %copy-done.12), kind=kOutput, calls=%fused_computation.83 | convolution fusion | flops 162269184 | bytes 16457728 | tf_op jit(solution)/shard_map/nhij,nihd->njhd/dot_general | solution.py:191
  820.7 25.1 %multiply_reduce_fusion = (f32[64,16,49]{2,1,0:T(8,128)S(1)}, f32[64,16,49,49]{2,3,1,0:T(8,128)}) fusion(f32[64,16,49,49]{2,3,1,0:T(8,128)} %get-tuple-element.133, f32[64,16,49]{2,1,0:T(8,128)S(1)} %copy-done.12, bf16[64,49,16,32]{1,3,2,0:T(8,128)(2,1)} %copy.177, bf16[3,64,16,49,32]{3,4,2,1,0:T(8,128)(2,1)} %bitcast.265), kind=kOutput, calls=%fused_computation.5 | convolution fusion | flops 164677632 | bytes 56373248 | tf_op jit(solution)/shard_map/nihd,nhjd->nhij/dot_general | solution.py:194
  845.8 27.0 %convert_reduce_fusion = (f32[16,49,49]{1,2,0:T(8,128)S(1)}, bf16[64,16,49,49]{2,3,1,0:T(8,128)(2,1)}) fusion(f32[64,16,49,49]{2,3,1,0:T(8,128)} %get-tuple-element.137, f32[64,16,49]{2,1,0:T(8,128)S(1)} %get-tuple-element.136, f32[64,16,49,49]{2,3,1,0:T(8,128)} %get-tuple-element.133, f32[64,16,49]{2,1,0:T(8,128)S(1)} %copy-done.12), kind=kLoop, calls=%fused_computation.3 | loop fusion | flops 14713328 | bytes 25141312 | tf_op jit(solution)/shard_map/reduce_sum | solution.py:199
  875.2 14.3 %multiply_bitcast_fusion = bf16[64,49,1,16,32]{1,4,3,0,2:T(8,128)(2,1)} fusion(bf16[64,16,49,49]{2,3,1,0:T(8,128)(2,1)} %get-tuple-element.92, bf16[3,64,16,49,32]{3,4,2,1,0:T(8,128)(2,1)} %bitcast.266), kind=kOutput, calls=%fused_computation.63 | convolution fusion | flops 160563200 | bytes 26279936 | tf_op jit(solution)/shard_map/nhij,nhid->njhd/dot_general | solution.py:210
  889.5 12.2 %multiply_bitcast_fusion.1 = bf16[64,49,1,16,32]{1,4,3,0,2:T(8,128)(2,1)} fusion(bf16[64,16,49,49]{2,3,1,0:T(8,128)(2,1)} %get-tuple-element.92, bf16[3,64,16,49,32]{3,4,2,1,0:T(8,128)(2,1)} %bitcast.267), kind=kOutput, calls=%fused_computation.64 | convolution fusion | flops 160563200 | bytes 26279936 | tf_op jit(solution)/shard_map/nhij,nhjd->nihd/dot_general | solution.py:207
  901.7 17.4 %pad_maximum_fusion = bf16[64,49,3,16,32]{1,4,3,0,2:T(8,128)(2,1)} fusion(bf16[64,49,1,16,32]{1,4,3,0,2:T(8,128)(2,1)} %convolution_bitcast_fusion, bf16[64,49,1,16,32]{1,4,3,0,2:T(8,128)(2,1)} %multiply_bitcast_fusion, bf16[64,49,1,16,32]{1,4,3,0,2:T(8,128)(2,1)} %multiply_bitcast_fusion.1), kind=kLoop, calls=%fused_computation | loop fusion | flops 9633792 | bytes 19267584 | tf_op jit(solution)/shard_map/stack | solution.py:213
  919.0 44.8 %copy.182 = bf16[64,49,3,16,32]{4,3,2,0,1:T(8,128)(2,1)} copy(bf16[64,49,3,16,32]{1,4,3,0,2:T(8,128)(2,1)} %pad_maximum_fusion) | data formatting | bytes 19267584 | tf_op jit(solution)/shard_map/stack | solution.py:213
  963.8 52.0 %reshape_reshape.13 = bf16[16,2,2,7,7,1536]{5,2,1,0,4,3:T(2,128)(2,1)} reshape(bf16[64,49,3,16,32]{4,3,2,0,1:T(8,128)(2,1)} %copy.182) | data formatting | bytes 19267584 | tf_op jit(solution)/shard_map/reshape;reshape | solution.py:46
  1015.8 9.8 copy.183
  1034.2 5.2 fusion.90
  1039.5 9.3 fusion.49
  1048.9 10.8 fusion.47
  1061.5 12.2 %add_convert_fusion.2 = bf16[16,14,14,512]{3,2,1,0:T(8,128)(2,1)S(1)} fusion(f32[16,14,14,512]{3,2,1,0:T(8,128)} %copy-done.9, f32[16,14,14]{2,1,0:T(8,128)S(1)} %negate_multiply_fusion.1, f32[16,14,14]{2,1,0:T(8,128)} %copy-done.31, f32[16,14,14]{2,1,0:T(8,128)S(1)} %copy-done.16, f32[16,14,14]{2,1,0:T(8,128)S(1)} %copy-done.25, f32[512]{0:T(512)S(1)} %copy-done.40, ...), kind=kLoop, calls=%fused_computation.101 | loop fusion | flops 16056320 | bytes 19319808 | tf_op jit(solution)/shard_map/convert_element_type | solution.py:232
  1077.5 19.1 %copy.189 = bf16[16,14,14,1536]{3,2,1,0:T(8,128)(2,1)} copy(bf16[16,14,14,1536]{3,0,2,1:T(8,128)(2,1)S(1)} %bitcast.273) | data formatting | bytes 19267584 | tf_op jit(solution)/shard_map/convert_element_type | solution.py:216
  1096.7 15.2 %convert_element_type.230 = bf16[3136,1536]{1,0:T(8,128)(2,1)} reshape(bf16[16,14,14,1536]{3,2,1,0:T(8,128)(2,1)} %copy.189) | data formatting | bytes 19267584 | tf_op jit(solution)/shard_map/convert_element_type | solution.py:216
  1111.8 13.0 %copy.190 = bf16[1536,3136]{1,0:T(8,128)(2,1)} copy(bf16[1536,3136]{0,1:T(8,128)(2,1)} %bitcast.275) | data formatting | bytes 19267584 | tf_op jit(solution)/shard_map/tc,tf->cf/dot_general | solution.py:217
  1124.9 8.2 convolution_convert_fusion.1
  1134.6 52.1 %reduce_shards.1 = (f32[128,512]{1,0:T(8,128)}, f32[64,512]{1,0:T(8,128)}, f32[72,128]{1,0:T(8,128)}) custom-call(bf16[4,2,2,2,128,512]{5,4,3,2,1,0:T(8,128)(2,1)} %pad_maximum_fusion.4.refs_0_, bf16[4,2,2,2,64,512]{5,4,3,2,1,0:T(8,128)(2,1)} %pad_maximum_fusion.6.refs_1_, f32[72,128]{1,0:T(8,128)} %bitcast.313), custom_call_target="tpu_custom_call" | custom-call | tf_op jit(solution)/shard_map/reduce_shards/pallas_call | solution.py:518
  (250 shorter events, 129.5 us)
Async XLA Ops:
  0.6 30.3 %copy-start = (bf16[169,16]{0,1:T(8,128)(2,1)S(1)}, bf16[169,16]{0,1:T(8,128)(2,1)}, u32[]{:S(2)}) copy-start(bf16[169,16]{0,1:T(8,128)(2,1)} %param.30) | copy-start | bytes 16228
  0.7 37.9 %copy-start.13 = (bf16[16,14,14,512]{3,0,2,1:T(8,128)(2,1)S(1)}, bf16[16,14,14,512]{3,0,2,1:T(8,128)(2,1)}, u32[]{:S(2)}) copy-start(bf16[16,14,14,512]{3,0,2,1:T(8,128)(2,1)} %param.33) | copy-start | bytes 9633796
  1.5 47.9 %copy-start.50 = (f32[16]{0:T(128)}, f32[16]{0:T(128)S(1)}, u32[]{:S(2)}) copy-start(f32[16]{0:T(128)S(1)} %convert_element_type.217) | copy-start | bytes 196
  9.1 40.3 %copy-start.44 = (s32[2401]{0:T(1024)}, s32[2401]{0:T(1024)S(1)}, u32[]{:S(2)}) copy-start(s32[2401]{0:T(1024)S(1)} %add.234) | copy-start | bytes 28816
  12.0 6.0 copy-start.37
  25.1 102.7 %copy-start.15 = (f32[16,14,14]{2,1,0:T(8,128)}, f32[16,14,14]{2,1,0:T(8,128)S(1)}, u32[]{:S(2)}) copy-start(f32[16,14,14]{2,1,0:T(8,128)S(1)} %broadcast_multiply_fusion.1) | copy-start | bytes 37636
  30.9 96.8 %copy-start.24 = (f32[16,14,14]{2,1,0:T(8,128)}, f32[16,14,14]{2,1,0:T(8,128)S(1)}, u32[]{:S(2)}) copy-start(f32[16,14,14]{2,1,0:T(8,128)S(1)} %fusion.76) | copy-start | bytes 37636
  96.4 7.4 copy-start.29
  106.0 21.7 %copy-start.39 = (f32[512]{0:T(512)}, f32[512]{0:T(512)S(1)}, u32[]{:S(2)}) copy-start(f32[512]{0:T(512)S(1)} %reshape.398) | copy-start | bytes 6148
  108.0 19.8 %copy-start.3 = (bf16[16,14,14,512]{3,0,2,1:T(8,128)(2,1)S(1)}, bf16[16,14,14,512]{3,0,2,1:T(8,128)(2,1)}, u32[]{:S(2)}) copy-start(bf16[16,14,14,512]{3,0,2,1:T(8,128)(2,1)} %param.17) | copy-start | bytes 9633796
  175.7 6.9 copy-start.7
  269.9 45.5 %copy-start.14 = (f32[16,4,49,49]{2,3,1,0:T(8,128)S(1)}, f32[16,4,49,49]{2,3,1,0:T(8,128)}, u32[]{:S(2)}) copy-start(f32[16,4,49,49]{2,3,1,0:T(8,128)} %add.238) | copy-start | bytes 1843972
  269.9 45.5 %copy-start.17 = (f32[16,49,49]{1,2,0:T(8,128)S(1)}, f32[16,49,49]{1,2,0:T(8,128)}, u32[]{:S(2)}) copy-start(f32[16,49,49]{1,2,0:T(8,128)} %copy.165) | copy-start | bytes 460996
  393.2 14.1 %copy-start.21 = (bf16[3136,512]{0,1:T(8,128)(2,1)}, bf16[3136,512]{0,1:T(8,128)(2,1)S(1)}, u32[]{:S(2)}) copy-start(bf16[3136,512]{0,1:T(8,128)(2,1)S(1)} %reshape.380) | copy-start | bytes 9633796
  416.8 4.4 copy-start.4
  421.2 9.1 copy-start.41
  421.2 9.0 copy-start.48
  426.4 3.1 copy-start.2
  426.5 3.1 copy-start.18
  441.3 13.7 %copy-start.23 = (bf16[3136,512]{1,0:T(8,128)(2,1)S(1)}, bf16[3136,512]{1,0:T(8,128)(2,1)}, u32[]{:S(2)}) copy-start(bf16[3136,512]{1,0:T(8,128)(2,1)} %convert_element_type.219) | copy-start | bytes 9633796
  441.3 13.7 %copy-start.28 = (bf16[32,64,512]{2,1,0:T(8,128)(2,1)S(1)}, bf16[32,64,512]{2,1,0:T(8,128)(2,1)}, u32[]{:S(2)}) copy-start(bf16[32,64,512]{2,1,0:T(8,128)(2,1)} %get-tuple-element.107) | copy-start | bytes 6291460
  441.3 13.7 %copy-start.38 = (f32[2048]{0:T(1024)S(1)}, f32[2048]{0:T(1024)}, u32[]{:S(2)}) copy-start(f32[2048]{0:T(1024)} %reshape.405) | copy-start | bytes 24580
  523.8 13.7 %copy-start.6 = (f32[3136,2048]{1,0:T(8,128)S(1)}, f32[3136,2048]{1,0:T(8,128)}, u32[]{:S(2)}) copy-start(f32[3136,2048]{1,0:T(8,128)} %fusion.91) | copy-start | bytes 77070336
  569.7 17.3 %slice-start.2 = ((s8[25690112]{0:T(1024)(128)(4,1)}), s8[4194304]{0:T(1024)(128)(4,1)S(1)}, s32[]{:S(2)}) async-start(s8[25690112]{0:T(1024)(128)(4,1)} %bitcast.270), calls=%async_computation.2 | async-start | bytes 8388608
  569.7 17.3 %slice-start.3 = ((s8[25690112]{0:T(1024)(128)(4,1)}), s8[4194304]{0:T(1024)(128)(4,1)S(1)}, s32[]{:S(2)}) async-start(s8[25690112]{0:T(1024)(128)(4,1)} %bitcast.270), calls=%async_computation.3 | async-start | bytes 8388608
  569.7 17.3 %slice-start.4 = ((s8[25690112]{0:T(1024)(128)(4,1)}), s8[4194304]{0:T(1024)(128)(4,1)S(1)}, s32[]{:S(2)}) async-start(s8[25690112]{0:T(1024)(128)(4,1)} %bitcast.270), calls=%async_computation.4 | async-start | bytes 8388608
  569.7 17.3 %slice-start.5 = ((s8[25690112]{0:T(1024)(128)(4,1)}), s8[4194304]{0:T(1024)(128)(4,1)S(1)}, s32[]{:S(2)}) async-start(s8[25690112]{0:T(1024)(128)(4,1)} %bitcast.270), calls=%async_computation.5 | async-start | bytes 8388608
  569.7 17.3 %slice-start.6 = ((s8[25690112]{0:T(1024)(128)(4,1)}), s8[4194304]{0:T(1024)(128)(4,1)S(1)}, s32[]{:S(2)}) async-start(s8[25690112]{0:T(1024)(128)(4,1)} %bitcast.270), calls=%async_computation.6 | async-start | bytes 8388608
  569.7 17.3 %slice-start.7 = ((s8[25690112]{0:T(1024)(128)(4,1)}), s8[4194304]{0:T(1024)(128)(4,1)S(1)}, s32[]{:S(2)}) async-start(s8[25690112]{0:T(1024)(128)(4,1)} %bitcast.270), calls=%async_computation.7 | async-start | bytes 8388608
  582.0 5.0 slice-start.8
  587.1 65.7 %copy-start.52 = (f32[512]{0:T(512)S(1)}, f32[512]{0:T(512)}, u32[]{:S(2)}) copy-start(f32[512]{0:T(512)} %reshape.406) | copy-start | bytes 6148
  682.0 17.8 %copy-start.19 = (f32[16,14,14]{2,1,0:T(8,128)S(1)}, f32[16,14,14]{2,1,0:T(8,128)}, u32[]{:S(2)}) copy-start(f32[16,14,14]{2,1,0:T(8,128)} %copy-done.18) | copy-start | bytes 37636
  682.0 17.8 %copy-start.42 = (f32[512]{0:T(512)S(1)}, f32[512]{0:T(512)}, u32[]{:S(2)}) copy-start(f32[512]{0:T(512)} %reshape.403) | copy-start | bytes 6148
  682.0 35.6 %slice-start = ((s8[7340032]{0:T(1024)(128)(4,1)}), s8[3145728]{0:T(1024)(128)(4,1)S(1)}, s32[]{:S(2)}) async-start(s8[7340032]{0:T(1024)(128)(4,1)} %bitcast.268), calls=%async_computation | async-start | bytes 6291456
  699.8 17.8 %copy-start.35 = (f32[16,14,14]{2,1,0:T(8,128)S(1)}, f32[16,14,14]{2,1,0:T(8,128)}, u32[]{:S(2)}) copy-start(f32[16,14,14]{2,1,0:T(8,128)} %copy-done.34) | copy-start | bytes 37636
  699.8 17.8 %slice-start.1 = ((s8[7340032]{0:T(1024)(128)(4,1)}), s8[4194304]{0:T(1024)(128)(4,1)S(1)}, s32[]{:S(2)}) async-start(s8[7340032]{0:T(1024)(128)(4,1)} %bitcast.268), calls=%async_computation.1 | async-start | bytes 8388608
  699.8 17.8 %copy-start.27 = (f32[16,14,14]{2,1,0:T(8,128)S(1)}, f32[16,14,14]{2,1,0:T(8,128)}, u32[]{:S(2)}) copy-start(f32[16,14,14]{2,1,0:T(8,128)} %copy-done.26) | copy-start | bytes 37636
  717.5 4.6 slice-start.12
  717.5 4.6 copy-start.51
  717.6 4.5 slice-start.13
  729.0 8.6 copy-start.9
  744.5 11.0 copy-start.22
  784.5 17.7 %copy-start.12 = (f32[64,16,49]{2,1,0:T(8,128)S(1)}, f32[64,16,49]{2,1,0:T(8,128)}, u32[]{:S(2)}) copy-start(f32[64,16,49]{2,1,0:T(8,128)} %copy-done.11) | copy-start | bytes 602116
  845.8 27.5 %copy-start.45 = (s32[2401]{0:T(1024)S(1)}, s32[2401]{0:T(1024)}, u32[]{:S(2)}) copy-start(s32[2401]{0:T(1024)} %copy-done.44) | copy-start | bytes 28816
  1031.1 3.0 copy-start.30
  1034.1 5.3 copy-start.10
  1034.1 5.3 copy-start.5
  1034.1 5.3 copy-start.16
  1034.1 5.3 copy-start.40
  1039.4 20.3 %copy-start.8 = (f32[16,14,14,512]{3,0,2,1:T(8,128)}, f32[16,14,14,512]{3,0,2,1:T(8,128)S(1)}, u32[]{:S(2)}) copy-start(f32[16,14,14,512]{3,0,2,1:T(8,128)S(1)} %get-tuple-element.139) | copy-start | bytes 19267588
  1039.4 9.4 copy-start.33
  1039.4 9.4 copy-start.25
  1039.4 20.3 %copy-start.43 = (f32[2048]{0:T(1024)S(1)}, f32[2048]{0:T(1024)}, u32[]{:S(2)}) copy-start(f32[2048]{0:T(1024)} %get-tuple-element.93) | copy-start | bytes 24580
  1039.5 20.3 %copy-start.46 = (f32[512]{0:T(512)S(1)}, f32[512]{0:T(512)}, u32[]{:S(2)}) copy-start(f32[512]{0:T(512)} %get-tuple-element.96) | copy-start | bytes 6148
  1039.5 20.3 %copy-start.47 = (f32[512]{0:T(512)S(1)}, f32[512]{0:T(512)}, u32[]{:S(2)}) copy-start(f32[512]{0:T(512)} %get-tuple-element.85) | copy-start | bytes 6148
  1039.5 20.3 %copy-start.49 = (f32[512]{0:T(512)S(1)}, f32[512]{0:T(512)}, u32[]{:S(2)}) copy-start(f32[512]{0:T(512)} %convert_reduce_fusion.5) | copy-start | bytes 6148
  1039.5 20.3 %copy-start.53 = (f32[512]{0:T(512)S(1)}, f32[512]{0:T(512)}, u32[]{:S(2)}) copy-start(f32[512]{0:T(512)} %get-tuple-element.89) | copy-start | bytes 6148
  1048.8 10.9 copy-start.31
  1060.4 17.1 %slice-start.9 = ((s8[9633792]{0:T(1024)(128)(4,1)}), s8[4194304]{0:T(1024)(128)(4,1)S(1)}, s32[]{:S(2)}) async-start(s8[9633792]{0:T(1024)(128)(4,1)} %bitcast.272), calls=%async_computation.9 | async-start | bytes 8388608
  1061.5 16.0 %slice-start.10 = ((s8[9633792]{0:T(1024)(128)(4,1)}), s8[4194304]{0:T(1024)(128)(4,1)S(1)}, s32[]{:S(2)}) async-start(s8[9633792]{0:T(1024)(128)(4,1)} %bitcast.272), calls=%async_computation.10 | async-start | bytes 8388608
  1061.5 16.0 %slice-start.11 = ((s8[9633792]{0:T(1024)(128)(4,1)}), s8[1245184]{0:T(1024)(128)(4,1)S(1)}, s32[]{:S(2)}) async-start(s8[9633792]{0:T(1024)(128)(4,1)} %bitcast.272), calls=%async_computation.11 | async-start | bytes 2490368
  1111.8 13.0 %copy-start.20 = (bf16[512,3136]{1,0:T(8,128)(2,1)S(1)}, bf16[512,3136]{1,0:T(8,128)(2,1)}, u32[]{:S(2)}) copy-start(bf16[512,3136]{1,0:T(8,128)(2,1)} %copy.188) | copy-start | bytes 9633796
  1124.9 8.2 copy-start.36
  1124.9 72.0 %copy-start.1 = (bf16[169,16]{0,1:T(8,128)(2,1)S(1)}, bf16[169,16]{0,1:T(8,128)(2,1)}, u32[]{:S(2)}) copy-start(bf16[169,16]{0,1:T(8,128)(2,1)} %param.30) | copy-start | bytes 16228
  (4 other events, 3.3 us)

commit v2 on v1

v2 whole, which is shorter than its diff:
```python
import functools

import jax
import jax.numpy as jnp
from jax import lax
from jax.experimental import pallas as pl
from jax.experimental.pallas import tpu as pltpu
from jax.sharding import PartitionSpec as P

C = 512
HEADS = 16
HEAD_DIM = 32
EXPAND = 2048
WIN = 7
SIDE = 14
SHIFT = 3
PANES = 4
RANKS = 32

epsilon = 1e-05
exact_mode = lax.Precision.HIGHEST

MESH = pl.DeviceIdType.MESH


def place():
    me = lax.axis_index("dp")
    return me, me // 8, (me // 4) % 2, (me // 2) % 2, me % 2


def rank_of(z, y, x, c):
    return z * 8 + y * 4 + x * 2 + c


def greet(peers):
    barrier = pltpu.get_barrier_semaphore()
    for peer in peers:
        pl.semaphore_signal(barrier, inc=1, device_id=(peer,), device_id_type=MESH)
    pl.semaphore_wait(barrier, len(peers))


def flip(z, k):
    low, high = z % 2, z // 2
    if k % 2:
        low = 1 - low
    if k // 2:
        high = 1 - high
    return high * 2 + low


def gather_kernel(groups, *refs):
    shards = refs[:groups]
    fulls = refs[groups : 2 * groups]
    local, send, recv = refs[2 * groups :]
    me, z, y, x, c = place()
    peer_x = rank_of(z, y, 1 - x, c)
    peer_y = rank_of(z, 1 - y, x, c)
    mate = rank_of(z, y, x, 1 - c)
    peers_z = [rank_of(flip(z, k), y, x, c) for k in (1, 2, 3)]
    greet([mate, peer_x, peer_y] + peers_z)

    def copy(group, lane, source, owner, target):
        return pltpu.make_async_remote_copy(
            src_ref=source,
            dst_ref=fulls[group].at[owner],
            send_sem=send.at[group, lane],
            recv_sem=recv.at[group, lane],
            device_id=(target,),
            device_id_type=MESH,
        )

    def column(k, dy, dx):
        return rank_of(flip(z, k), 1 - y if dy else y, 1 - x if dx else x, c)

    def incoming(group, lane):
        return copy(group, lane, shards[group], me, mate)

    started = []
    keep = []

    def push(group, lane, source, owner, target):
        made = copy(group, lane, source, owner, target)
        made.start()
        started.append(made)

    for group in range(groups):
        own = shards[group]
        for k in (1, 2, 3):
            push(group, k - 1, own, me, peers_z[k - 1])
        push(group, 3, own, me, peer_x)
        push(group, 7, own, me, peer_y)
        push(group, 15, own, me, mate)
        made = pltpu.make_async_copy(own, fulls[group].at[me], local.at[group])
        made.start()
        keep.append(made)
    for group in range(groups):
        full = fulls[group]
        for k in (1, 2, 3):
            incoming(group, k - 1).wait_recv()
            owner = column(k, 0, 0)
            push(group, 3 + k, full.at[owner], owner, peer_x)
            push(group, 7 + k, full.at[owner], owner, peer_y)
            push(group, 15 + k, full.at[owner], owner, mate)
        for k in range(4):
            incoming(group, 3 + k).wait_recv()
            owner = column(k, 0, 1)
            if k % 2 == 0:
                push(group, 11 + k, full.at[owner], owner, peer_y)
            push(group, 15 + 4 + k, full.at[owner], owner, mate)
            incoming(group, 7 + k).wait_recv()
            owner = column(k, 1, 0)
            if k % 2 == 1:
                push(group, 11 + k, full.at[owner], owner, peer_x)
            push(group, 15 + 8 + k, full.at[owner], owner, mate)
        for k in range(4):
            incoming(group, 11 + k).wait_recv()
            owner = column(k, 1, 1)
            push(group, 15 + 12 + k, full.at[owner], owner, mate)
    for group in range(groups):
        for lane in range(15, 31):
            incoming(group, lane).wait_recv()
    for made in started:
        made.wait_send()
    for made in keep:
        made.wait()


def gather_all(*shards):
    count = len(shards)
    return pl.pallas_call(
        functools.partial(gather_kernel, count),
        out_shape=[jax.ShapeDtypeStruct((32,) + s.shape, s.dtype) for s in shards],
        in_specs=[pl.BlockSpec(memory_space=pl.ANY)] * count,
        out_specs=[pl.BlockSpec(memory_space=pl.ANY)] * count,
        scratch_shapes=[
            pltpu.SemaphoreType.DMA((count,)),
            pltpu.SemaphoreType.DMA((count, 31)),
            pltpu.SemaphoreType.DMA((count, 31)),
        ],
        compiler_params=pltpu.CompilerParams(collective_id=0, has_side_effects=True),
        name="gather_shards",
    )(*shards)


def reduce_kernel(groups, chunks, *refs):
    parts = refs[:groups]
    sums_in = refs[groups]
    outs = refs[groups + 1 : 2 * groups + 1]
    sums_out = refs[2 * groups + 1]
    rest = refs[2 * groups + 2 :]
    acc, rc, r1x, r1y, r2x, r2y, rz = (rest[i * groups : (i + 1) * groups] for i in range(7))
    vec, vecs, local, send, recv, vsend, vrecv = rest[7 * groups :]
    me, z, y, x, c = place()
    peer_x = rank_of(z, y, 1 - x, c)
    peer_y = rank_of(z, 1 - y, x, c)
    mate = rank_of(z, y, x, 1 - c)
    peers_z = [rank_of(flip(z, k), y, x, c) for k in (1, 2, 3)]
    greet([mate, peer_x, peer_y] + peers_z)
    started = []

    def copy(source, target_ref, sems, index, target):
        return pltpu.make_async_remote_copy(
            src_ref=source,
            dst_ref=target_ref,
            send_sem=sems[0].at[index],
            recv_sem=sems[1].at[index],
            device_id=(target,),
            device_id_type=MESH,
        )

    def push(*what):
        made = copy(*what)
        made.start()
        started.append(made)
        return made

    wide = (send, recv)
    slim = (vsend, vrecv)
    spans = []
    first = {}
    mine = {}
    for group, count in enumerate(chunks):
        rows = parts[group].shape[-2] // count
        for index in range(count):
            spans.append((group, index * rows, rows))
    for number, (group, start, rows) in enumerate(spans):
        cut = pl.ds(start, rows)
        first[number] = push(
            parts[group].at[:, :, :, 1 - c, cut], rc[group].at[:, :, :, cut], wide, (number, 0), mate
        )
        made = pltpu.make_async_copy(
            parts[group].at[:, :, :, c, cut], acc[group].at[:, :, :, cut], local.at[number]
        )
        made.start()
        mine[number] = made
    hop = push(sums_in, vecs.at[0], slim, 0, mate)
    hop.wait_recv()
    vec[0] = sums_in[...] + vecs[0]
    hop = push(vec.at[0], vecs.at[1], slim, 1, peer_x)

    def add(into, where, other):
        into[where] = (into[where].astype(jnp.float32) + other.astype(jnp.float32)).astype(jnp.bfloat16)

    second = {}
    for number, (group, start, rows) in enumerate(spans):
        cut = pl.ds(start, rows)
        mine[number].wait()
        first[number].wait_recv()
        a = acc[group]
        for zz in range(4):
            for yy in range(2):
                for xx in range(2):
                    add(a, (zz, yy, xx, cut), rc[group][zz, yy, xx, cut])
        second[number] = (
            push(a.at[0:2, :, 1 - x, cut], r1x[group].at[:, :, cut], wide, (number, 1), peer_x),
            push(a.at[2:4, 1 - y, :, cut], r1y[group].at[:, :, cut], wide, (number, 2), peer_y),
        )
    hop.wait_recv()
    vec[1] = vec[0] + vecs[1]
    hop = push(vec.at[1], vecs.at[2], slim, 2, peer_y)
    third = {}
    for number, (group, start, rows) in enumerate(spans):
        cut = pl.ds(start, rows)
        for made in second[number]:
            made.wait_recv()
        a = acc[group]
        for zz in range(2):
            for other in range(2):
                add(a, (zz, other, x, cut), r1x[group][zz, other, cut])
                add(a, (2 + zz, y, other, cut), r1y[group][zz, other, cut])
        third[number] = (
            push(a.at[0:2, 1 - y, x, cut], r2y[group].at[:, cut], wide, (number, 3), peer_y),
            push(a.at[2:4, y, 1 - x, cut], r2x[group].at[:, cut], wide, (number, 4), peer_x),
        )
    hop.wait_recv()
    vec[2] = vec[1] + vecs[2]
    hops = [push(vec.at[2], vecs.at[2 + k], slim, 2 + k, peers_z[k - 1]) for k in (1, 2, 3)]
    fourth = {}
    for number, (group, start, rows) in enumerate(spans):
        cut = pl.ds(start, rows)
        for made in third[number]:
            made.wait_recv()
        a = acc[group]
        for zz in range(2):
            add(a, (zz, y, x, cut), r2y[group][zz, cut])
            add(a, (2 + zz, y, x, cut), r2x[group][zz, cut])
        fourth[number] = [
            push(
                a.at[flip(z, k), y, x, cut],
                rz[group].at[k - 1, cut],
                wide,
                (number, 4 + k),
                peers_z[k - 1],
            )
            for k in (1, 2, 3)
        ]
    for number, (group, start, rows) in enumerate(spans):
        cut = pl.ds(start, rows)
        total = acc[group][z, y, x, cut].astype(jnp.float32)
        for k in (1, 2, 3):
            fourth[number][k - 1].wait_recv()
            total += rz[group][k - 1, cut].astype(jnp.float32)
        outs[group][cut, :] = total
    for made in hops:
        made.wait_recv()
    sums_out[...] = (vec[2] + vecs[3]) + (vecs[4] + vecs[5])
    for made in started:
        made.wait_send()


def reduce_all(parts, sums, chunks, collective_id):
    groups = len(parts)
    rows = [p.shape[1] for p in parts]
    number = sum(chunks)
    scratch = [pltpu.VMEM((4, 2, 2, r, C), jnp.bfloat16) for r in rows]
    scratch += [pltpu.VMEM((4, 2, 2, r, C), jnp.bfloat16) for r in rows]
    scratch += [pltpu.VMEM((2, 2, r, C), jnp.bfloat16) for r in rows]
    scratch += [pltpu.VMEM((2, 2, r, C), jnp.bfloat16) for r in rows]
    scratch += [pltpu.VMEM((2, r, C), jnp.bfloat16) for r in rows]
    scratch += [pltpu.VMEM((2, r, C), jnp.bfloat16) for r in rows]
    scratch += [pltpu.VMEM((3, r, C), jnp.bfloat16) for r in rows]
    scratch += [
        pltpu.VMEM((3,) + sums.shape, jnp.float32),
        pltpu.VMEM((6,) + sums.shape, jnp.float32),
        pltpu.SemaphoreType.DMA((number,)),
        pltpu.SemaphoreType.DMA((number, 8)),
        pltpu.SemaphoreType.DMA((number, 8)),
        pltpu.SemaphoreType.DMA((6,)),
        pltpu.SemaphoreType.DMA((6,)),
    ]
    return pl.pallas_call(
        functools.partial(reduce_kernel, groups, chunks),
        out_shape=[jax.ShapeDtypeStruct((r, C), jnp.float32) for r in rows]
        + [jax.ShapeDtypeStruct(sums.shape, jnp.float32)],
        in_specs=[pl.BlockSpec(memory_space=pl.ANY)] * groups
        + [pl.BlockSpec(memory_space=pltpu.VMEM)],
        out_specs=[pl.BlockSpec(memory_space=pltpu.VMEM)] * (groups + 1),
        scratch_shapes=scratch,
        compiler_params=pltpu.CompilerParams(
            collective_id=collective_id, has_side_effects=True, vmem_limit_bytes=60 << 20
        ),
        name="reduce_shards",
    )(*[p.reshape(4, 2, 2, 2, p.shape[1], C) for p in parts], sums)


def pack_shards(joint_weight, output_weight, expand_weight, reduce_weight, vectors):
    row = jnp.concatenate([v.reshape(-1) for v in vectors])
    tail = jnp.zeros((16 * C - row.shape[0],), row.dtype)
    near = jnp.concatenate(
        [joint_weight[:, i * C : (i + 1) * C] for i in range(3)]
        + [output_weight, jnp.concatenate([row, tail]).reshape(16, C)],
        axis=0,
    )
    far = jnp.concatenate(
        [expand_weight[:, i * C : (i + 1) * C] for i in range(4)] + [reduce_weight], axis=0
    )
    return near, far

ERFC_SLOPE = 0.4
ERFC_TERMS = (
    0.23192538182549352,
    0.16180412136440986,
    0.4683198256010739,
    -0.3709611648908394,
    0.7091781371622337,
    -0.20026632849062864,
)


def gelu_pair(v):
    bell = jnp.exp(v * v * -0.5)
    t = 1.0 / (1.0 + jnp.abs(v) * (ERFC_SLOPE * 0.5**0.5))
    tail = ERFC_TERMS[5] * 0.5
    for term in ERFC_TERMS[4::-1]:
        tail = tail * t + term * 0.5
    tail = tail * t * bell
    below = jnp.where(v < 0, tail, 1.0 - tail)
    return v * below, below + v * (bell * 0.3989422804014327)


def norm_parts(v):
    center = jnp.mean(v, axis=-1, keepdims=True)
    centred = v - center
    spread = jnp.mean(centred * centred, axis=-1, keepdims=True)
    rate = lax.rsqrt(spread + epsilon)
    return centred * rate, rate


def norm_pull(grad, gain, xhat, rate):
    scaled = grad * gain
    first = jnp.mean(scaled, axis=-1, keepdims=True)
    second = jnp.mean(scaled * xhat, axis=-1, keepdims=True)
    return rate * (scaled - first - xhat * second)


def dot_nn(a, b):
    return lax.dot_general(a, b, (((1,), (0,)), ((), ())), preferred_element_type=jnp.float32)


def dot_nt(a, b):
    return lax.dot_general(a, b, (((1,), (1,)), ((), ())), preferred_element_type=jnp.float32)


def dot_tn(a, b):
    return lax.dot_general(a, b, (((0,), (0,)), ((), ())), preferred_element_type=jnp.float32)


def column_sum(v):
    return jnp.sum(v, axis=0, keepdims=True)


def mlp_kernel(
    res_ref, cot_ref, live_ref, far_ref, gain_ref, shift_ref, ebias_ref, rbias_ref,
    out_ref, rgrad_ref, part_ref, vec_ref, ebg_ref, we_acc, wr_acc,
):
    step = pl.program_id(0)
    rows = res_ref.shape[0]

    @pl.when(step == 0)
    def _():
        we_acc[...] = jnp.zeros_like(we_acc)
        wr_acc[...] = jnp.zeros_like(wr_acc)
        vec_ref[...] = jnp.zeros_like(vec_ref)
        ebg_ref[...] = jnp.zeros_like(ebg_ref)

    res = res_ref[...]
    gain = gain_ref[...]
    xhat, rate = norm_parts(res)
    second = (xhat * gain + shift_ref[...]).astype(jnp.bfloat16)
    upstream = (
        cot_ref[...].astype(jnp.float32).reshape(rows // 16, 16, C) * live_ref[...][None, :, :1]
    ).reshape(rows, C)
    low = upstream.astype(jnp.bfloat16)
    second_t = second.T
    low_t = low.T
    reduced = jnp.zeros((rows, C), jnp.float32)
    pulled = jnp.zeros((rows, C), jnp.float32)
    for b in range(4):
        we = far_ref[:, b * 16 : (b + 1) * 16, :].reshape(C, C)
        wr = far_ref[b * 8 : (b + 1) * 8, 64:128, :].reshape(C, C)
        hidden = dot_nn(second, we) + ebias_ref[:, b * C : (b + 1) * C]
        active, slope = gelu_pair(hidden)
        active = active.astype(jnp.bfloat16)
        reduced += dot_nn(active, wr)
        hgrad = (dot_nt(low, wr) * slope).astype(jnp.bfloat16)
        pulled += dot_nt(hgrad, we)
        wr_acc[b] += dot_nn(low_t, active)
        we_acc[b] += dot_nn(second_t, hgrad)
        ebg_ref[:, b * C : (b + 1) * C] += column_sum(hgrad.astype(jnp.float32))
    out_ref[...] = (res + reduced + rbias_ref[...]).astype(jnp.bfloat16)
    rgrad_ref[...] = upstream + norm_pull(pulled, gain, xhat, rate)
    vec_ref[0:1] += column_sum(pulled * xhat)
    vec_ref[1:2] += column_sum(pulled)
    vec_ref[2:3] += column_sum(low.astype(jnp.float32))

    @pl.when(step == pl.num_programs(0) - 1)
    def _():
        for b in range(4):
            part_ref[:, b * 16 : (b + 1) * 16, :] = we_acc[b].reshape(RANKS, 16, C).astype(jnp.bfloat16)
            part_ref[b * 8 : (b + 1) * 8, 64:128, :] = (
                wr_acc[b].T.reshape(8, 64, C).astype(jnp.bfloat16)
            )


def mlp_block(res, cot, live, far, gain, shift, ebias, rbias, rows=448):
    tokens = res.shape[0]
    fixed = lambda shape: pl.BlockSpec(shape, lambda i: (0,) * len(shape), pipeline_mode=pl.Buffered(1))
    moving = pl.BlockSpec((rows, C), lambda i: (i, 0))
    return pl.pallas_call(
        mlp_kernel,
        grid=(tokens // rows,),
        in_specs=[moving, moving, fixed((16, 128)), fixed((RANKS, 128, C)), fixed((1, C)), fixed((1, C)),
                  fixed((1, EXPAND)), fixed((1, C))],
        out_specs=[moving, moving, fixed((RANKS, 128, C)), fixed((8, C)), fixed((1, EXPAND))],
        out_shape=[
            jax.ShapeDtypeStruct((tokens, C), jnp.bfloat16),
            jax.ShapeDtypeStruct((tokens, C), jnp.float32),
            jax.ShapeDtypeStruct((RANKS, 128, C), jnp.bfloat16),
            jax.ShapeDtypeStruct((8, C), jnp.float32),
            jax.ShapeDtypeStruct((1, EXPAND), jnp.float32),
        ],
        scratch_shapes=[pltpu.VMEM((4, C, C), jnp.float32), pltpu.VMEM((4, C, C), jnp.float32)],
        compiler_params=pltpu.CompilerParams(vmem_limit_bytes=60 << 20, dimension_semantics=("arbitrary",)),
        name="mlp_block",
    )(res, cot, live, far, gain, shift, ebias, rbias)

SPOTS = WIN * WIN
ROWS = SPOTS * 16
QUERY_ROWS = 56
KEY_ROWS = 64
QUAD = 4 * HEAD_DIM
SPAN = 4 * KEY_ROWS
SCALE = HEAD_DIM**-0.5


def spot_of(pane, spot):
    y = lax.rem((pane // 2) * WIN + spot // WIN + SHIFT, SIDE)
    x = lax.rem((pane % 2) * WIN + spot % WIN + SHIFT, SIDE)
    return y, x


def take_pane(pane, source, target):
    for spot in range(SPOTS):
        y, x = spot_of(pane, spot)
        target[spot * 16 : (spot + 1) * 16, :] = source[y, x]


def give_pane(pane, value, target):
    for spot in range(SPOTS):
        y, x = spot_of(pane, spot)
        target[y, x] = value[spot * 16 : (spot + 1) * 16, :]


def put_tiles(target, first, value):
    for tile in range(4):
        target[first + tile, 0:ROWS, :] = value[:, tile * QUAD : (tile + 1) * QUAD]


def get_tiles(source, first):
    return jnp.concatenate([source[first + tile, 0:ROWS, :] for tile in range(4)], axis=1)


def low_half(rows):
    return lax.broadcasted_iota(jnp.int32, (rows, 128), 1) < KEY_ROWS


def by_segment(value, op, neutral):
    low = low_half(value.shape[0])
    tiles = []
    for tile in range(2):
        part = value[:, tile * 128 : (tile + 1) * 128]
        first = op(jnp.where(low, part, neutral), axis=-1, keepdims=True)
        second = op(jnp.where(low, neutral, part), axis=-1, keepdims=True)
        tiles.append(jnp.where(low, first, second))
    return jnp.concatenate(tiles, axis=1)


def head_lanes(rows):
    return lax.broadcasted_iota(jnp.int32, (rows, QUAD), 1) // HEAD_DIM


def spread_heads(tile):
    lanes = head_lanes(KEY_ROWS)
    return jnp.concatenate(
        [jnp.where(lanes == h, tile, jnp.zeros_like(tile)) for h in range(4)], axis=0
    )


def merge_heads(value):
    lanes = head_lanes(KEY_ROWS)
    parts = [value[h * KEY_ROWS : (h + 1) * KEY_ROWS] for h in range(4)]
    return jnp.where(
        lanes < 2, jnp.where(lanes == 0, parts[0], parts[1]), jnp.where(lanes == 2, parts[2], parts[3])
    )


def attend_kernel(
    x_ref, near_ref, bias_ref, mask_ref, gain_ref, shift_ref, jbias_ref, obias_ref,
    joint_ref, probs_ref, mixed_ref, res_ref, window, wide, blend,
):
    pane = pl.program_id(0)

    @pl.when(pane == 0)
    def _():
        wide[...] = jnp.zeros_like(wide)

    take_pane(pane, x_ref, window)
    source = window[...].astype(jnp.float32)
    xhat, _ = norm_parts(source)
    normed = (xhat * gain_ref[...] + shift_ref[...]).astype(jnp.bfloat16)
    for b in range(3):
        weight = near_ref[:, b * 16 : (b + 1) * 16, :].reshape(C, C)
        block = (dot_nn(normed, weight) + jbias_ref[:, b * C : (b + 1) * C]).astype(jnp.bfloat16)
        joint_ref[0, :, b * C : (b + 1) * C] = block
        put_tiles(wide, b * 4, block.astype(jnp.float32))
    mask = mask_ref[0]

    def per_image(m, carry):
        for quad in range(4):
            few, many = pl.ds(m, QUERY_ROWS, stride=16), pl.ds(m, KEY_ROWS, stride=16)
            q = wide[quad, few, :].astype(jnp.bfloat16)
            k = wide[4 + quad, many, :].astype(jnp.bfloat16)
            v = wide[8 + quad, many, :].astype(jnp.bfloat16)
            scores = dot_nt(q, spread_heads(k)) * SCALE + bias_ref[quad] + mask
            peak = by_segment(scores, jnp.max, -jnp.inf)
            powers = jnp.exp(scores - peak)
            total = by_segment(powers, jnp.sum, 0.0)
            probs = (powers * (1.0 / total)).astype(jnp.bfloat16)
            probs_ref[0, m, quad] = probs
            blend[quad, few, :] = dot_nn(probs, spread_heads(v))
        return carry

    lax.fori_loop(0, 16, per_image, 0)
    mixed = get_tiles(blend, 0).astype(jnp.bfloat16)
    mixed_ref[0] = mixed
    projected = dot_nn(mixed, near_ref[:, 48:64, :].reshape(C, C)) + obias_ref[...]
    give_pane(pane, window[...].astype(jnp.float32) + projected, res_ref)


def fixed(shape):
    return pl.BlockSpec(shape, lambda i: (0,) * len(shape), pipeline_mode=pl.Buffered(1))


def attend(x, near, bias, mask, gain, shift, jbias, obias):
    step = lambda shape: pl.BlockSpec((1,) + shape, lambda i: (i,) + (0,) * len(shape))
    return pl.pallas_call(
        attend_kernel,
        grid=(PANES,),
        in_specs=[fixed((SIDE, SIDE, 16, C)), fixed((RANKS, 80, C)), fixed((4, QUERY_ROWS, SPAN)),
                  step((QUERY_ROWS, SPAN)), fixed((1, C)), fixed((1, C)), fixed((1, 3 * C)), fixed((1, C))],
        out_specs=[step((ROWS, 3 * C)), step((16, 4, QUERY_ROWS, SPAN)), step((ROWS, C)),
                   fixed((SIDE, SIDE, 16, C))],
        out_shape=[
            jax.ShapeDtypeStruct((PANES, ROWS, 3 * C), jnp.bfloat16),
            jax.ShapeDtypeStruct((PANES, 16, 4, QUERY_ROWS, SPAN), jnp.bfloat16),
            jax.ShapeDtypeStruct((PANES, ROWS, C), jnp.bfloat16),
            jax.ShapeDtypeStruct((SIDE, SIDE, 16, C), jnp.float32),
        ],
        scratch_shapes=[
            pltpu.VMEM((ROWS, C), jnp.bfloat16),
            pltpu.VMEM((12, KEY_ROWS * 16, QUAD), jnp.float32),
            pltpu.VMEM((4, KEY_ROWS * 16, QUAD), jnp.float32),
        ],
        compiler_params=pltpu.CompilerParams(vmem_limit_bytes=62 << 20, dimension_semantics=("arbitrary",)),
        name="attend",
    )(x, near, bias, mask, gain, shift, jbias, obias)


def attend_back_kernel(
    x_ref, near_ref, joint_ref, probs_ref, mixed_ref, rgrad_ref, gain_ref, shift_ref,
    dx_ref, part_ref, vec_ref, pairs_ref, window, rwindow, wide, blend, turned, wj_acc, wo_acc,
):
    pane = pl.program_id(0)

    @pl.when(pane == 0)
    def _():
        wide[...] = jnp.zeros_like(wide)
        blend[...] = jnp.zeros_like(blend)
        wj_acc[...] = jnp.zeros_like(wj_acc)
        wo_acc[...] = jnp.zeros_like(wo_acc)
        vec_ref[...] = jnp.zeros_like(vec_ref)
        pairs_ref[...] = jnp.zeros_like(pairs_ref)

    take_pane(pane, x_ref, window)
    take_pane(pane, rgrad_ref, rwindow)
    pulled = rwindow[...].astype(jnp.bfloat16)
    wo = near_ref[:, 48:64, :].reshape(C, C)
    wo_acc[...] += dot_tn(mixed_ref[0], pulled)
    vec_ref[0:1] += column_sum(pulled.astype(jnp.float32))
    put_tiles(blend, 0, dot_nt(pulled, wo).astype(jnp.bfloat16).astype(jnp.float32))
    for b in range(3):
        put_tiles(wide, b * 4, joint_ref[0, :, b * C : (b + 1) * C].astype(jnp.float32))

    def per_image(m, carry):
        for quad in range(4):
            few, many = pl.ds(m, QUERY_ROWS, stride=16), pl.ds(m, KEY_ROWS, stride=16)
            q = wide[quad, few, :].astype(jnp.bfloat16)
            k = spread_heads(wide[4 + quad, many, :].astype(jnp.bfloat16))
            v = spread_heads(wide[8 + quad, many, :].astype(jnp.bfloat16))
            pull = blend[quad, few, :].astype(jnp.bfloat16)
            probs = probs_ref[0, m, quad]
            wider = probs.astype(jnp.float32)
            weighted = dot_nt(pull, v) * wider
            sgrad = (weighted - wider * by_segment(weighted, jnp.sum, 0.0)).astype(jnp.bfloat16)
            pairs_ref[quad] += sgrad.astype(jnp.float32)
            turned[quad, few, :] = dot_nn(sgrad, k) * SCALE
            turned[4 + quad, many, :] = merge_heads(dot_tn(sgrad, q)) * SCALE
            turned[8 + quad, many, :] = merge_heads(dot_tn(probs, pull))
        return carry

    lax.fori_loop(0, 16, per_image, 0)
    gain = gain_ref[...]
    xhat, rate = norm_parts(window[...].astype(jnp.float32))
    normed = (xhat * gain + shift_ref[...]).astype(jnp.bfloat16)
    normed_t = normed.T
    total = jnp.zeros((ROWS, C), jnp.float32)
    for b in range(3):
        weight = near_ref[:, b * 16 : (b + 1) * 16, :].reshape(C, C)
        block = get_tiles(turned, b * 4).astype(jnp.bfloat16)
        wj_acc[b] += dot_nn(normed_t, block)
        total += dot_nt(block, weight)
        if b != 1:
            vec_ref[1 + b // 2 : 2 + b // 2] += column_sum(block.astype(jnp.float32))
    vec_ref[3:4] += column_sum(total * xhat)
    vec_ref[4:5] += column_sum(total)
    dx = rwindow[...] + norm_pull(total, gain, xhat, rate)
    give_pane(pane, dx.astype(jnp.bfloat16), dx_ref)

    @pl.when(pane == PANES - 1)
    def _():
        for b in range(3):
            part_ref[:, b * 16 : (b + 1) * 16, :] = wj_acc[b].reshape(RANKS, 16, C).astype(jnp.bfloat16)
        part_ref[:, 48:64, :] = wo_acc[...].reshape(RANKS, 16, C).astype(jnp.bfloat16)


def attend_back(x, near, joint, probs, mixed, rgrad, gain, shift):
    step = lambda shape: pl.BlockSpec((1,) + shape, lambda i: (i,) + (0,) * len(shape))
    return pl.pallas_call(
        attend_back_kernel,
        grid=(PANES,),
        in_specs=[fixed((SIDE, SIDE, 16, C)), fixed((RANKS, 80, C)), step((ROWS, 3 * C)),
                  step((16, 4, QUERY_ROWS, SPAN)), step((ROWS, C)), fixed((SIDE, SIDE, 16, C)),
                  fixed((1, C)), fixed((1, C))],
        out_specs=[fixed((SIDE, SIDE, 16, C)), fixed((RANKS, 64, C)), fixed((8, C)),
                   fixed((4, QUERY_ROWS, SPAN))],
        out_shape=[
            jax.ShapeDtypeStruct((SIDE, SIDE, 16, C), jnp.bfloat16),
            jax.ShapeDtypeStruct((RANKS, 64, C), jnp.bfloat16),
            jax.ShapeDtypeStruct((8, C), jnp.float32),
            jax.ShapeDtypeStruct((4, QUERY_ROWS, SPAN), jnp.float32),
        ],
        scratch_shapes=[
            pltpu.VMEM((ROWS, C), jnp.bfloat16),
            pltpu.VMEM((ROWS, C), jnp.float32),
            pltpu.VMEM((12, KEY_ROWS * 16, QUAD), jnp.float32),
            pltpu.VMEM((4, KEY_ROWS * 16, QUAD), jnp.float32),
            pltpu.VMEM((12, KEY_ROWS * 16, QUAD), jnp.float32),
            pltpu.VMEM((3, C, C), jnp.float32),
            pltpu.VMEM((C, C), jnp.float32),
        ],
        compiler_params=pltpu.CompilerParams(vmem_limit_bytes=62 << 20, dimension_semantics=("arbitrary",)),
        name="attend_back",
    )(x, near, joint, probs, mixed, rgrad, gain, shift)


def pair_tables(bias_table, regions):
    rows, cols = jnp.arange(QUERY_ROWS), jnp.arange(KEY_ROWS)
    real = (rows < SPOTS)[:, None] & (cols < SPOTS)[None, :]
    cells = (
        (rows[:, None] // WIN - cols[None, :] // WIN + WIN - 1) * (2 * WIN - 1)
        + rows[:, None] % WIN - cols[None, :] % WIN + WIN - 1
    )
    cells = jnp.where(real, cells, -1).reshape(-1)
    onehot = (cells[None, :] == jnp.arange((2 * WIN - 1) ** 2)[:, None]).astype(jnp.bfloat16)
    bias = dot_tn(bias_table, onehot).reshape(4, 4, QUERY_ROWS, KEY_ROWS)
    bias = jnp.where((cols < SPOTS)[None, None, None, :], bias, -1e30)
    bias = bias.transpose(0, 2, 1, 3).reshape(4, QUERY_ROWS, SPAN)
    labels = jnp.roll(regions, (-SHIFT, -SHIFT), axis=(0, 1)).reshape(2, WIN, 2, WIN)
    labels = labels.transpose(0, 2, 1, 3).reshape(PANES, SPOTS)
    across = jnp.pad(labels, ((0, 0), (0, QUERY_ROWS - SPOTS)))
    along = jnp.pad(labels, ((0, 0), (0, KEY_ROWS - SPOTS)))
    along = jnp.tile(along, (1, 4))
    mask = jnp.where(across[:, :, None] == along[:, None, :], 0.0, -100.0).astype(jnp.float32)
    return bias, mask, onehot


def table_sums(pairs, onehot):
    heads = pairs.reshape(4, QUERY_ROWS, 4, KEY_ROWS).transpose(0, 2, 1, 3).reshape(HEADS, QUERY_ROWS * KEY_ROWS)
    return lax.dot_general(
        onehot.astype(jnp.float32), heads, (((1,), (1,)), ((), ())),
        precision=exact_mode, preferred_element_type=jnp.float32,
    )

def regroup(packed, blocks, rows):
    count = packed.shape[0] // RANKS
    return (
        packed.reshape(RANKS, count, blocks, rows, C)
        .transpose(0, 2, 1, 3, 4)
        .reshape(RANKS, blocks * rows * count, C)
    )


def ungroup(parts, blocks, ranks):
    rows = parts.shape[1] // blocks
    flat = parts.reshape(RANKS, blocks, rows, C).transpose(1, 0, 2, 3).reshape(blocks, RANKS * rows, C)
    return flat.reshape(blocks, ranks, RANKS * rows // ranks, C).transpose(1, 0, 2, 3)


def on_device(
    images,
    first_gain,
    first_shift,
    joint_weight,
    joint_bias,
    output_weight,
    output_bias,
    second_gain,
    second_shift,
    expand_weight,
    expand_bias,
    reduce_weight,
    reduce_bias,
    bias_table,
    regions,
    live_slots,
    cotangent,
):
    ranks = lax.axis_size("dp")
    me = lax.axis_index("dp")
    count = images.shape[0]
    small = (
        first_gain,
        first_shift,
        joint_bias[0],
        joint_bias[1],
        output_bias,
        second_gain,
        second_shift,
        reduce_bias,
        expand_bias,
    )
    x = images.transpose(1, 2, 0, 3)
    cot = cotangent.transpose(1, 2, 0, 3).reshape(-1, C)
    live = jnp.broadcast_to(live_slots.astype(jnp.float32)[:, None], (count, 128))
    bias, mask, onehot = pair_tables(bias_table, regions)
    if ranks == RANKS:
        near, far = pack_shards(joint_weight, output_weight, expand_weight, reduce_weight, small)
        near, far = gather_all(near, far)
        row = near[:, 64, : 12 * 16].astype(jnp.float32)
        vectors = [row[:, 16 * i : 16 * i + 16].reshape(1, C) for i in range(8)]
        vectors.append(row[:, 128:].reshape(1, EXPAND))
    else:
        wide = lambda w: lax.all_gather(w, "dp", axis=0)
        rows = C // ranks
        near = jnp.concatenate(
            [wide(joint_weight[:, i * C : (i + 1) * C]) for i in range(3)] + [wide(output_weight)], axis=1
        )
        near = regroup(near, 4, rows)
        near = jnp.concatenate([near, jnp.zeros((RANKS, 16, C), near.dtype)], axis=1)
        far = jnp.concatenate([wide(expand_weight[:, i * C : (i + 1) * C]) for i in range(4)], axis=1)
        far = jnp.concatenate([regroup(far, 4, rows), wide(reduce_weight).reshape(RANKS, 64, C)], axis=1)
        vectors = [
            lax.all_gather(v, "dp", axis=0, tiled=True).astype(jnp.float32).reshape(1, -1) for v in small
        ]
    gain1, shift1, qbias, vbias, obias, gain2, shift2, rbias, ebias = vectors
    jbias = jnp.concatenate([qbias, jnp.zeros((1, C), jnp.float32), vbias], axis=1)
    joint, probs, mixed, res = attend(x, near, bias, mask, gain1, shift1, jbias, obias)
    out, rgrad, far_part, far_vec, ebias_grad = mlp_block(
        res.reshape(-1, C), cot, live, far, gain2, shift2, ebias, rbias
    )
    rgrad = rgrad.reshape(SIDE, SIDE, count, C)
    dx, near_part, near_vec, pairs = attend_back(x, near, joint, probs, mixed, rgrad, gain1, shift1)
    table = table_sums(pairs, onehot)
    small_sums = [near_vec[i] for i in (3, 4, 1, 2, 0)] + [far_vec[i] for i in (0, 1, 2)] + [ebias_grad[0]]
    if ranks == RANKS:
        flat = jnp.concatenate(small_sums + [table.reshape(-1)])
        sums = jnp.concatenate([flat, jnp.zeros((72 * 128 - flat.shape[0],), jnp.float32)]).reshape(72, 128)
        gfar, gnear, sums = reduce_all([far_part, near_part], sums, (4, 2), 1)
        sums = sums.reshape(-1)
        own = [lax.dynamic_slice(sums, (C * i + 16 * me,), (16,)) for i in range(8)]
        own.append(lax.dynamic_slice(sums, (C * 8 + 64 * me,), (64,)))
        table = sums[C * 12 : C * 12 + 169 * HEADS].reshape(169, HEADS)
        pick = lambda part, start, blocks: jnp.concatenate(
            [part[start + 16 * i : start + 16 * i + 16] for i in range(blocks)], axis=1
        )
        gj, go, ge, gr = pick(gnear, 0, 3), gnear[48:], pick(gfar, 0, 4), gfar[64:]
    else:
        rows = C // ranks
        scatter = lambda g: lax.psum_scatter(g.astype(jnp.float32), "dp", scatter_dimension=0, tiled=True)
        cut = lambda part, blocks: scatter(
            ungroup(part, blocks, ranks).transpose(0, 2, 1, 3).reshape(C, blocks * C)
        )
        gj, go = cut(near_part[:, :48], 3), cut(near_part[:, 48:], 1)
        ge, gr = cut(far_part[:, :64], 4), scatter(far_part[:, 64:].reshape(EXPAND, C))
        own = [scatter(g) for g in small_sums]
        table = lax.psum(table, "dp")
    image_order = lambda v: v.reshape(SIDE, SIDE, count, C).transpose(2, 0, 1, 3)
    return (
        image_order(out),
        image_order(dx),
        own[0],
        own[1],
        gj,
        jnp.stack([own[2], own[3]]),
        go,
        own[4],
        own[5],
        own[6],
        ge,
        own[8],
        gr,
        own[7],
        table,
    )


def solution(mesh):
    in_specs = (
        P("dp", None, None, None),
        P("dp"),
        P("dp"),
        P("dp", None),
        P(None, "dp"),
        P("dp", None),
        P("dp"),
        P("dp"),
        P("dp"),
        P("dp", None),
        P("dp"),
        P("dp", None),
        P("dp"),
        P(),
        P(),
        P("dp"),
        P("dp", None, None, None),
    )
    out_specs = (
        P("dp", None, None, None),
        P("dp", None, None, None),
        P("dp"),
        P("dp"),
        P("dp", None),
        P(None, "dp"),
        P("dp", None),
        P("dp"),
        P("dp"),
        P("dp"),
        P("dp", None),
        P("dp"),
        P("dp", None),
        P("dp"),
        P(),
    )
    return jax.shard_map(
        on_device, mesh=mesh, in_specs=in_specs, out_specs=out_specs, check_vma=False
    )
```

time: 1210 us -> 441 us (0.36)
  local copies, waits for them, and re-layouts: 562 us -> 32.2 us
  Pallas kernels: 93.1 us -> 400 us
  matrix products: 294 us -> 1.74 us
  other arithmetic: 246 us -> 4.68 us
    pallas_call x0 -> x3, Pallas kernels: none -> 307 us  [the longest x1 126 us: attend_back(): pl.pallas_call(attend_back_kernel, grid=(PANES,), in_specs=[fixed((SIDE,...]
    dot_general x20 -> x2, matrix products: 294 us -> 1.74 us  [the longest x1 1.24 us: table_sums(): lax.dot_general(onehot.astype(jnp.float32), heads, (((1,), (1,)), ((), ()...]
    another operation x5 -> x2, local copies, waits for them, and re-layouts: 198 us -> 0.09 us  [pair_tables(): along = jnp.tile(along, (1, 4))]
    reduce_sum x13 -> x0, other arithmetic: 160 us -> none  [the longest x1 65.6 us: backward_pass(): expand_bias_grad = jnp.sum(hidden_grad.astype(jnp.float32), axis=0)]
    convert_element_type x18 -> x0, local copies, waits for them, and re-layouts: 93.3 us -> none  [the longest x2 34.3 us: backward_pass(): joint_grad = images_of(panes_grad).reshape(-1, 3 * C).astype(jnp.bfloat16)]
    reshape x15 -> x18, local copies, waits for them, and re-layouts: 90.7 us -> 7.5 us  [the longest x8 4.11 us: on_device(): vectors = [row[:, 16 * i:16 * i + 16].reshape(1, C) for i in range(8)]]
    transpose x5 -> x0, local copies, waits for them, and re-layouts: 40.6 us -> none  [the longest x2 18.7 us: windows_of(): parted.transpose(0, 1, 3, 2, 4, 5).reshape(count * PANES, WIN * WIN, width)]
    dot_general x4 -> x0, local copies, waits for them, and re-layouts: 38.5 us -> none  [the longest x1 17.8 us: backward_pass(): jnp.einsum('tf,cf->tc', hidden_grad, expand_weight, preferred_element_typ...]
where the time goes in v2:
time: 441 us; the launch traced here: 440 us
  Pallas kernels  400 us (91%)
  local copies, waits for them, and re-layouts  32.2 us (7%)
  other arithmetic  4.68 us (1%)
    pallas_call x1, Pallas kernels, attend_back(): pl.pallas_call(attend_back_kernel, grid=(PANES,), in_specs=[fixed((SIDE,...  126 us
    pallas_call x1, Pallas kernels, attend(): pl.pallas_call(attend_kernel, grid=(PANES,), in_specs=[fixed((SIDE, SIDE,...  111 us
    pallas_call x1, Pallas kernels, mlp_block(): pl.pallas_call(mlp_kernel, grid=(tokens // rows,), in_specs=[moving, movi...  70.5 us
    pallas_call x1, Pallas kernels, reduce_all(): pl.pallas_call(functools.partial(reduce_kernel, groups, chunks), out_shap...  52 us
    pallas_call x1, Pallas kernels, gather_all(): pl.pallas_call(functools.partial(gather_kernel, count), out_shape=[jax.Sh...  40.9 us

profile of v2, /device:TPU:0, one launch (start us, length us, event | category | flops | bytes accessed | tf_op | source)
XLA Modules:
  0.0 439.9 jit_solution(14204284830157098972)
XLA Ops:
  0.6 0.0 copy-start
  0.7 0.7 slice_bitcast_fusion
  1.4 4.8 %concatenate.29 = bf16[8192]{0:T(1024)(128)(2,1)S(1)} concatenate(bf16[16]{0:T(256)(128)(2,1)} %param.18, bf16[16]{0:T(256)(128)(2,1)} %param.19, bf16[16]{0:T(256)(128)(2,1)S(1)} %get-tuple-element.99, bf16[16]{0:T(256)(128)(2,1)S(1)} %get-tuple-element.98, bf16[16]{0:T(256)(128)(2,1)} %param.23, bf16[16]{0:T(256)(128)(2,1)} %param.24, bf16[16]{0:T(256)(128)(2,1)} %param.25, ...), dimensions={0} | concatenate | bytes 32768 | tf_op jit(solution)/shard_map/concatenate | solution.py:311
  6.2 0.7 constant_dynamic-update-slice_fusion.4
  6.9 0.7 constant_dynamic-update-slice_fusion.3
  7.6 0.7 constant_dynamic-update-slice_fusion.2
  8.4 0.7 constant_dynamic-update-slice_fusion.1
  9.1 0.7 constant_dynamic-update-slice_fusion.9
  9.8 0.7 constant_dynamic-update-slice_fusion.8
  10.5 0.7 constant_dynamic-update-slice_fusion.7
  11.2 0.7 constant_dynamic-update-slice_fusion.6
  12.0 0.8 constant_dynamic-update-slice_fusion.5.refs_1_
  12.8 0.0 copy-done.2
  12.8 0.7 copy-done.1
  13.5 40.9 %gather_shards.1 = (bf16[32,80,512]{2,1,0:T(8,128)(2,1)}, bf16[32,128,512]{2,1,0:T(8,128)(2,1)}) custom-call(bf16[80,512]{1,0:T(8,128)(2,1)} %copy-done.2, bf16[128,512]{1,0:T(8,128)(2,1)} %copy-done.1), custom_call_target="tpu_custom_call" | custom-call | tf_op jit(solution)/shard_map/gather_shards/pallas_call | solution.py:130
  54.4 0.9 slice_convert_fusion
  55.3 0.1 fusion.8
  55.4 0.1 reshape.258
  55.5 0.1 reshape.259
  55.6 0.6 fusion.4.jbias_ref
  56.2 0.7 reshape.256.gain_ref
  56.9 0.7 reshape.257.shift_ref
  57.6 0.7 reshape.260.obias_ref
  58.2 0.7 slice.139
  58.9 0.7 slice.140
  59.6 0.1 slice_add_fusion
  59.7 0.1 pad_add_fusion.1
  59.8 0.1 reshape.254
  59.9 0.1 reshape.255
  60.0 0.1 tile.9
  60.0 0.8 compare_select_fusion.mask_ref
  60.9 0.1 add_select_fusion
  61.0 0.1 reshape.281
  61.1 0.0 copy-done
  61.1 0.5 convolution_bitcast_fusion
  61.6 0.1 reshape.252
  61.7 0.2 fusion.3
  61.9 1.0 reshape.253.bias_ref
  62.9 111.4 %attend.1 = (bf16[4,784,1536]{2,1,0:T(8,128)(2,1)}, bf16[4,16,4,56,256]{4,3,2,1,0:T(8,128)(2,1)}, bf16[4,784,512]{2,1,0:T(8,128)(2,1)}, f32[14,14,16,512]{3,2,1,0:T(8,128)}) custom-call(bf16[14,14,16,512]{3,2,1,0:T(8,128)(2,1)} %bitcast.48, bf16[32,80,512]{2,1,0:T(8,128)(2,1)} %get-tuple-element.33.near_ref, f32[4,56,256]{2,1,0:T(8,128)} %reshape.253.bias_ref, ...), custom_call_target="tpu_custom_call" | custom-call | tf_op jit(solution)/shard_map/attend/pallas_call | solution.py:566
  174.3 0.7 reshape.263.gain_ref
  175.0 0.7 reshape.264.shift_ref
  175.6 0.7 reshape.266.rbias_ref
  176.3 0.7 reshape.265.ebias_ref
  177.0 0.0 copy-done.5
  177.0 0.7 broadcast_in_dim.52.live_ref
  177.6 70.5 %mlp_block.1 = (bf16[3136,512]{1,0:T(8,128)(2,1)}, f32[3136,512]{1,0:T(8,128)}, bf16[32,128,512]{2,1,0:T(8,128)(2,1)}, f32[8,512]{1,0:T(8,128)}, f32[1,2048]{1,0:T(1,128)}) custom-call(f32[3136,512]{1,0:T(8,128)} %bitcast.50, bf16[3136,512]{1,0:T(8,128)(2,1)} %bitcast.53, f32[16,128]{1,0:T(8,128)} %broadcast_in_dim.52.live_ref, ...), custom_call_target="tpu_custom_call" | custom-call | tf_op jit(solution)/shard_map/mlp_block/pallas_call | solution.py:429
  248.1 125.6 %attend_back.1 = (bf16[14,14,16,512]{3,2,1,0:T(8,128)(2,1)}, bf16[32,64,512]{2,1,0:T(8,128)(2,1)}, f32[8,512]{1,0:T(8,128)}, f32[4,56,256]{2,1,0:T(8,128)}) custom-call(bf16[14,14,16,512]{3,2,1,0:T(8,128)(2,1)} %bitcast.49, bf16[32,80,512]{2,1,0:T(8,128)(2,1)} %get-tuple-element.33.near_ref, bf16[4,784,1536]{2,1,0:T(8,128)(2,1)} %get-tuple-element.37.joint_ref, ...), custom_call_target="tpu_custom_call" | custom-call | tf_op jit(solution)/shard_map/attend_back/pallas_call | solution.py:658
  373.7 1.2 reshape.271
  374.9 0.1 reshape.272
  375.0 1.2 fusion
  376.3 0.1 reshape.273
  376.4 0.8 fusion.9
  377.2 0.7 concatenate.35
  377.9 52.0 %reduce_shards.1 = (f32[128,512]{1,0:T(8,128)}, f32[64,512]{1,0:T(8,128)}, f32[72,128]{1,0:T(8,128)}) custom-call(bf16[4,2,2,2,128,512]{5,4,3,2,1,0:T(8,128)(2,1)} %bitcast.52, bf16[4,2,2,2,64,512]{5,4,3,2,1,0:T(8,128)(2,1)} %bitcast.54, f32[72,128]{1,0:T(8,128)} %bitcast.58), custom_call_target="tpu_custom_call" | custom-call | tf_op jit(solution)/shard_map/reduce_shards/pallas_call | solution.py:291
  430.0 0.8 fusion.5
  430.8 0.7 pad_maximum_fusion
  431.5 0.9 slice.170
  432.4 0.7 copy.39
  433.1 1.4 fusion.7
  434.5 0.6 pad_maximum_fusion.2
  435.0 1.4 fusion.6
  436.5 0.6 pad_maximum_fusion.1
  437.1 1.6 slice.169
  438.7 1.3 dynamic_slice.34
  (28 shorter events, 0.2 us)
Async XLA Ops:
  0.6 60.4 %copy-start = (bf16[169,16]{0,1:T(8,128)(2,1)S(1)}, bf16[169,16]{0,1:T(8,128)(2,1)}, u32[]{:S(2)}) copy-start(bf16[169,16]{0,1:T(8,128)(2,1)} %param.30) | copy-start | bytes 16228
  9.1 3.7 copy-start.2
  12.8 0.7 copy-start.1
  62.9 114.1 %copy-start.5 = (s32[16]{0:T(128)S(1)}, s32[16]{0:T(128)}, u32[]{:S(2)}) copy-start(s32[16]{0:T(128)} %param.32) | copy-start | bytes 196
  373.7 2.7 copy-start.4
  373.7 3.6 copy-start.3

commit v3 on v2

v3 whole, which is shorter than its diff:
```python
import functools

import jax
import jax.numpy as jnp
from jax import lax
from jax.experimental import pallas as pl
from jax.experimental.pallas import tpu as pltpu
from jax.sharding import PartitionSpec as P

C = 512
HEADS = 16
HEAD_DIM = 32
EXPAND = 2048
WIN = 7
SIDE = 14
SHIFT = 3
PANES = 4
RANKS = 32

epsilon = 1e-05
exact_mode = lax.Precision.HIGHEST

MESH = pl.DeviceIdType.MESH
NEAR = 80
FAR = 128


def rank_of(z, y, x, c):
    return z * 8 + y * 4 + x * 2 + c


def flip(z, k):
    low, high = lax.rem(z, 2), z // 2
    if k % 2:
        low = 1 - low
    if k // 2:
        high = 1 - high
    return high * 2 + low


class Place:
    def __init__(self):
        self.me = lax.axis_index("dp")
        self.z, self.y = self.me // 8, lax.rem(self.me // 4, 2)
        self.x, self.c = lax.rem(self.me // 2, 2), lax.rem(self.me, 2)
        self.peer_x = rank_of(self.z, self.y, 1 - self.x, self.c)
        self.peer_y = rank_of(self.z, 1 - self.y, self.x, self.c)
        self.mate = rank_of(self.z, self.y, self.x, 1 - self.c)
        self.peers_z = [rank_of(flip(self.z, k), self.y, self.x, self.c) for k in (1, 2, 3)]

    def column(self, k, dy, dx):
        y = 1 - self.y if dy else self.y
        x = 1 - self.x if dx else self.x
        return rank_of(flip(self.z, k), y, x, self.c)

    def greet(self):
        barrier = pltpu.get_barrier_semaphore()
        peers = [self.mate, self.peer_x, self.peer_y] + self.peers_z
        for peer in peers:
            pl.semaphore_signal(barrier, inc=1, device_id=(peer,), device_id_type=MESH)
        pl.semaphore_wait(barrier, len(peers))


def remote(source, target, send, recv, rank):
    return pltpu.make_async_remote_copy(
        src_ref=source, dst_ref=target, send_sem=send, recv_sem=recv, device_id=(rank,), device_id_type=MESH
    )


class Gather:
    def __init__(self, place, own, full, send, recv):
        self.place, self.own, self.full, self.send, self.recv = place, own, full, send, recv

    def push(self, lane, owner, rank, source=None):
        source = self.full.at[owner] if source is None else source
        remote(source, self.full.at[owner], self.send.at[lane], self.recv.at[lane], rank).start()

    def some(self, lane):
        place = self.place
        return remote(
            self.own, self.full.at[place.me], self.send.at[lane], self.recv.at[lane], place.mate
        )

    def start(self):
        place = self.place
        for k in (1, 2, 3):
            self.push(k - 1, place.me, place.peers_z[k - 1], self.own)
        self.push(3, place.me, place.peer_x, self.own)
        self.push(7, place.me, place.peer_y, self.own)
        self.push(15, place.me, place.mate, self.own)

    def relay_columns(self):
        place = self.place
        for k in (1, 2, 3):
            self.some(k - 1).wait_recv()
            owner = place.column(k, 0, 0)
            self.push(3 + k, owner, place.peer_x)
            self.push(7 + k, owner, place.peer_y)
            self.push(15 + k, owner, place.mate)

    def relay_sides(self):
        place = self.place
        for k in range(4):
            self.some(3 + k).wait_recv()
            owner = place.column(k, 0, 1)
            if k % 2 == 0:
                self.push(11 + k, owner, place.peer_y)
            self.push(19 + k, owner, place.mate)
            self.some(7 + k).wait_recv()
            owner = place.column(k, 1, 0)
            if k % 2 == 1:
                self.push(11 + k, owner, place.peer_x)
            self.push(23 + k, owner, place.mate)

    def relay_corners(self):
        place = self.place
        for k in range(4):
            self.some(11 + k).wait_recv()
            self.push(27 + k, place.column(k, 1, 1), place.mate)

    def finish(self):
        for lane in range(15, 31):
            self.some(lane).wait_recv()

    def drain(self):
        for lane in range(31):
            self.some(lane).wait_send()


class Reduce:
    def __init__(self, place, parts, scratch):
        self.place, self.parts = place, parts
        self.acc, self.rc, self.r1x, self.r1y, self.r2x, self.r2y, self.rz = scratch[:7]
        self.local, self.send, self.recv = scratch[7:]

    @staticmethod
    def scratch(rows):
        shapes = [(4, 2, 2), (4, 2, 2), (2, 2), (2, 2), (2,), (2,), (3,)]
        return [pltpu.VMEM(s + (rows, C), jnp.bfloat16) for s in shapes] + [
            pltpu.SemaphoreType.DMA(()),
            pltpu.SemaphoreType.DMA((8,)),
            pltpu.SemaphoreType.DMA((8,)),
        ]

    def copies(self, lane):
        p, a = self.place, self.acc
        source, target, rank = {
            0: lambda: (self.parts.at[:, :, :, 1 - p.c], self.rc, p.mate),
            1: lambda: (a.at[0:2, :, 1 - p.x], self.r1x, p.peer_x),
            2: lambda: (a.at[2:4, 1 - p.y, :], self.r1y, p.peer_y),
            3: lambda: (a.at[0:2, 1 - p.y, p.x], self.r2y, p.peer_y),
            4: lambda: (a.at[2:4, p.y, 1 - p.x], self.r2x, p.peer_x),
            5: lambda: (a.at[flip(p.z, 1), p.y, p.x], self.rz.at[0], p.peers_z[0]),
            6: lambda: (a.at[flip(p.z, 2), p.y, p.x], self.rz.at[1], p.peers_z[1]),
            7: lambda: (a.at[flip(p.z, 3), p.y, p.x], self.rz.at[2], p.peers_z[2]),
        }[lane]()
        return remote(source, target, self.send.at[lane], self.recv.at[lane], rank)

    def mine(self):
        return pltpu.make_async_copy(self.parts.at[:, :, :, self.place.c], self.acc, self.local)

    def add(self, where, other):
        total = self.acc[where].astype(jnp.float32) + other.astype(jnp.float32)
        self.acc[where] = total.astype(jnp.bfloat16)

    def start(self):
        self.copies(0).start()
        self.mine().start()

    def cores(self):
        self.mine().wait()
        self.copies(0).wait_recv()

        def body(zz, carry):
            for yy in range(2):
                for xx in range(2):
                    self.add((zz, yy, xx), self.rc[zz, yy, xx])
            return carry

        lax.fori_loop(0, 4, body, 0)
        self.copies(1).start()
        self.copies(2).start()

    def sides(self):
        p = self.place
        self.copies(1).wait_recv()
        self.copies(2).wait_recv()
        for zz in range(2):
            for other in range(2):
                self.add((zz, other, p.x), self.r1x[zz, other])
                self.add((2 + zz, p.y, other), self.r1y[zz, other])
        self.copies(3).start()
        self.copies(4).start()

    def corners(self):
        p = self.place
        self.copies(3).wait_recv()
        self.copies(4).wait_recv()
        for zz in range(2):
            self.add((zz, p.y, p.x), self.r2y[zz])
            self.add((2 + zz, p.y, p.x), self.r2x[zz])
        for lane in (5, 6, 7):
            self.copies(lane).start()

    def finish(self):
        p = self.place
        total = self.acc[p.z, p.y, p.x].astype(jnp.float32)
        for lane in (5, 6, 7):
            self.copies(lane).wait_recv()
            total += self.rz[lane - 5].astype(jnp.float32)
        return total

    def drain(self):
        for lane in range(8):
            self.copies(lane).wait_send()


class Swap:
    def __init__(self, place, scratch):
        self.place = place
        self.own, self.got, self.send, self.recv = scratch

    @staticmethod
    def scratch(shape):
        return [
            pltpu.VMEM((4,) + shape, jnp.float32),
            pltpu.VMEM((6,) + shape, jnp.float32),
            pltpu.SemaphoreType.DMA((6,)),
            pltpu.SemaphoreType.DMA((6,)),
        ]

    def copies(self, lane):
        p = self.place
        rank = ([p.mate, p.peer_x, p.peer_y] + p.peers_z)[lane]
        return remote(
            self.own.at[min(lane, 3)], self.got.at[lane], self.send.at[lane], self.recv.at[lane], rank
        )

    def hop(self, lane):
        self.copies(lane).wait_recv()
        self.own[lane + 1] = self.own[lane] + self.got[lane]
        if lane < 2:
            self.copies(lane + 1).start()
        else:
            for last in (3, 4, 5):
                self.copies(last).start()

    def finish(self):
        for lane in (3, 4, 5):
            self.copies(lane).wait_recv()
        return (self.own[3] + self.got[3]) + (self.got[4] + self.got[5])

    def drain(self):
        for lane in range(6):
            self.copies(lane).wait_send()


def reduce_near_kernel(
    parts, near_vec, far_vec, table_ref,
    gj_ref, go_ref, table_out, jb_ref, eb_ref, *rest,
):
    owns = rest[:7]
    spread = rest[7]
    reduce_scratch, vec_scratch, table_scratch = rest[8:18], rest[18:22], rest[22:26]
    place = Place()
    place.greet()
    big = Reduce(place, parts, reduce_scratch)
    vec = Swap(place, vec_scratch)
    tab = Swap(place, table_scratch)
    big.start()
    vec.own[0, 0:8] = near_vec[...]
    vec.own[0, 8:16] = far_vec[...]
    tab.own[0] = table_ref[...]
    vec.copies(0).start()
    tab.copies(0).start()
    big.cores()
    vec.hop(0)
    tab.hop(0)
    big.sides()
    vec.hop(1)
    tab.hop(1)
    big.corners()
    vec.hop(2)
    tab.hop(2)
    total = big.finish()
    for b in range(3):
        gj_ref[:, b * C : (b + 1) * C] = total[b * 16 : (b + 1) * 16]
    go_ref[...] = total[48:64]
    sums = vec.finish()
    table_out[...] = tab.finish()
    for tile in range(4):
        spread[tile] = sums[:, tile * 128 : (tile + 1) * 128]
    me = place.me
    turn = lax.rem(128 - 16 * lax.rem(me, 8), 128)
    mine = pltpu.roll(spread[me // 8], turn, 1)[:, 0:16]
    jb_ref[...] = mine[1:3]
    for own, row in zip(owns, (0, 3, 4, 8, 9, 10)):
        own[...] = mine[row : row + 1]
    wide = pltpu.roll(spread[lax.rem(me, 8) // 2], 64 * lax.rem(me, 2), 1)[:, 0:64]
    owns[6][...] = wide[8:16]
    eb_ref[...] = owns[6][pl.ds(3 + me // 8, 1), :]
    big.drain()
    vec.drain()
    tab.drain()


def reduce_near(parts, near_vec, far_vec, table):
    one = jax.ShapeDtypeStruct((1, 16), jnp.float32)
    outs = pl.pallas_call(
        reduce_near_kernel,
        out_shape=[
            jax.ShapeDtypeStruct((16, 3 * C), jnp.float32),
            jax.ShapeDtypeStruct((16, C), jnp.float32),
            jax.ShapeDtypeStruct(table.shape, jnp.float32),
            jax.ShapeDtypeStruct((2, 16), jnp.float32),
            jax.ShapeDtypeStruct((1, 64), jnp.float32),
        ]
        + [one] * 6,
        in_specs=[pl.BlockSpec(memory_space=pl.ANY)] + [pl.BlockSpec(memory_space=pltpu.VMEM)] * 3,
        out_specs=[pl.BlockSpec(memory_space=pltpu.VMEM)] * 11,
        scratch_shapes=[pltpu.VMEM((8, 64), jnp.float32), pltpu.VMEM((4, 16, 128), jnp.float32)]
        + Reduce.scratch(64)
        + Swap.scratch((16, C))
        + Swap.scratch(table.shape),
        compiler_params=pltpu.CompilerParams(
            collective_id=2, has_side_effects=True, vmem_limit_bytes=40 << 20
        ),
        name="reduce_near",
    )(parts.reshape(4, 2, 2, 2, 64, C), near_vec, far_vec, table)
    return outs

ERFC_SLOPE = 0.4
ERFC_TERMS = (
    0.23192538182549352,
    0.16180412136440986,
    0.4683198256010739,
    -0.3709611648908394,
    0.7091781371622337,
    -0.20026632849062864,
)


def gelu_pair(v):
    bell = jnp.exp(v * v * -0.5)
    t = 1.0 / (1.0 + jnp.abs(v) * (ERFC_SLOPE * 0.5**0.5))
    tail = ERFC_TERMS[5] * 0.5
    for term in ERFC_TERMS[4::-1]:
        tail = tail * t + term * 0.5
    tail = tail * t * bell
    below = jnp.where(v < 0, tail, 1.0 - tail)
    return v * below, below + v * (bell * 0.3989422804014327)


def norm_parts(v):
    center = jnp.mean(v, axis=-1, keepdims=True)
    centred = v - center
    spread = jnp.mean(centred * centred, axis=-1, keepdims=True)
    rate = lax.rsqrt(spread + epsilon)
    return centred * rate, rate


def norm_pull(grad, gain, xhat, rate):
    scaled = grad * gain
    first = jnp.mean(scaled, axis=-1, keepdims=True)
    second = jnp.mean(scaled * xhat, axis=-1, keepdims=True)
    return rate * (scaled - first - xhat * second)


def dot_nn(a, b):
    return lax.dot_general(a, b, (((1,), (0,)), ((), ())), preferred_element_type=jnp.float32)


def dot_nt(a, b):
    return lax.dot_general(a, b, (((1,), (1,)), ((), ())), preferred_element_type=jnp.float32)


def dot_tn(a, b):
    return lax.dot_general(a, b, (((0,), (0,)), ((), ())), preferred_element_type=jnp.float32)


def column_sum(v):
    return jnp.sum(v, axis=0, keepdims=True)


def mlp_kernel(
    res_ref, cot_ref, live_ref, far_ref, bias_ref, ebias_ref,
    out_ref, rgrad_ref, part_ref, vec_ref, we_acc, wr_acc,
):
    step = pl.program_id(0)
    rows = res_ref.shape[0]

    @pl.when(step == 0)
    def _():
        we_acc[...] = jnp.zeros_like(we_acc)
        wr_acc[...] = jnp.zeros_like(wr_acc)
        vec_ref[...] = jnp.zeros_like(vec_ref)

    res = res_ref[...]
    gain = bias_ref[5:6]
    xhat, rate = norm_parts(res)
    second = (xhat * gain + bias_ref[6:7]).astype(jnp.bfloat16)
    upstream = (
        cot_ref[...].astype(jnp.float32).reshape(rows // 16, 16, C) * live_ref[...].astype(jnp.float32)[None]
    ).reshape(rows, C)
    low = upstream.astype(jnp.bfloat16)
    second_t = second.T
    low_t = low.T
    reduced = jnp.zeros((rows, C), jnp.float32)
    pulled = jnp.zeros((rows, C), jnp.float32)
    for b in range(4):
        we = far_ref[:, b * 16 : (b + 1) * 16, :].reshape(C, C)
        wr = far_ref[b * 8 : (b + 1) * 8, 64:128, :].reshape(C, C)
        hidden = dot_nn(second, we) + ebias_ref[:, b * C : (b + 1) * C]
        active, slope = gelu_pair(hidden)
        active = active.astype(jnp.bfloat16)
        reduced += dot_nn(active, wr)
        hgrad = (dot_nt(low, wr) * slope).astype(jnp.bfloat16)
        pulled += dot_nt(hgrad, we)
        wr_acc[b] += dot_nn(low_t, active)
        we_acc[b] += dot_nn(second_t, hgrad)
        vec_ref[3 + b : 4 + b] += column_sum(hgrad.astype(jnp.float32))
    out_ref[...] = (res + reduced + bias_ref[7:8]).astype(jnp.bfloat16)
    rgrad_ref[...] = upstream + norm_pull(pulled, gain, xhat, rate)
    vec_ref[0:1] += column_sum(pulled * xhat)
    vec_ref[1:2] += column_sum(pulled)
    vec_ref[2:3] += column_sum(low.astype(jnp.float32))

    @pl.when(step == pl.num_programs(0) - 1)
    def _():
        for b in range(4):
            part_ref[:, b * 16 : (b + 1) * 16, :] = we_acc[b].reshape(RANKS, 16, C).astype(jnp.bfloat16)
            part_ref[b * 8 : (b + 1) * 8, 64:128, :] = (
                wr_acc[b].T.reshape(8, 64, C).astype(jnp.bfloat16)
            )


def mlp_block(res, cot, live, far, vectors, ebias, rows=448):
    tokens = res.shape[0]
    moving = pl.BlockSpec((rows, C), lambda i: (i, 0))
    return pl.pallas_call(
        mlp_kernel,
        grid=(tokens // rows,),
        in_specs=[moving, moving, fixed((16, 1)), fixed((RANKS, FAR, C)), fixed((8, C)), fixed((1, EXPAND))],
        out_specs=[moving, moving, fixed((RANKS, FAR, C)), fixed((8, C))],
        out_shape=[
            jax.ShapeDtypeStruct((tokens, C), jnp.bfloat16),
            jax.ShapeDtypeStruct((tokens, C), jnp.float32),
            jax.ShapeDtypeStruct((RANKS, 128, C), jnp.bfloat16),
            jax.ShapeDtypeStruct((8, C), jnp.float32),
        ],
        scratch_shapes=[pltpu.VMEM((4, C, C), jnp.float32), pltpu.VMEM((4, C, C), jnp.float32)],
        compiler_params=pltpu.CompilerParams(vmem_limit_bytes=60 << 20, dimension_semantics=("arbitrary",)),
        name="mlp_block",
    )(res, cot, live, far, vectors, ebias)

SPOTS = WIN * WIN
ROWS = SPOTS * 16
QUERY_ROWS = 64
KEY_ROWS = 56
QUAD = 4 * HEAD_DIM
PAIR_SHAPE = (4 * KEY_ROWS, 2 * QUERY_ROWS)
SCALE = HEAD_DIM**-0.5


def spot_of(pane, spot):
    y = lax.rem((pane // 2) * WIN + spot // WIN + SHIFT, SIDE)
    x = lax.rem((pane % 2) * WIN + spot % WIN + SHIFT, SIDE)
    return y, x


def take_pane(pane, source, target):
    for spot in range(SPOTS):
        y, x = spot_of(pane, spot)
        target[spot * 16 : (spot + 1) * 16, :] = source[y, x]


def give_pane(pane, value, target):
    for spot in range(SPOTS):
        y, x = spot_of(pane, spot)
        target[y, x] = value[spot * 16 : (spot + 1) * 16, :]


def put_tiles(target, first, value):
    for tile in range(4):
        target[first + tile, 0:ROWS, :] = value[:, tile * QUAD : (tile + 1) * QUAD]


def get_tiles(source, first):
    return jnp.concatenate([source[first + tile, 0:ROWS, :] for tile in range(4)], axis=1)


def heads_mask(rows):
    return lax.rem(lax.broadcasted_iota(jnp.int32, (rows, 2 * QUAD), 1), QUAD) // HEAD_DIM


def load_pair(source, first, rows):
    return jnp.concatenate([source[first, rows, :], source[first + 1, rows, :]], axis=1)


def spread_heads(pair):
    lanes = heads_mask(KEY_ROWS)
    zero = jnp.zeros_like(pair)
    return jnp.concatenate([jnp.where(lanes == h, pair, zero) for h in range(4)], axis=0).astype(jnp.bfloat16)


def merge_heads(value):
    lanes = heads_mask(KEY_ROWS)
    parts = [value[h * KEY_ROWS : (h + 1) * KEY_ROWS] for h in range(4)]
    return jnp.where(
        lanes < 2, jnp.where(lanes == 0, parts[0], parts[1]), jnp.where(lanes == 2, parts[2], parts[3])
    )


def two_blocks(source, first, rows):
    upper = source[first, rows, :].astype(jnp.bfloat16)
    lower = source[first + 1, rows, :].astype(jnp.bfloat16)
    zero = jnp.zeros_like(upper)
    return jnp.concatenate(
        [jnp.concatenate([upper, zero], axis=1), jnp.concatenate([zero, lower], axis=1)], axis=0
    )


def over_keys(op, value):
    parts = value.reshape(4, KEY_ROWS, 2 * QUERY_ROWS)
    return jnp.broadcast_to(op(parts, axis=1, keepdims=True), parts.shape).reshape(value.shape)


def bias_rows(near, vec_ref, ebias_ref):
    rows = jnp.sum(near[:, 64:80, 0:256].astype(jnp.float32), axis=1)
    lane = lax.broadcasted_iota(jnp.int32, (RANKS, 256), 1)
    parts = [jnp.where(lane // 16 == i, rows, 0.0) for i in range(8)]
    parts = jnp.concatenate(parts, axis=0).astype(jnp.bfloat16)

    def taken(lhs, width):
        source = lax.broadcasted_iota(jnp.int32, (256, RANKS * width), 0)
        target = lax.broadcasted_iota(jnp.int32, (256, RANKS * width), 1)
        onehot = jnp.where(lax.rem(source, width) == lax.rem(target, width), 1.0, 0.0).astype(jnp.bfloat16)
        count = lhs.shape[0]
        shard = lax.rem(lax.broadcasted_iota(jnp.int32, (count, RANKS * width), 0), RANKS)
        place = lax.broadcasted_iota(jnp.int32, (count, RANKS * width), 1) // width
        return jnp.where(shard == place, dot_nn(lhs, onehot), 0.0)

    vec_ref[...] = jnp.sum(taken(parts, 16).reshape(8, RANKS, C), axis=1)
    tail = jnp.where(lane // 64 == 2, rows, 0.0).astype(jnp.bfloat16)
    ebias_ref[...] = jnp.sum(taken(tail, 64), axis=0, keepdims=True)


def attend_kernel(linked, *refs):
    x_ref, bias_ref, mask_ref, *refs = refs
    if linked:
        shards, refs = refs[:5], refs[5:]
    else:
        near_ref, *refs = refs
    joint_ref, probs_ref, mixed_ref, res_ref, vec_ref, ebias_ref, *refs = refs
    if linked:
        near_out, far_out, *refs = refs
    window, wide, blend, both, *refs = refs
    pane = pl.program_id(0)
    last = pl.num_programs(0) - 1
    if linked:
        near, far_own, local, near_send, near_recv, far_send, far_recv = refs
        place = Place()
        close = Gather(place, near.at[place.me], near, near_send, near_recv)
        distant = Gather(place, far_own, far_out, far_send, far_recv)
        joint_w, output_w, expand_w, reduce_w, row_w = shards
        own = near.at[place.me]
        pieces = [(joint_w.at[:, b * C : (b + 1) * C], own.at[b * 16 : (b + 1) * 16]) for b in range(3)]
        pieces += [(output_w, own.at[48:64]), (row_w, own.at[64:80])]
        pieces += [
            (expand_w.at[:, b * C : (b + 1) * C], far_own.at[b * 16 : (b + 1) * 16]) for b in range(4)
        ]
        pieces += [(reduce_w, far_own.at[64:128])]
        pieces = [pltpu.make_async_copy(a, b, local.at[i]) for i, (a, b) in enumerate(pieces)]
        keep_near = pltpu.make_async_copy(near, near_out, local.at[10])
        keep_far = pltpu.make_async_copy(far_own, far_out.at[place.me], local.at[11])
    else:
        near = near_ref

    @pl.when(pane == 0)
    def _():
        if linked:
            for piece in pieces:
                piece.start()
            place.greet()
            for piece in pieces[:5]:
                piece.wait()
            close.start()
            for piece in pieces[5:]:
                piece.wait()
        wide[...] = jnp.zeros_like(wide)
        if linked:
            close.relay_columns()
            close.relay_sides()
            close.relay_corners()
            distant.start()
            keep_far.start()
            close.finish()
            keep_near.start()
        bias_rows(near, vec_ref, ebias_ref)

    if linked:
        @pl.when(pane == 1)
        def _():
            distant.relay_columns()

        @pl.when(pane == 2)
        def _():
            distant.relay_sides()

        @pl.when(pane == 3)
        def _():
            distant.relay_corners()

    take_pane(pane, x_ref, window)
    source = window[...].astype(jnp.float32)
    xhat, _ = norm_parts(source)
    normed = (xhat * vec_ref[0:1] + vec_ref[1:2]).astype(jnp.bfloat16)
    for b in range(3):
        weight = near[:, b * 16 : (b + 1) * 16, :].reshape(C, C)
        block = dot_nn(normed, weight)
        if b != 1:
            block += vec_ref[2 + b // 2 : 3 + b // 2]
        block = block.astype(jnp.bfloat16)
        joint_ref[0, :, b * C : (b + 1) * C] = block
        put_tiles(wide, b * 4, block.astype(jnp.float32))
    for pair in range(2):
        both[pair] = bias_ref[pair] + mask_ref[0]

    def per_image(m, carry):
        few, many = pl.ds(m, QUERY_ROWS, stride=16), pl.ds(m, KEY_ROWS, stride=16)
        for pair in range(2):
            q = two_blocks(wide, 2 * pair, few)
            k = spread_heads(load_pair(wide, 4 + 2 * pair, many))
            v = spread_heads(load_pair(wide, 8 + 2 * pair, many))
            scores = dot_nt(k, q) * SCALE + both[pair]
            powers = jnp.exp(scores - over_keys(jnp.max, scores))
            probs = (powers * (1.0 / over_keys(jnp.sum, powers))).astype(jnp.bfloat16)
            probs_ref[0, m, pair] = probs
            blended = dot_tn(probs, v)
            blend[2 * pair, many, :] = blended[0:KEY_ROWS, 0:QUAD]
            blend[2 * pair + 1, many, :] = blended[QUERY_ROWS : QUERY_ROWS + KEY_ROWS, QUAD:]
        return carry

    lax.fori_loop(0, 16, per_image, 0, unroll=2)
    mixed = get_tiles(blend, 0).astype(jnp.bfloat16)
    mixed_ref[0] = mixed
    projected = dot_nn(mixed, near[:, 48:64, :].reshape(C, C)) + vec_ref[4:5]
    give_pane(pane, window[...].astype(jnp.float32) + projected, res_ref)

    if linked:
        @pl.when(pane == last)
        def _():
            distant.finish()
            close.drain()
            distant.drain()
            keep_near.wait()
            keep_far.wait()


def fixed(shape):
    return pl.BlockSpec(shape, lambda i: (0,) * len(shape), pipeline_mode=pl.Buffered(1))


def stepped(shape):
    return pl.BlockSpec((1,) + shape, lambda i: (i,) + (0,) * len(shape))


def attend(x, bias, mask, weights, linked):
    anywhere = pl.BlockSpec(memory_space=pl.ANY)
    out_specs = [stepped((ROWS, 3 * C)), stepped((16, 2) + PAIR_SHAPE), stepped((ROWS, C)),
                 fixed((SIDE, SIDE, 16, C)), fixed((8, C)), fixed((1, EXPAND))]
    out_shape = [
        jax.ShapeDtypeStruct((PANES, ROWS, 3 * C), jnp.bfloat16),
        jax.ShapeDtypeStruct((PANES, 16, 2) + PAIR_SHAPE, jnp.bfloat16),
        jax.ShapeDtypeStruct((PANES, ROWS, C), jnp.bfloat16),
        jax.ShapeDtypeStruct((SIDE, SIDE, 16, C), jnp.float32),
        jax.ShapeDtypeStruct((8, C), jnp.float32),
        jax.ShapeDtypeStruct((1, EXPAND), jnp.float32),
    ]
    scratch = [
        pltpu.VMEM((ROWS, C), jnp.bfloat16),
        pltpu.VMEM((12, QUERY_ROWS * 16, QUAD), jnp.float32),
        pltpu.VMEM((4, QUERY_ROWS * 16, QUAD), jnp.float32),
        pltpu.VMEM((2,) + PAIR_SHAPE, jnp.float32),
    ]
    in_specs = [fixed((SIDE, SIDE, 16, C)), fixed((2,) + PAIR_SHAPE), stepped(PAIR_SHAPE)]
    if linked:
        in_specs += [anywhere] * 5
        out_specs += [anywhere] * 2
        out_shape += [
            jax.ShapeDtypeStruct((RANKS, NEAR, C), jnp.bfloat16),
            jax.ShapeDtypeStruct((RANKS, FAR, C), jnp.bfloat16),
        ]
        scratch += [
            pltpu.VMEM((RANKS, NEAR, C), jnp.bfloat16),
            pltpu.VMEM((FAR, C), jnp.bfloat16),
            pltpu.SemaphoreType.DMA((12,)),
        ] + [pltpu.SemaphoreType.DMA((31,))] * 4
        extra = dict(collective_id=0, has_side_effects=True)
    else:
        in_specs += [fixed((RANKS, NEAR, C))]
        extra = {}
    return pl.pallas_call(
        functools.partial(attend_kernel, linked),
        grid=(PANES,),
        in_specs=in_specs,
        out_specs=out_specs,
        out_shape=out_shape,
        scratch_shapes=scratch,
        compiler_params=pltpu.CompilerParams(
            vmem_limit_bytes=62 << 20, dimension_semantics=("arbitrary",), **extra
        ),
        name="attend",
    )(x, bias, mask, *weights)


def attend_back_kernel(linked, *refs):
    x_ref, near_ref, joint_ref, probs_ref, mixed_ref, rgrad_ref, bias_ref, *refs = refs
    if linked:
        far_parts, *refs = refs
    dx_ref, part_ref, vec_ref, pairs_ref, *refs = refs
    if linked:
        ge_ref, gr_ref, *refs = refs
    window, rwindow, wide, blend, turned, wj_acc, wo_acc, *refs = refs
    pane = pl.program_id(0)
    if linked:
        place = Place()
        distant = Reduce(place, far_parts, refs)

    @pl.when(pane == 0)
    def _():
        if linked:
            place.greet()
            distant.start()
        wide[...] = jnp.zeros_like(wide)
        blend[...] = jnp.zeros_like(blend)
        wj_acc[...] = jnp.zeros_like(wj_acc)
        wo_acc[...] = jnp.zeros_like(wo_acc)
        vec_ref[...] = jnp.zeros_like(vec_ref)
        pairs_ref[...] = jnp.zeros_like(pairs_ref)

    if linked:
        @pl.when(pane == 1)
        def _():
            distant.cores()

        @pl.when(pane == 2)
        def _():
            distant.sides()

        @pl.when(pane == 3)
        def _():
            distant.corners()

    take_pane(pane, x_ref, window)
    take_pane(pane, rgrad_ref, rwindow)
    pulled = rwindow[...].astype(jnp.bfloat16)
    wo = near_ref[:, 48:64, :].reshape(C, C)
    wo_acc[...] += dot_tn(mixed_ref[0], pulled)
    vec_ref[0:1] += column_sum(pulled.astype(jnp.float32))
    put_tiles(blend, 0, dot_nt(pulled, wo).astype(jnp.bfloat16).astype(jnp.float32))
    for b in range(3):
        put_tiles(wide, b * 4, joint_ref[0, :, b * C : (b + 1) * C].astype(jnp.float32))

    def per_image(m, carry):
        few, many = pl.ds(m, QUERY_ROWS, stride=16), pl.ds(m, KEY_ROWS, stride=16)
        for pair in range(2):
            q = two_blocks(wide, 2 * pair, few)
            k = spread_heads(load_pair(wide, 4 + 2 * pair, many))
            v = spread_heads(load_pair(wide, 8 + 2 * pair, many))
            pull = two_blocks(blend, 2 * pair, few)
            probs = probs_ref[0, m, pair]
            wider = probs.astype(jnp.float32)
            weighted = dot_nt(v, pull) * wider
            sgrad = (weighted - wider * over_keys(jnp.sum, weighted)).astype(jnp.bfloat16)
            pairs_ref[pair] += sgrad.astype(jnp.float32)
            qgrad = dot_tn(sgrad, k) * SCALE
            turned[2 * pair, many, :] = qgrad[0:KEY_ROWS, 0:QUAD]
            turned[2 * pair + 1, many, :] = qgrad[QUERY_ROWS : QUERY_ROWS + KEY_ROWS, QUAD:]
            kgrad = merge_heads(dot_nn(sgrad, q)) * SCALE
            turned[4 + 2 * pair, many, :] = kgrad[:, 0:QUAD]
            turned[5 + 2 * pair, many, :] = kgrad[:, QUAD:]
            vgrad = merge_heads(dot_nn(probs, pull))
            turned[8 + 2 * pair, many, :] = vgrad[:, 0:QUAD]
            turned[9 + 2 * pair, many, :] = vgrad[:, QUAD:]
        return carry

    lax.fori_loop(0, 16, per_image, 0, unroll=2)
    gain = bias_ref[0:1]
    xhat, rate = norm_parts(window[...].astype(jnp.float32))
    normed = (xhat * gain + bias_ref[1:2]).astype(jnp.bfloat16)
    normed_t = normed.T
    total = jnp.zeros((ROWS, C), jnp.float32)
    for b in range(3):
        weight = near_ref[:, b * 16 : (b + 1) * 16, :].reshape(C, C)
        block = get_tiles(turned, b * 4).astype(jnp.bfloat16)
        wj_acc[b] += dot_nn(normed_t, block)
        total += dot_nt(block, weight)
        if b != 1:
            vec_ref[1 + b // 2 : 2 + b // 2] += column_sum(block.astype(jnp.float32))
    vec_ref[3:4] += column_sum(total * xhat)
    vec_ref[4:5] += column_sum(total)
    dx = rwindow[...] + norm_pull(total, gain, xhat, rate)
    give_pane(pane, dx.astype(jnp.bfloat16), dx_ref)

    @pl.when(pane == PANES - 1)
    def _():
        for b in range(3):
            part_ref[:, b * 16 : (b + 1) * 16, :] = wj_acc[b].reshape(RANKS, 16, C).astype(jnp.bfloat16)
        part_ref[:, 48:64, :] = wo_acc[...].reshape(RANKS, 16, C).astype(jnp.bfloat16)
        if linked:
            total = distant.finish()
            for b in range(4):
                ge_ref[:, b * C : (b + 1) * C] = total[b * 16 : (b + 1) * 16]
            gr_ref[...] = total[64:128]
            distant.drain()


def attend_back(x, near, joint, probs, mixed, rgrad, vectors, far_parts, linked):
    in_specs = [fixed((SIDE, SIDE, 16, C)), fixed((RANKS, NEAR, C)), stepped((ROWS, 3 * C)),
                stepped((16, 2) + PAIR_SHAPE), stepped((ROWS, C)), fixed((SIDE, SIDE, 16, C)), fixed((8, C))]
    out_specs = [fixed((SIDE, SIDE, 16, C)), fixed((RANKS, 64, C)), fixed((8, C)), fixed((2,) + PAIR_SHAPE)]
    out_shape = [
        jax.ShapeDtypeStruct((SIDE, SIDE, 16, C), jnp.bfloat16),
        jax.ShapeDtypeStruct((RANKS, 64, C), jnp.bfloat16),
        jax.ShapeDtypeStruct((8, C), jnp.float32),
        jax.ShapeDtypeStruct((2,) + PAIR_SHAPE, jnp.float32),
    ]
    scratch = [
        pltpu.VMEM((ROWS, C), jnp.bfloat16),
        pltpu.VMEM((ROWS, C), jnp.float32),
        pltpu.VMEM((12, QUERY_ROWS * 16, QUAD), jnp.float32),
        pltpu.VMEM((4, QUERY_ROWS * 16, QUAD), jnp.float32),
        pltpu.VMEM((12, QUERY_ROWS * 16, QUAD), jnp.float32),
        pltpu.VMEM((3, C, C), jnp.float32),
        pltpu.VMEM((C, C), jnp.float32),
    ]
    operands = [x, near, joint, probs, mixed, rgrad, vectors]
    extra = {}
    if linked:
        in_specs.append(pl.BlockSpec(memory_space=pl.ANY))
        out_specs += [fixed((16, EXPAND)), fixed((64, C))]
        out_shape += [
            jax.ShapeDtypeStruct((16, EXPAND), jnp.float32),
            jax.ShapeDtypeStruct((64, C), jnp.float32),
        ]
        scratch += Reduce.scratch(FAR)
        operands.append(far_parts.reshape(4, 2, 2, 2, FAR, C))
        extra = dict(collective_id=1, has_side_effects=True)
    return pl.pallas_call(
        functools.partial(attend_back_kernel, linked),
        grid=(PANES,),
        in_specs=in_specs,
        out_specs=out_specs,
        out_shape=out_shape,
        scratch_shapes=scratch,
        compiler_params=pltpu.CompilerParams(
            vmem_limit_bytes=(1 << 26) - (64 << 10), dimension_semantics=("arbitrary",), **extra
        ),
        name="attend_back",
    )(*operands)


def pair_tables(bias_table, regions):
    keys, queries = jnp.arange(KEY_ROWS), jnp.arange(QUERY_ROWS)
    real = (keys < SPOTS)[:, None] & (queries < SPOTS)[None, :]
    cells = (
        (queries[None, :] // WIN - keys[:, None] // WIN + WIN - 1) * (2 * WIN - 1)
        + queries[None, :] % WIN - keys[:, None] % WIN + WIN - 1
    )
    cells = jnp.where(real, cells, -1).reshape(-1)
    onehot = (cells[None, :] == jnp.arange((2 * WIN - 1) ** 2)[:, None]).astype(jnp.bfloat16)
    bias = dot_tn(bias_table, onehot).reshape(2, 2, 4, KEY_ROWS, QUERY_ROWS)
    bias = jnp.where((keys < SPOTS)[:, None], bias, -1e30)
    bias = bias.transpose(0, 2, 3, 1, 4).reshape((2,) + PAIR_SHAPE)
    labels = jnp.roll(regions, (-SHIFT, -SHIFT), axis=(0, 1)).reshape(2, WIN, 2, WIN)
    labels = labels.transpose(0, 2, 1, 3).reshape(PANES, SPOTS)
    along = jnp.tile(jnp.pad(labels, ((0, 0), (0, KEY_ROWS - SPOTS))), (1, 4))
    across = jnp.tile(jnp.pad(labels, ((0, 0), (0, QUERY_ROWS - SPOTS))), (1, 2))
    mask = jnp.where(along[:, :, None] == across[:, None, :], 0.0, -100.0).astype(jnp.float32)
    return bias, mask, onehot


def table_sums(pairs, onehot):
    heads = pairs.reshape(2, 4, KEY_ROWS, 2, QUERY_ROWS).transpose(0, 3, 1, 2, 4)
    return lax.dot_general(
        heads.reshape(HEADS, KEY_ROWS * QUERY_ROWS), onehot.astype(jnp.float32), (((1,), (1,)), ((), ())),
        precision=exact_mode, preferred_element_type=jnp.float32,
    )

def regroup(packed, blocks, rows):
    count = packed.shape[0] // RANKS
    return (
        packed.reshape(RANKS, count, blocks, rows, C)
        .transpose(0, 2, 1, 3, 4)
        .reshape(RANKS, blocks * rows * count, C)
    )


def ungroup(parts, blocks, ranks):
    rows = parts.shape[1] // blocks
    flat = parts.reshape(RANKS, blocks, rows, C).transpose(1, 0, 2, 3).reshape(blocks, RANKS * rows, C)
    return flat.reshape(blocks, ranks, RANKS * rows // ranks, C).transpose(1, 0, 2, 3)


def on_device(
    images,
    first_gain,
    first_shift,
    joint_weight,
    joint_bias,
    output_weight,
    output_bias,
    second_gain,
    second_shift,
    expand_weight,
    expand_bias,
    reduce_weight,
    reduce_bias,
    bias_table,
    regions,
    live_slots,
    cotangent,
):
    ranks = lax.axis_size("dp")
    count = images.shape[0]
    linked = ranks == RANKS
    small = (
        first_gain,
        first_shift,
        joint_bias[0],
        joint_bias[1],
        output_bias,
        second_gain,
        second_shift,
        reduce_bias,
        expand_bias,
    )
    x = images.transpose(1, 2, 0, 3)
    cot = cotangent.transpose(1, 2, 0, 3).reshape(-1, C)
    bias, mask, onehot = pair_tables(bias_table, regions)
    if linked:
        start, row = 0, jnp.zeros((C,), jnp.float32)
        for vector in small:
            size = vector.shape[0]
            row += jnp.pad(vector.astype(jnp.float32), (start, C - start - size))
            start += size
        row = jnp.pad(row.astype(jnp.bfloat16)[None], ((0, 15), (0, 0)))
        weights = (joint_weight, output_weight, expand_weight, reduce_weight, row)
        joint, probs, mixed, res, vectors, ebias, near, far = attend(x, bias, mask, weights, True)
    else:
        rows = C // ranks
        wide = lambda w: lax.all_gather(w, "dp", axis=0)
        near = jnp.concatenate(
            [wide(joint_weight[:, i * C : (i + 1) * C]) for i in range(3)] + [wide(output_weight)], axis=1
        )
        row = jnp.concatenate(
            [lax.all_gather(v, "dp", axis=0, tiled=True).reshape(RANKS, -1) for v in small], axis=1
        )
        row = jnp.pad(row[:, None], ((0, 0), (0, 15), (0, C - row.shape[1])))
        near = jnp.concatenate([regroup(near, 4, rows), row], axis=1)
        far = jnp.concatenate([wide(expand_weight[:, i * C : (i + 1) * C]) for i in range(4)], axis=1)
        far = jnp.concatenate([regroup(far, 4, rows), wide(reduce_weight).reshape(RANKS, 64, C)], axis=1)
        joint, probs, mixed, res, vectors, ebias = attend(x, bias, mask, (near,), False)
    out, rgrad, far_part, far_vec = mlp_block(
        res.reshape(-1, C), cot, live_slots[:, None], far, vectors, ebias
    )
    rgrad = rgrad.reshape(SIDE, SIDE, count, C)
    dx, near_part, near_vec, pairs, *far_grads = attend_back(
        x, near, joint, probs, mixed, rgrad, vectors, far_part, linked
    )
    table = table_sums(pairs, onehot)
    if linked:
        ge, gr = far_grads
        gj, go, table, jb, eb, *own = reduce_near(near_part, near_vec, far_vec, table)
        own = [v.reshape(-1) for v in own]
        ob, gain1, shift1, gain2, shift2, rb = own
        eb = eb.reshape(-1)
    else:
        scatter = lambda g: lax.psum_scatter(g.astype(jnp.float32), "dp", scatter_dimension=0, tiled=True)
        cut = lambda part, blocks: scatter(
            ungroup(part, blocks, ranks).transpose(0, 2, 1, 3).reshape(C, blocks * C)
        )
        gj, go = cut(near_part[:, :48], 3), cut(near_part[:, 48:], 1)
        ge, gr = cut(far_part[:, :64], 4), scatter(far_part[:, 64:].reshape(EXPAND, C))
        ob, qb, vb, gain1, shift1 = [scatter(near_vec[i]) for i in range(5)]
        gain2, shift2, rb = [scatter(far_vec[i]) for i in range(3)]
        eb, jb = scatter(far_vec[3:7].reshape(-1)), jnp.stack([qb, vb])
        table = lax.psum(table, "dp")
    image_order = lambda v: v.reshape(SIDE, SIDE, count, C).transpose(2, 0, 1, 3)
    return (
        image_order(out),
        image_order(dx),
        gain1,
        shift1,
        gj,
        jb,
        go,
        ob,
        gain2,
        shift2,
        ge,
        eb,
        gr,
        rb,
        table.T,
    )


def solution(mesh):
    in_specs = (
        P("dp", None, None, None),
        P("dp"),
        P("dp"),
        P("dp", None),
        P(None, "dp"),
        P("dp", None),
        P("dp"),
        P("dp"),
        P("dp"),
        P("dp", None),
        P("dp"),
        P("dp", None),
        P("dp"),
        P(),
        P(),
        P("dp"),
        P("dp", None, None, None),
    )
    out_specs = (
        P("dp", None, None, None),
        P("dp", None, None, None),
        P("dp"),
        P("dp"),
        P("dp", None),
        P(None, "dp"),
        P("dp", None),
        P("dp"),
        P("dp"),
        P("dp"),
        P("dp", None),
        P("dp"),
        P("dp", None),
        P("dp"),
        P(),
    )
    return jax.shard_map(
        on_device, mesh=mesh, in_specs=in_specs, out_specs=out_specs, check_vma=False
    )
```

time: 441 us -> 287 us (0.65)
  Pallas kernels: 400 us -> 259 us
  local copies, waits for them, and re-layouts: 32.2 us -> 20.5 us
    pallas_call x4 -> x3, Pallas kernels: 330 us -> 188 us  [the longest x1 83.5 us: attend_back(): pl.pallas_call(functools.partial(attend_back_kernel, linked), grid=(PANES...]
    concatenate x5 -> x0, local copies, waits for them, and re-layouts: 6.31 us -> none  [the longest x1 4.76 us: pack_shards(): jnp.concatenate([row, tail]).reshape(16, C)]
    unnamed x22 -> x26, local copies, waits for them, and re-layouts: 7.11 us -> 13.4 us
    slice x9 -> x0, local copies, waits for them, and re-layouts: 5.66 us -> none  [the longest x1 1.57 us: on_device(): gfar[64:]]
    reshape x16 -> x5, local copies, waits for them, and re-layouts: 7.36 us -> 2.62 us  [the longest x2 1.39 us: table_sums(): pairs.reshape(2, 4, KEY_ROWS, 2, QUERY_ROWS).transpose(0, 3, 1, 2, 4)]
where the time goes in v3:
time: 287 us; the launch traced here: 286 us
  Pallas kernels  259 us (90%)
  local copies, waits for them, and re-layouts  20.5 us (7%)
  matrix products  3.15 us (1%)
    pallas_call x1, Pallas kernels, attend_back(): pl.pallas_call(functools.partial(attend_back_kernel, linked), grid=(PANES...  83.5 us
    pallas_call x1, Pallas kernels, attend(): pl.pallas_call(functools.partial(attend_kernel, linked), grid=(PANES,), i...  77.8 us
    pallas_call x1, Pallas kernels, mlp_block(): pl.pallas_call(mlp_kernel, grid=(tokens // rows,), in_specs=[moving, movi...  70.6 us
    pallas_call x1, Pallas kernels, reduce_near(): pl.pallas_call(reduce_near_kernel, out_shape=[jax.ShapeDtypeStruct((16, 3...  27 us
    unnamed x26, local copies, waits for them, and re-layouts  13.4 us

profile of v3, /device:TPU:0, one launch (start us, length us, event | category | flops | bytes accessed | tf_op | source)
XLA Modules:
  0.0 286.0 jit_solution(109363577488202067)
XLA Ops:
  0.7 0.7 slice_bitcast_fusion.1
  1.4 0.8 add_convert_fusion
  2.3 0.7 slice.23
  3.0 0.7 slice.22
  3.7 0.1 slice_add_fusion
  3.8 0.1 pad_add_fusion.1
  3.8 0.1 reshape.234
  3.9 0.1 reshape.235
  4.0 0.1 tile.19
  4.1 0.1 tile.17
  4.2 1.3 copy.36.live_ref
  5.5 0.6 pad.95.refs_7_
  6.2 0.1 add_select_fusion
  6.2 0.1 reshape.255
  6.3 0.0 copy-start.5
  6.3 0.6 copy-done.5
  6.9 1.2 convolution_bitcast_fusion
  8.1 0.1 reshape.232
  8.3 0.5 fusion.3
  8.8 1.0 reshape.233.refs_1_
  9.8 1.0 compare_select_fusion.refs_2_
  10.7 77.8 %attend.1 = (bf16[4,784,1536]{2,1,0:T(8,128)(2,1)}, bf16[4,16,2,224,128]{4,3,2,1,0:T(8,128)(2,1)}, bf16[4,784,512]{2,1,0:T(8,128)(2,1)}, f32[14,14,16,512]{3,2,1...) custom-call(bf16[14,14,16,512]{3,2,1,0:T(8,128)(2,1)} %bitcast.48, ...), custom_call_target="tpu_custom_call" | custom-call | tf_op jit(solution)/shard_map/attend/pallas_call | solution.py:703
  88.6 70.6 %mlp_block.1 = (bf16[3136,512]{1,0:T(8,128)(2,1)}, f32[3136,512]{1,0:T(8,128)}, bf16[32,128,512]{2,1,0:T(8,128)(2,1)}, f32[8,512]{1,0:T(8,128)}) custom-call(f32[3136,512]{1,0:T(8,128)} %bitcast.50, bf16[3136,512]{1,0:T(8,128)(2,1)} %bitcast.53, s32[16,1]{1,0:T(8,128)} %copy.36.live_ref, bf16[32,128,512]{2,1,0:T(8,128)(2,1)} %get-tuple-element.45.far_ref, ...), custom_call_target="tpu_custom_call" | custom-call | tf_op jit(solution)/shard_map/mlp_block/pallas_call | solution.py:440
  159.2 83.5 %attend_back.1 = (bf16[14,14,16,512]{3,2,1,0:T(8,128)(2,1)}, bf16[32,64,512]{2,1,0:T(8,128)(2,1)}, f32[8,512]{1,0:T(8,128)}, f32[2,224,128]{2,1,0:T(8,128)}, f32[16,2048]{1,0:T(8,128)}, /*index=5*/f32[64,512]{1,0:T(8,128)}) custom-call(bf16[14,14,16,512]{3,2,1,0:T(8,128)(2,1)} %bitcast.49, bf16[32,80,512]{2,1,0:T(8,128)(2,1)} %get-tuple-element.49.refs_1_, ...), custom_call_target="tpu_custom_call" | custom-call | tf_op jit(solution)/shard_map/attend_back/pallas_call | solution.py:850
  242.7 0.0 copy-start
  242.7 1.4 reshape.242
  244.1 0.1 reshape.243
  244.2 1.9 fusion.table_ref
  246.2 0.0 copy-done
  246.2 0.0 copy-start.1
  246.2 0.7 copy-done.1
  246.9 0.0 copy-start.2
  246.9 0.7 copy-done.2
  247.6 27.0 %reduce_near.1 = (f32[16,1536]{1,0:T(8,128)S(1)}, f32[16,512]{1,0:T(8,128)S(1)}, f32[16,169]{1,0:T(8,128)S(1)}, f32[2,16]{1,0:T(2,128)S(1)}, f32[1,64]{1,0:T(1,1...) custom-call(bf16[4,2,2,2,64,512]{5,4,3,2,1,0:T(8,128)(2,1)S(1)} %bit, ...), custom_call_target="tpu_custom_call" | custom-call | tf_op jit(solution)/shard_map/reduce_near/pallas_call | solution.py:309
  274.7 0.0 copy-start.4
  274.7 0.0 copy-start.3
  274.7 4.0 %copy.59 = bf16[16,14,14,512]{3,0,2,1:T(8,128)(2,1)} copy(bf16[16,14,14,512]{3,0,2,1:T(8,128)(2,1)} %bitcast.54) | data formatting | bytes 6422528
  278.7 0.5 copy.60
  279.2 0.5 copy.61
  279.7 0.6 copy.62
  280.4 0.6 copy.63
  280.9 0.6 copy.64
  281.6 0.5 copy.65
  282.1 0.5 copy.66
  282.6 0.5 copy.67
  283.1 0.0 copy-done.4
  283.1 0.7 copy.68
  283.7 0.5 copy.69
  284.3 0.0 copy-done.3
  284.3 0.7 copy.70
  284.9 0.5 copy.71
  285.4 0.6 copy.72
  (12 shorter events, 0.1 us)
Async XLA Ops:
  6.3 0.6 copy-start.5
  242.7 3.5 %copy-start = (bf16[32,64,512]{2,1,0:T(8,128)(2,1)S(1)}, bf16[32,64,512]{2,1,0:T(8,128)(2,1)}, u32[]{:S(2)}) copy-start(bf16[32,64,512]{2,1,0:T(8,128)(2,1)} %get-tuple-element.56) | copy-start | bytes 6291460
  246.2 0.7 copy-start.1
  246.9 0.7 copy-start.2
  274.7 8.4 %copy-start.4 = (f32[16,2048]{1,0:T(8,128)S(1)}, f32[16,2048]{1,0:T(8,128)}, u32[]{:S(2)}) copy-start(f32[16,2048]{1,0:T(8,128)} %get-tuple-element.104) | copy-start | bytes 393220
  274.7 9.6 %copy-start.3 = (f32[64,512]{1,0:T(8,128)S(1)}, f32[64,512]{1,0:T(8,128)}, u32[]{:S(2)}) copy-start(f32[64,512]{1,0:T(8,128)} %get-tuple-element.106) | copy-start | bytes 393220

commit v4 on v3

--- a/solution.py
+++ b/solution.py
@@ -21,7 +21,7 @@
 exact_mode = lax.Precision.HIGHEST
 
 MESH = pl.DeviceIdType.MESH
-NEAR = 80
+NEAR = 48
 FAR = 128
 
 
@@ -128,8 +128,11 @@
 
 
 class Reduce:
-    def __init__(self, place, parts, scratch):
-        self.place, self.parts = place, parts
+    def __init__(self, place, parts, scratch, start=0):
+        self.place = place
+        self.acc = scratch[0]
+        self.cut = pl.ds(start, self.acc.shape[3])
+        self.parts = parts
         self.acc, self.rc, self.r1x, self.r1y, self.r2x, self.r2y, self.rz = scratch[:7]
         self.local, self.send, self.recv = scratch[7:]
 
@@ -145,7 +148,7 @@
     def copies(self, lane):
         p, a = self.place, self.acc
         source, target, rank = {
-            0: lambda: (self.parts.at[:, :, :, 1 - p.c], self.rc, p.mate),
+            0: lambda: (self.parts.at[:, :, :, 1 - p.c, self.cut], self.rc, p.mate),
             1: lambda: (a.at[0:2, :, 1 - p.x], self.r1x, p.peer_x),
             2: lambda: (a.at[2:4, 1 - p.y, :], self.r1y, p.peer_y),
             3: lambda: (a.at[0:2, 1 - p.y, p.x], self.r2y, p.peer_y),
@@ -157,7 +160,7 @@
         return remote(source, target, self.send.at[lane], self.recv.at[lane], rank)
 
     def mine(self):
-        return pltpu.make_async_copy(self.parts.at[:, :, :, self.place.c], self.acc, self.local)
+        return pltpu.make_async_copy(self.parts.at[:, :, :, self.place.c, self.cut], self.acc, self.local)
 
     def add(self, where, other):
         total = self.acc[where].astype(jnp.float32) + other.astype(jnp.float32)
@@ -255,37 +258,50 @@
             self.copies(lane).wait_send()
 
 
+HALVES = 2
+HALF = 64 // HALVES
+
+
 def reduce_near_kernel(
     parts, near_vec, far_vec, table_ref,
     gj_ref, go_ref, table_out, jb_ref, eb_ref, *rest,
 ):
-    owns = rest[:7]
-    spread = rest[7]
-    reduce_scratch, vec_scratch, table_scratch = rest[8:18], rest[18:22], rest[22:26]
+    owns, rest = rest[:6], rest[6:]
+    bias_scratch, spread, rest = rest[0], rest[1], rest[2:]
+    bigs, rest = [rest[i * 10 : i * 10 + 10] for i in range(HALVES)], rest[10 * HALVES :]
     place = Place()
     place.greet()
-    big = Reduce(place, parts, reduce_scratch)
-    vec = Swap(place, vec_scratch)
-    tab = Swap(place, table_scratch)
-    big.start()
+    bigs = [Reduce(place, parts, scratch, i * HALF) for i, scratch in enumerate(bigs)]
+    vec = Swap(place, rest[0:4])
+    tab = Swap(place, rest[4:8])
+    for big in bigs:
+        big.start()
     vec.own[0, 0:8] = near_vec[...]
     vec.own[0, 8:16] = far_vec[...]
     tab.own[0] = table_ref[...]
     vec.copies(0).start()
     tab.copies(0).start()
-    big.cores()
+    for big in bigs:
+        big.cores()
     vec.hop(0)
     tab.hop(0)
-    big.sides()
+    for big in bigs:
+        big.sides()
     vec.hop(1)
     tab.hop(1)
-    big.corners()
+    for big in bigs:
+        big.corners()
     vec.hop(2)
     tab.hop(2)
-    total = big.finish()
-    for b in range(3):
-        gj_ref[:, b * C : (b + 1) * C] = total[b * 16 : (b + 1) * 16]
-    go_ref[...] = total[48:64]
+    for i, big in enumerate(bigs):
+        total = big.finish()
+        for block in range(HALF // 16):
+            b = i * (HALF // 16) + block
+            rows = total[block * 16 : (block + 1) * 16]
+            if b < 3:
+                gj_ref[:, b * C : (b + 1) * C] = rows
+            else:
+                go_ref[...] = rows
     sums = vec.finish()
     table_out[...] = tab.finish()
     for tile in range(4):
@@ -297,16 +313,20 @@
     for own, row in zip(owns, (0, 3, 4, 8, 9, 10)):
         own[...] = mine[row : row + 1]
     wide = pltpu.roll(spread[lax.rem(me, 8) // 2], 64 * lax.rem(me, 2), 1)[:, 0:64]
-    owns[6][...] = wide[8:16]
-    eb_ref[...] = owns[6][pl.ds(3 + me // 8, 1), :]
-    big.drain()
+    bias_scratch[...] = wide[8:16]
+    eb_ref[...] = bias_scratch[pl.ds(3 + me // 8, 1), :]
+    for big in bigs:
+        big.drain()
     vec.drain()
     tab.drain()
 
 
 def reduce_near(parts, near_vec, far_vec, table):
     one = jax.ShapeDtypeStruct((1, 16), jnp.float32)
-    outs = pl.pallas_call(
+    scratch = [pltpu.VMEM((8, 64), jnp.float32), pltpu.VMEM((4, 16, 128), jnp.float32)]
+    for _ in range(HALVES):
+        scratch += Reduce.scratch(HALF)
+    return pl.pallas_call(
         reduce_near_kernel,
         out_shape=[
             jax.ShapeDtypeStruct((16, 3 * C), jnp.float32),
@@ -318,16 +338,32 @@
         + [one] * 6,
         in_specs=[pl.BlockSpec(memory_space=pl.ANY)] + [pl.BlockSpec(memory_space=pltpu.VMEM)] * 3,
         out_specs=[pl.BlockSpec(memory_space=pltpu.VMEM)] * 11,
-        scratch_shapes=[pltpu.VMEM((8, 64), jnp.float32), pltpu.VMEM((4, 16, 128), jnp.float32)]
-        + Reduce.scratch(64)
-        + Swap.scratch((16, C))
-        + Swap.scratch(table.shape),
+        scratch_shapes=scratch + Swap.scratch((16, C)) + Swap.scratch(table.shape),
         compiler_params=pltpu.CompilerParams(
             collective_id=2, has_side_effects=True, vmem_limit_bytes=40 << 20
         ),
         name="reduce_near",
     )(parts.reshape(4, 2, 2, 2, 64, C), near_vec, far_vec, table)
-    return outs
+
+
+def settle_kernel(count, *refs):
+    for source, target in zip(refs[:count], refs[count:]):
+        target[...] = source[...]
+
+
+def settle(dx, others):
+    steps = SIDE // 2
+    block = pl.BlockSpec((2, SIDE, 16, C), lambda i: (i, 0, 0, 0))
+    whole = [pl.BlockSpec(v.shape, lambda i: (0, 0), pipeline_mode=pl.Buffered(1)) for v in others]
+    return pl.pallas_call(
+        functools.partial(settle_kernel, 1 + len(others)),
+        grid=(steps,),
+        in_specs=[block] + whole,
+        out_specs=[block] + whole,
+        out_shape=[jax.ShapeDtypeStruct(v.shape, v.dtype) for v in (dx, *others)],
+        compiler_params=pltpu.CompilerParams(dimension_semantics=("arbitrary",)),
+        name="settle",
+    )(dx, *others)
 
 ERFC_SLOPE = 0.4
 ERFC_TERMS = (
@@ -384,7 +420,7 @@
 
 def mlp_kernel(
     res_ref, cot_ref, live_ref, far_ref, bias_ref, ebias_ref,
-    out_ref, rgrad_ref, part_ref, vec_ref, we_acc, wr_acc,
+    out_ref, rgrad_ref, part_ref, vec_ref, we_acc, wr_acc, act, hg,
 ):
     step = pl.program_id(0)
     rows = res_ref.shape[0]
@@ -399,26 +435,31 @@
     gain = bias_ref[5:6]
     xhat, rate = norm_parts(res)
     second = (xhat * gain + bias_ref[6:7]).astype(jnp.bfloat16)
+    slot = lax.broadcasted_iota(jnp.int32, (16, 1), 0)
+    live = jnp.zeros((16, 1), jnp.float32)
+    for i in range(16):
+        live = jnp.where(slot == i, live_ref[i].astype(jnp.float32), live)
     upstream = (
-        cot_ref[...].astype(jnp.float32).reshape(rows // 16, 16, C) * live_ref[...].astype(jnp.float32)[None]
+        cot_ref[...].astype(jnp.float32).reshape(rows // 16, 16, C) * live[None]
     ).reshape(rows, C)
     low = upstream.astype(jnp.bfloat16)
     second_t = second.T
     low_t = low.T
-    reduced = jnp.zeros((rows, C), jnp.float32)
-    pulled = jnp.zeros((rows, C), jnp.float32)
     for b in range(4):
+        cut = slice(b * C, (b + 1) * C)
         we = far_ref[:, b * 16 : (b + 1) * 16, :].reshape(C, C)
+        hidden = dot_nn(second, we) + ebias_ref[:, cut]
+        active, slope = gelu_pair(hidden)
+        act[:, cut] = active.astype(jnp.bfloat16)
         wr = far_ref[b * 8 : (b + 1) * 8, 64:128, :].reshape(C, C)
-        hidden = dot_nn(second, we) + ebias_ref[:, b * C : (b + 1) * C]
-        active, slope = gelu_pair(hidden)
-        active = active.astype(jnp.bfloat16)
-        reduced += dot_nn(active, wr)
-        hgrad = (dot_nt(low, wr) * slope).astype(jnp.bfloat16)
-        pulled += dot_nt(hgrad, we)
-        wr_acc[b] += dot_nn(low_t, active)
-        we_acc[b] += dot_nn(second_t, hgrad)
-        vec_ref[3 + b : 4 + b] += column_sum(hgrad.astype(jnp.float32))
+        hg[:, cut] = (dot_nt(low, wr) * slope).astype(jnp.bfloat16)
+    reduced = dot_nn(act[...], far_ref[:, 64:128, :].reshape(EXPAND, C))
+    pulled = dot_nt(hg[...], jnp.concatenate([far_ref[:, b * 16 : (b + 1) * 16, :].reshape(C, C) for b in range(4)], axis=1))
+    for b in range(4):
+        cut = slice(b * C, (b + 1) * C)
+        wr_acc[b] += dot_nn(low_t, act[:, cut])
+        we_acc[b] += dot_nn(second_t, hg[:, cut])
+        vec_ref[3 + b : 4 + b] += column_sum(hg[:, cut].astype(jnp.float32))
     out_ref[...] = (res + reduced + bias_ref[7:8]).astype(jnp.bfloat16)
     rgrad_ref[...] = upstream + norm_pull(pulled, gain, xhat, rate)
     vec_ref[0:1] += column_sum(pulled * xhat)
@@ -440,7 +481,7 @@
     return pl.pallas_call(
         mlp_kernel,
         grid=(tokens // rows,),
-        in_specs=[moving, moving, fixed((16, 1)), fixed((RANKS, FAR, C)), fixed((8, C)), fixed((1, EXPAND))],
+        in_specs=[moving, moving, pl.BlockSpec(memory_space=pltpu.SMEM), fixed((RANKS, FAR, C)), fixed((8, C)), fixed((1, EXPAND))],
         out_specs=[moving, moving, fixed((RANKS, FAR, C)), fixed((8, C))],
         out_shape=[
             jax.ShapeDtypeStruct((tokens, C), jnp.bfloat16),
@@ -448,7 +489,7 @@
             jax.ShapeDtypeStruct((RANKS, 128, C), jnp.bfloat16),
             jax.ShapeDtypeStruct((8, C), jnp.float32),
         ],
-        scratch_shapes=[pltpu.VMEM((4, C, C), jnp.float32), pltpu.VMEM((4, C, C), jnp.float32)],
+        scratch_shapes=[pltpu.VMEM((4, C, C), jnp.float32), pltpu.VMEM((4, C, C), jnp.float32), pltpu.VMEM((rows, EXPAND), jnp.bfloat16), pltpu.VMEM((rows, EXPAND), jnp.bfloat16)],
         compiler_params=pltpu.CompilerParams(vmem_limit_bytes=60 << 20, dimension_semantics=("arbitrary",)),
         name="mlp_block",
     )(res, cot, live, far, vectors, ebias)
@@ -525,24 +566,20 @@
     return jnp.broadcast_to(op(parts, axis=1, keepdims=True), parts.shape).reshape(value.shape)
 
 
-def bias_rows(near, vec_ref, ebias_ref):
-    rows = jnp.sum(near[:, 64:80, 0:256].astype(jnp.float32), axis=1)
-    lane = lax.broadcasted_iota(jnp.int32, (RANKS, 256), 1)
-    parts = [jnp.where(lane // 16 == i, rows, 0.0) for i in range(8)]
-    parts = jnp.concatenate(parts, axis=0).astype(jnp.bfloat16)
+def bias_rows(rows, vec_ref, ebias_ref):
+    values = rows[...].astype(jnp.float32)
 
     def taken(lhs, width):
-        source = lax.broadcasted_iota(jnp.int32, (256, RANKS * width), 0)
-        target = lax.broadcasted_iota(jnp.int32, (256, RANKS * width), 1)
-        onehot = jnp.where(lax.rem(source, width) == lax.rem(target, width), 1.0, 0.0).astype(jnp.bfloat16)
-        count = lhs.shape[0]
-        shard = lax.rem(lax.broadcasted_iota(jnp.int32, (count, RANKS * width), 0), RANKS)
-        place = lax.broadcasted_iota(jnp.int32, (count, RANKS * width), 1) // width
-        return jnp.where(shard == place, dot_nn(lhs, onehot), 0.0)
-
-    vec_ref[...] = jnp.sum(taken(parts, 16).reshape(8, RANKS, C), axis=1)
-    tail = jnp.where(lane // 64 == 2, rows, 0.0).astype(jnp.bfloat16)
-    ebias_ref[...] = jnp.sum(taken(tail, 64), axis=0, keepdims=True)
+        source = lax.broadcasted_iota(jnp.int32, (128, RANKS * width), 0)
+        target = lax.broadcasted_iota(jnp.int32, (128, RANKS * width), 1)
+        onehot = jnp.where(source == lax.rem(target, width), 1.0, 0.0).astype(jnp.bfloat16)
+        spread = dot_nn(lhs.reshape(-1, 128).astype(jnp.bfloat16), onehot).reshape(RANKS, -1, RANKS * width)
+        shard = lax.broadcasted_iota(jnp.int32, spread.shape, 0)
+        place = lax.broadcasted_iota(jnp.int32, spread.shape, 2) // width
+        return jnp.sum(jnp.where(shard == place, spread, 0.0), axis=0)
+
+    vec_ref[...] = taken(values[:, 0:8], 16)
+    ebias_ref[...] = taken(values[:, 8:16], 64)[0:1]
 
 
 def attend_kernel(linked, *refs):
@@ -550,31 +587,32 @@
     if linked:
         shards, refs = refs[:5], refs[5:]
     else:
-        near_ref, *refs = refs
+        near, output, rows, *refs = refs
     joint_ref, probs_ref, mixed_ref, res_ref, vec_ref, ebias_ref, *refs = refs
     if linked:
-        near_out, far_out, *refs = refs
-    window, wide, blend, both, *refs = refs
+        near_out, output_out, far_out, *refs = refs
+    window, wide, blend, both, score_a, score_b, probs_a, probs_b, *refs = refs
     pane = pl.program_id(0)
     last = pl.num_programs(0) - 1
     if linked:
-        near, far_own, local, near_send, near_recv, far_send, far_recv = refs
+        near, rows, output, far_own, local, *sems = refs
         place = Place()
-        close = Gather(place, near.at[place.me], near, near_send, near_recv)
-        distant = Gather(place, far_own, far_out, far_send, far_recv)
+        close = Gather(place, near.at[place.me], near, *sems[0:2])
+        little = Gather(place, rows.at[place.me], rows, *sems[2:4])
+        middle = Gather(place, output.at[place.me], output, *sems[4:6])
+        distant = Gather(place, far_own, far_out, *sems[6:8])
         joint_w, output_w, expand_w, reduce_w, row_w = shards
-        own = near.at[place.me]
-        pieces = [(joint_w.at[:, b * C : (b + 1) * C], own.at[b * 16 : (b + 1) * 16]) for b in range(3)]
-        pieces += [(output_w, own.at[48:64]), (row_w, own.at[64:80])]
+        pieces = [
+            (joint_w.at[:, b * C : (b + 1) * C], near.at[place.me].at[b * 16 : (b + 1) * 16]) for b in range(3)
+        ]
+        pieces += [(row_w, rows.at[place.me]), (output_w, output.at[place.me])]
         pieces += [
             (expand_w.at[:, b * C : (b + 1) * C], far_own.at[b * 16 : (b + 1) * 16]) for b in range(4)
         ]
         pieces += [(reduce_w, far_own.at[64:128])]
         pieces = [pltpu.make_async_copy(a, b, local.at[i]) for i, (a, b) in enumerate(pieces)]
-        keep_near = pltpu.make_async_copy(near, near_out, local.at[10])
-        keep_far = pltpu.make_async_copy(far_own, far_out.at[place.me], local.at[11])
-    else:
-        near = near_ref
+        keep = [(near, near_out), (output, output_out), (far_own, far_out.at[place.me])]
+        keep = [pltpu.make_async_copy(a, b, local.at[10 + i]) for i, (a, b) in enumerate(keep)]
 
     @pl.when(pane == 0)
     def _():
@@ -582,25 +620,36 @@
             for piece in pieces:
                 piece.start()
             place.greet()
-            for piece in pieces[:5]:
+            for piece in pieces[:4]:
                 piece.wait()
             close.start()
-            for piece in pieces[5:]:
+            little.start()
+            for piece in pieces[4:]:
                 piece.wait()
-        wide[...] = jnp.zeros_like(wide)
+            middle.start()
+            keep[2].start()
+        wide[:, ROWS:, :] = jnp.zeros((12, QUERY_ROWS * 16 - ROWS, QUAD), jnp.float32)
+        probs_b[...] = jnp.zeros_like(probs_b)
         if linked:
             close.relay_columns()
+            little.relay_columns()
             close.relay_sides()
+            little.relay_sides()
+            middle.relay_columns()
+            distant.start()
             close.relay_corners()
-            distant.start()
-            keep_far.start()
+            little.relay_corners()
+            little.finish()
+        bias_rows(rows, vec_ref, ebias_ref)
+        if linked:
             close.finish()
-            keep_near.start()
-        bias_rows(near, vec_ref, ebias_ref)
+            keep[0].start()
+            middle.relay_sides()
 
     if linked:
         @pl.when(pane == 1)
         def _():
+            keep[1].start()
             distant.relay_columns()
 
         @pl.when(pane == 2)
@@ -626,35 +675,67 @@
     for pair in range(2):
         both[pair] = bias_ref[pair] + mask_ref[0]
 
-    def per_image(m, carry):
-        few, many = pl.ds(m, QUERY_ROWS, stride=16), pl.ds(m, KEY_ROWS, stride=16)
+    def rows_of(m):
+        return pl.ds(m, QUERY_ROWS, stride=16), pl.ds(m, KEY_ROWS, stride=16)
+
+    def score(m, target):
+        few, many = rows_of(m)
         for pair in range(2):
-            q = two_blocks(wide, 2 * pair, few)
             k = spread_heads(load_pair(wide, 4 + 2 * pair, many))
-            v = spread_heads(load_pair(wide, 8 + 2 * pair, many))
-            scores = dot_nt(k, q) * SCALE + both[pair]
+            target[pair] = dot_nt(k, two_blocks(wide, 2 * pair, few))
+
+    def soften(m, source, target):
+        for pair in range(2):
+            scores = source[pair] * SCALE + both[pair]
             powers = jnp.exp(scores - over_keys(jnp.max, scores))
             probs = (powers * (1.0 / over_keys(jnp.sum, powers))).astype(jnp.bfloat16)
+            target[pair] = probs
             probs_ref[0, m, pair] = probs
-            blended = dot_tn(probs, v)
+
+    def mix(m, source):
+        few, many = rows_of(m)
+        for pair in range(2):
+            v = spread_heads(load_pair(wide, 8 + 2 * pair, many))
+            blended = dot_tn(source[pair], v)
             blend[2 * pair, many, :] = blended[0:KEY_ROWS, 0:QUAD]
             blend[2 * pair + 1, many, :] = blended[QUERY_ROWS : QUERY_ROWS + KEY_ROWS, QUAD:]
+
+    def two_images(step, carry):
+        m = 2 * step
+        if linked:
+            @pl.when((pane == 0) & (step == 2))
+            def _():
+                middle.relay_corners()
+
+        mix(jnp.maximum(m - 1, 0), probs_b)
+        soften(m, score_a, probs_a)
+        score(m + 1, score_b)
+        mix(m, probs_a)
+        soften(m + 1, score_b, probs_b)
+        score(jnp.minimum(m + 2, 15), score_a)
         return carry
 
-    lax.fori_loop(0, 16, per_image, 0, unroll=2)
+    score(0, score_a)
+    lax.fori_loop(0, 8, two_images, 0)
+    mix(15, probs_b)
+    if linked:
+        @pl.when(pane == 0)
+        def _():
+            middle.finish()
+
     mixed = get_tiles(blend, 0).astype(jnp.bfloat16)
     mixed_ref[0] = mixed
-    projected = dot_nn(mixed, near[:, 48:64, :].reshape(C, C)) + vec_ref[4:5]
+    projected = dot_nn(mixed, output[...].reshape(C, C)) + vec_ref[4:5]
     give_pane(pane, window[...].astype(jnp.float32) + projected, res_ref)
 
     if linked:
         @pl.when(pane == last)
         def _():
             distant.finish()
-            close.drain()
-            distant.drain()
-            keep_near.wait()
-            keep_far.wait()
+            for group in (close, little, middle, distant):
+                group.drain()
+            for kept in keep:
+                kept.wait()
 
 
 def fixed(shape):
@@ -682,23 +763,30 @@
         pltpu.VMEM((12, QUERY_ROWS * 16, QUAD), jnp.float32),
         pltpu.VMEM((4, QUERY_ROWS * 16, QUAD), jnp.float32),
         pltpu.VMEM((2,) + PAIR_SHAPE, jnp.float32),
+        pltpu.VMEM((2,) + PAIR_SHAPE, jnp.float32),
+        pltpu.VMEM((2,) + PAIR_SHAPE, jnp.float32),
+        pltpu.VMEM((2,) + PAIR_SHAPE, jnp.bfloat16),
+        pltpu.VMEM((2,) + PAIR_SHAPE, jnp.bfloat16),
     ]
     in_specs = [fixed((SIDE, SIDE, 16, C)), fixed((2,) + PAIR_SHAPE), stepped(PAIR_SHAPE)]
     if linked:
         in_specs += [anywhere] * 5
-        out_specs += [anywhere] * 2
+        out_specs += [anywhere] * 3
         out_shape += [
             jax.ShapeDtypeStruct((RANKS, NEAR, C), jnp.bfloat16),
+            jax.ShapeDtypeStruct((RANKS, 16, C), jnp.bfloat16),
             jax.ShapeDtypeStruct((RANKS, FAR, C), jnp.bfloat16),
         ]
         scratch += [
             pltpu.VMEM((RANKS, NEAR, C), jnp.bfloat16),
+            pltpu.VMEM((RANKS, 16, 128), jnp.bfloat16),
+            pltpu.VMEM((RANKS, 16, C), jnp.bfloat16),
             pltpu.VMEM((FAR, C), jnp.bfloat16),
-            pltpu.SemaphoreType.DMA((12,)),
-        ] + [pltpu.SemaphoreType.DMA((31,))] * 4
+            pltpu.SemaphoreType.DMA((13,)),
+        ] + [pltpu.SemaphoreType.DMA((31,))] * 8
         extra = dict(collective_id=0, has_side_effects=True)
     else:
-        in_specs += [fixed((RANKS, NEAR, C))]
+        in_specs += [fixed((RANKS, NEAR, C)), fixed((RANKS, 16, C)), fixed((RANKS, 16, 128))]
         extra = {}
     return pl.pallas_call(
         functools.partial(attend_kernel, linked),
@@ -715,13 +803,13 @@
 
 
 def attend_back_kernel(linked, *refs):
-    x_ref, near_ref, joint_ref, probs_ref, mixed_ref, rgrad_ref, bias_ref, *refs = refs
+    x_ref, near_ref, output_ref, joint_ref, probs_ref, mixed_ref, rgrad_ref, bias_ref, *refs = refs
     if linked:
         far_parts, *refs = refs
     dx_ref, part_ref, vec_ref, pairs_ref, *refs = refs
     if linked:
         ge_ref, gr_ref, *refs = refs
-    window, rwindow, wide, blend, turned, wj_acc, wo_acc, *refs = refs
+    window, rwindow, wide, blend, turned, wj_acc, wo_acc, pgrad_a, pgrad_b, sgrad_a, sgrad_b, *refs = refs
     pane = pl.program_id(0)
     if linked:
         place = Place()
@@ -732,8 +820,10 @@
         if linked:
             place.greet()
             distant.start()
-        wide[...] = jnp.zeros_like(wide)
-        blend[...] = jnp.zeros_like(blend)
+        pads = QUERY_ROWS * 16 - ROWS
+        wide[:, ROWS:, :] = jnp.zeros((12, pads, QUAD), jnp.float32)
+        blend[:, ROWS:, :] = jnp.zeros((4, pads, QUAD), jnp.float32)
+        sgrad_b[...] = jnp.zeros_like(sgrad_b)
         wj_acc[...] = jnp.zeros_like(wj_acc)
         wo_acc[...] = jnp.zeros_like(wo_acc)
         vec_ref[...] = jnp.zeros_like(vec_ref)
@@ -755,37 +845,58 @@
     take_pane(pane, x_ref, window)
     take_pane(pane, rgrad_ref, rwindow)
     pulled = rwindow[...].astype(jnp.bfloat16)
-    wo = near_ref[:, 48:64, :].reshape(C, C)
+    wo = output_ref[...].reshape(C, C)
     wo_acc[...] += dot_tn(mixed_ref[0], pulled)
     vec_ref[0:1] += column_sum(pulled.astype(jnp.float32))
     put_tiles(blend, 0, dot_nt(pulled, wo).astype(jnp.bfloat16).astype(jnp.float32))
     for b in range(3):
         put_tiles(wide, b * 4, joint_ref[0, :, b * C : (b + 1) * C].astype(jnp.float32))
 
-    def per_image(m, carry):
-        few, many = pl.ds(m, QUERY_ROWS, stride=16), pl.ds(m, KEY_ROWS, stride=16)
+    def rows_of(m):
+        return pl.ds(m, QUERY_ROWS, stride=16), pl.ds(m, KEY_ROWS, stride=16)
+
+    def pull_probs(m, target):
+        few, many = rows_of(m)
         for pair in range(2):
-            q = two_blocks(wide, 2 * pair, few)
+            v = spread_heads(load_pair(wide, 8 + 2 * pair, many))
+            target[pair] = dot_nt(v, two_blocks(blend, 2 * pair, few))
+
+    def pull_scores(m, source, target):
+        for pair in range(2):
+            probs = probs_ref[0, m, pair].astype(jnp.float32)
+            weighted = source[pair] * probs
+            sgrad = (weighted - probs * over_keys(jnp.sum, weighted)).astype(jnp.bfloat16)
+            target[pair] = sgrad
+            pairs_ref[pair] += sgrad.astype(jnp.float32)
+
+    def pull_rest(m, source):
+        few, many = rows_of(m)
+        for pair in range(2):
+            sgrad = source[pair]
             k = spread_heads(load_pair(wide, 4 + 2 * pair, many))
-            v = spread_heads(load_pair(wide, 8 + 2 * pair, many))
-            pull = two_blocks(blend, 2 * pair, few)
-            probs = probs_ref[0, m, pair]
-            wider = probs.astype(jnp.float32)
-            weighted = dot_nt(v, pull) * wider
-            sgrad = (weighted - wider * over_keys(jnp.sum, weighted)).astype(jnp.bfloat16)
-            pairs_ref[pair] += sgrad.astype(jnp.float32)
             qgrad = dot_tn(sgrad, k) * SCALE
             turned[2 * pair, many, :] = qgrad[0:KEY_ROWS, 0:QUAD]
             turned[2 * pair + 1, many, :] = qgrad[QUERY_ROWS : QUERY_ROWS + KEY_ROWS, QUAD:]
-            kgrad = merge_heads(dot_nn(sgrad, q)) * SCALE
+            kgrad = merge_heads(dot_nn(sgrad, two_blocks(wide, 2 * pair, few))) * SCALE
             turned[4 + 2 * pair, many, :] = kgrad[:, 0:QUAD]
             turned[5 + 2 * pair, many, :] = kgrad[:, QUAD:]
-            vgrad = merge_heads(dot_nn(probs, pull))
+            vgrad = merge_heads(dot_nn(probs_ref[0, m, pair], two_blocks(blend, 2 * pair, few)))
             turned[8 + 2 * pair, many, :] = vgrad[:, 0:QUAD]
             turned[9 + 2 * pair, many, :] = vgrad[:, QUAD:]
+
+    def two_images(step, carry):
+        m = 2 * step
+        pull_rest(jnp.maximum(m - 1, 0), sgrad_b)
+        pull_scores(m, pgrad_a, sgrad_a)
+        pull_probs(m + 1, pgrad_b)
+        pull_rest(m, sgrad_a)
+        pull_scores(m + 1, pgrad_b, sgrad_b)
+        pull_probs(jnp.minimum(m + 2, 15), pgrad_a)
         return carry
 
-    lax.fori_loop(0, 16, per_image, 0, unroll=2)
+    pull_probs(0, pgrad_a)
+    lax.fori_loop(0, 8, two_images, 0)
+    pull_rest(15, sgrad_b)
     gain = bias_ref[0:1]
     xhat, rate = norm_parts(window[...].astype(jnp.float32))
     normed = (xhat * gain + bias_ref[1:2]).astype(jnp.bfloat16)
@@ -816,8 +927,8 @@
             distant.drain()
 
 
-def attend_back(x, near, joint, probs, mixed, rgrad, vectors, far_parts, linked):
-    in_specs = [fixed((SIDE, SIDE, 16, C)), fixed((RANKS, NEAR, C)), stepped((ROWS, 3 * C)),
+def attend_back(x, near, output, joint, probs, mixed, rgrad, vectors, far_parts, linked):
+    in_specs = [fixed((SIDE, SIDE, 16, C)), fixed((RANKS, NEAR, C)), fixed((RANKS, 16, C)), stepped((ROWS, 3 * C)),
                 stepped((16, 2) + PAIR_SHAPE), stepped((ROWS, C)), fixed((SIDE, SIDE, 16, C)), fixed((8, C))]
     out_specs = [fixed((SIDE, SIDE, 16, C)), fixed((RANKS, 64, C)), fixed((8, C)), fixed((2,) + PAIR_SHAPE)]
     out_shape = [
@@ -834,8 +945,12 @@
         pltpu.VMEM((12, QUERY_ROWS * 16, QUAD), jnp.float32),
         pltpu.VMEM((3, C, C), jnp.float32),
         pltpu.VMEM((C, C), jnp.float32),
+        pltpu.VMEM((2,) + PAIR_SHAPE, jnp.float32),
+        pltpu.VMEM((2,) + PAIR_SHAPE, jnp.float32),
+        pltpu.VMEM((2,) + PAIR_SHAPE, jnp.bfloat16),
+        pltpu.VMEM((2,) + PAIR_SHAPE, jnp.bfloat16),
     ]
-    operands = [x, near, joint, probs, mixed, rgrad, vectors]
+    operands = [x, near, output, joint, probs, mixed, rgrad, vectors]
     extra = {}
     if linked:
         in_specs.append(pl.BlockSpec(memory_space=pl.ANY))
@@ -940,39 +1055,41 @@
     cot = cotangent.transpose(1, 2, 0, 3).reshape(-1, C)
     bias, mask, onehot = pair_tables(bias_table, regions)
     if linked:
-        start, row = 0, jnp.zeros((C,), jnp.float32)
-        for vector in small:
-            size = vector.shape[0]
-            row += jnp.pad(vector.astype(jnp.float32), (start, C - start - size))
-            start += size
-        row = jnp.pad(row.astype(jnp.bfloat16)[None], ((0, 15), (0, 0)))
+        row = jnp.zeros((16, 128), jnp.bfloat16)
+        for first, vector in (
+            (0, first_gain), (1, first_shift), (2, joint_bias), (4, output_bias), (5, second_gain),
+            (6, second_shift), (7, reduce_bias), (8, expand_bias),
+        ):
+            vector = jnp.atleast_2d(vector)
+            height, width = vector.shape
+            row += jnp.pad(vector, ((first, 16 - first - height), (0, 128 - width)))
         weights = (joint_weight, output_weight, expand_weight, reduce_weight, row)
-        joint, probs, mixed, res, vectors, ebias, near, far = attend(x, bias, mask, weights, True)
+        joint, probs, mixed, res, vectors, ebias, near, output, far = attend(x, bias, mask, weights, True)
     else:
         rows = C // ranks
         wide = lambda w: lax.all_gather(w, "dp", axis=0)
-        near = jnp.concatenate(
-            [wide(joint_weight[:, i * C : (i + 1) * C]) for i in range(3)] + [wide(output_weight)], axis=1
-        )
-        row = jnp.concatenate(
-            [lax.all_gather(v, "dp", axis=0, tiled=True).reshape(RANKS, -1) for v in small], axis=1
-        )
-        row = jnp.pad(row[:, None], ((0, 0), (0, 15), (0, C - row.shape[1])))
-        near = jnp.concatenate([regroup(near, 4, rows), row], axis=1)
+        near = jnp.concatenate([wide(joint_weight[:, i * C : (i + 1) * C]) for i in range(3)], axis=1)
+        near, output = regroup(near, 3, rows), regroup(wide(output_weight), 1, rows)
+        pieces = [
+            lax.all_gather(v, "dp", axis=0, tiled=True).reshape(RANKS, 1, -1) for v in small
+        ]
+        row = jnp.concatenate([jnp.pad(v, ((0, 0), (0, 0), (0, 128 - v.shape[2]))) for v in pieces], axis=1)
+        row = jnp.pad(row, ((0, 0), (0, 7), (0, 0)))
         far = jnp.concatenate([wide(expand_weight[:, i * C : (i + 1) * C]) for i in range(4)], axis=1)
         far = jnp.concatenate([regroup(far, 4, rows), wide(reduce_weight).reshape(RANKS, 64, C)], axis=1)
-        joint, probs, mixed, res, vectors, ebias = attend(x, bias, mask, (near,), False)
+        joint, probs, mixed, res, vectors, ebias = attend(x, bias, mask, (near, output, row), False)
     out, rgrad, far_part, far_vec = mlp_block(
-        res.reshape(-1, C), cot, live_slots[:, None], far, vectors, ebias
+        res.reshape(-1, C), cot, live_slots, far, vectors, ebias
     )
     rgrad = rgrad.reshape(SIDE, SIDE, count, C)
     dx, near_part, near_vec, pairs, *far_grads = attend_back(
-        x, near, joint, probs, mixed, rgrad, vectors, far_part, linked
+        x, near, output, joint, probs, mixed, rgrad, vectors, far_part, linked
     )
     table = table_sums(pairs, onehot)
     if linked:
         ge, gr = far_grads
-        gj, go, table, jb, eb, *own = reduce_near(near_part, near_vec, far_vec, table)
+        reduced = reduce_near(near_part, near_vec, far_vec, table)
+        dx, ge, gr, gj, go, table, jb, eb, *own = settle(dx, (ge, gr, *reduced))
         own = [v.reshape(-1) for v in own]
         ob, gain1, shift1, gain2, shift2, rb = own
         eb = eb.reshape(-1)

time: 287 us -> 260 us (0.906)
  Pallas kernels: 259 us -> 240 us
  local copies, waits for them, and re-layouts: 20.5 us -> 12.5 us
    pallas_call x1, Pallas kernels: 77.8 us -> 65.5 us  [attend(): pl.pallas_call(functools.partial(attend_kernel, linked), grid=(PANES,), i...]
    pallas_call x1, Pallas kernels: 83.5 us -> 72.8 us  [attend_back(): pl.pallas_call(functools.partial(attend_back_kernel, linked), grid=(PANES...]
    pallas_call x0 -> x1, Pallas kernels: none -> 6.15 us  [settle(): pl.pallas_call(functools.partial(settle_kernel, 1 + len(others)), grid=(s...]
    unnamed x26 -> x30, local copies, waits for them, and re-layouts: 13.4 us -> 8.08 us
where the time goes in v4:
time: 260 us
  Pallas kernels  240 us (92%)
  local copies, waits for them, and re-layouts  12.5 us (5%)
  matrix products  3.15 us (1%)
  other arithmetic  3.14 us (1%)
    pallas_call x1, Pallas kernels, attend_back(): pl.pallas_call(functools.partial(attend_back_kernel, linked), grid=(PANES...  72.8 us
    pallas_call x1, Pallas kernels, mlp_block(): pl.pallas_call(mlp_kernel, grid=(tokens // rows,), in_specs=[moving, movi...  68.7 us
    pallas_call x1, Pallas kernels, attend(): pl.pallas_call(functools.partial(attend_kernel, linked), grid=(PANES,), i...  65.5 us
    pallas_call x1, Pallas kernels, reduce_near(): pl.pallas_call(reduce_near_kernel, out_shape=[jax.ShapeDtypeStruct((16, 3...  26.6 us
    unnamed x30, local copies, waits for them, and re-layouts  8.08 us
    pallas_call x1, Pallas kernels, settle(): pl.pallas_call(functools.partial(settle_kernel, 1 + len(others)), grid=(s...  6.15 us

profile of v4, /device:TPU:0, one launch (start us, length us, event | category | flops | bytes accessed | tf_op | source)
XLA Modules:
  0.0 259.6 jit_solution(7527666055468809932)
XLA Ops:
  0.7 0.7 slice.17
  1.4 1.4 pad_add_fusion.2.refs_7_
  2.8 0.7 slice.16
  3.5 0.1 slice_add_fusion
  3.6 0.1 pad_add_fusion.1
  3.6 0.1 reshape.230
  3.7 0.1 reshape.231
  3.8 0.1 tile.19
  3.9 0.1 tile.17
  4.0 0.1 add_select_fusion
  4.1 0.1 reshape.251
  4.2 0.0 copy-start.14
  4.2 0.6 copy-done.14
  4.8 1.2 convolution_bitcast_fusion
  6.0 0.1 reshape.228
  6.1 0.5 fusion.3
  6.6 1.0 reshape.229.refs_1_
  7.6 1.0 compare_select_fusion.refs_2_
  8.6 65.5 %attend.1 = (bf16[4,784,1536]{2,1,0:T(8,128)(2,1)}, bf16[4,16,2,224,128]{4,3,2,1,0:T(8,128)(2,1)}, bf16[4,784,512]{2,1,0:T(8,128)(2,1)}, f32[14,14,16,512]{3,2,1...) custom-call(bf16[14,14,16,512]{3,2,1,0:T(8,128)(2,1)} %bitcast.42, ...), custom_call_target="tpu_custom_call" | custom-call | tf_op jit(solution)/shard_map/attend/pallas_call | solution.py:791
  74.1 68.7 %mlp_block.1 = (bf16[3136,512]{1,0:T(8,128)(2,1)}, f32[3136,512]{1,0:T(8,128)}, bf16[32,128,512]{2,1,0:T(8,128)(2,1)}, f32[8,512]{1,0:T(8,128)}) custom-call(f32[3136,512]{1,0:T(8,128)} %bitcast.44, bf16[3136,512]{1,0:T(8,128)(2,1)} %bitcast.47, s32[16]{0:T(128)} %live_ref.1, bf16[32,128,512]{2,1,0:T(8,128)(2,1)} %get-tuple-element.60.far_ref, ...), custom_call_target="tpu_custom_call" | custom-call | tf_op jit(solution)/shard_map/mlp_block/pallas_call | solution.py:481
  142.8 72.8 %attend_back.1 = (bf16[14,14,16,512]{3,2,1,0:T(8,128)(2,1)}, bf16[32,64,512]{2,1,0:T(8,128)(2,1)}, f32[8,512]{1,0:T(8,128)}, f32[2,224,128]{2,1,0:T(8,128)}, f32[16,2048]{1,0:T(8,128)}, /*index=5*/f32[64,512]{1,0:T(8,128)}) custom-call(bf16[14,14,16,512]{3,2,1,0:T(8,128)(2,1)} %bitcast.43, bf16[32,48,512]{2,1,0:T(8,128)(2,1)} %get-tuple-element.64.refs_1_, ...), custom_call_target="tpu_custom_call" | custom-call | tf_op jit(solution)/shard_map/attend_back/pallas_call | solution.py:965
  215.6 0.0 copy-start
  215.6 1.4 reshape.238
  217.0 0.1 reshape.239
  217.2 1.9 fusion.table_ref
  219.1 0.0 copy-done
  219.2 0.0 copy-start.3
  219.2 0.7 copy-done.3
  219.9 0.0 copy-start.4
  219.9 0.7 copy-done.4
  220.6 26.6 %reduce_near.1 = (f32[16,1536]{1,0:T(8,128)S(1)}, f32[16,512]{1,0:T(8,128)S(1)}, f32[16,169]{1,0:T(8,128)S(1)}, f32[2,16]{1,0:T(2,128)S(1)}, f32[1,64]{1,0:T(1,1...) custom-call(bf16[4,2,2,2,64,512]{5,4,3,2,1,0:T(8,128)(2,1)S(1)} %bit, ...), custom_call_target="tpu_custom_call" | custom-call | tf_op jit(solution)/shard_map/reduce_near/pallas_call | solution.py:329
  247.2 0.0 copy-start.1
  247.3 0.6 copy-done.1
  247.9 0.0 copy-start.2
  247.9 0.6 copy-done.2
  248.5 0.0 copy-start.5
  248.5 0.6 copy-done.5
  249.1 0.0 copy-start.6
  249.1 0.5 copy-done.6
  249.6 0.0 copy-start.7
  249.6 0.5 copy-done.7
  250.1 0.0 copy-start.8
  250.1 0.6 copy-done.8
  250.7 0.0 copy-start.9
  250.7 0.5 copy-done.9
  251.2 0.0 copy-start.10
  251.2 0.5 copy-done.10
  251.7 0.0 copy-start.11
  251.7 0.5 copy-done.11
  252.2 0.0 copy-start.12
  252.2 0.5 copy-done.12
  252.7 0.0 copy-start.13
  252.7 0.6 copy-done.13
  253.3 6.2 %settle.1 = (bf16[14,14,16,512]{3,2,1,0:T(8,128)(2,1)}, f32[16,2048]{1,0:T(8,128)}, f32[64,512]{1,0:T(8,128)}, f32[16,1536]{1,0:T(8,128)}, f32[16,512]{1,0:T(8,1...) custom-call(bf16[14,14,16,512]{3,2,1,0:T(8,128)(2,1)} %get-tuple-ele, ...), custom_call_target="tpu_custom_call" | custom-call | tf_op jit(solution)/shard_map/settle/pallas_call | solution.py:358
  (11 shorter events, 0.1 us)
Async XLA Ops:
  4.2 0.6 copy-start.14
  215.6 3.5 %copy-start = (bf16[32,64,512]{2,1,0:T(8,128)(2,1)S(1)}, bf16[32,64,512]{2,1,0:T(8,128)(2,1)}, u32[]{:S(2)}) copy-start(bf16[32,64,512]{2,1,0:T(8,128)(2,1)} %get-tuple-element.74) | copy-start | bytes 6291460
  219.2 0.7 copy-start.3
  219.9 0.7 copy-start.4
  247.2 0.6 copy-start.1
  247.9 0.6 copy-start.2
  248.5 0.6 copy-start.5
  249.1 0.5 copy-start.6
  249.6 0.5 copy-start.7
  250.1 0.6 copy-start.8
  250.7 0.5 copy-start.9
  251.2 0.5 copy-start.10
  251.7 0.5 copy-start.11
  252.2 0.5 copy-start.12
  252.7 0.6 copy-start.13

commit v5 on v4

--- a/solution.py
+++ b/solution.py
@@ -68,17 +68,21 @@
 
 
 class Gather:
-    def __init__(self, place, own, full, send, recv):
+    def __init__(self, place, own, full, send, recv, start=0, rows=None):
         self.place, self.own, self.full, self.send, self.recv = place, own, full, send, recv
+        self.cut = pl.ds(start, full.shape[1] if rows is None else rows)
+
+    def at(self, owner):
+        return self.full.at[owner, self.cut]
 
     def push(self, lane, owner, rank, source=None):
-        source = self.full.at[owner] if source is None else source
-        remote(source, self.full.at[owner], self.send.at[lane], self.recv.at[lane], rank).start()
+        source = self.at(owner) if source is None else source
+        remote(source, self.at(owner), self.send.at[lane], self.recv.at[lane], rank).start()
 
     def some(self, lane):
         place = self.place
         return remote(
-            self.own, self.full.at[place.me], self.send.at[lane], self.recv.at[lane], place.mate
+            self.own, self.at(place.me), self.send.at[lane], self.recv.at[lane], place.mate
         )
 
     def start(self):
@@ -260,38 +264,88 @@
 
 HALVES = 2
 HALF = 64 // HALVES
+CELLS = (2 * WIN - 1) ** 2
+KEYS, QUERIES = 56, 64
+
+
+def seventh(v):
+    return (v * 37) >> 8
+
+
+def offset_onehot():
+    lane = lax.broadcasted_iota(jnp.int32, (1, KEYS * QUERIES), 1)
+    key, query = lane >> 6, lane & 63
+    key_y, query_y = seventh(key), seventh(query)
+    key_x, query_x = key - WIN * key_y, query - WIN * query_y
+    cell = (query_y - key_y + WIN - 1) * (2 * WIN - 1) + query_x - key_x + WIN - 1
+    offset = lax.broadcasted_iota(jnp.int32, (CELLS, KEYS * QUERIES), 0)
+    return jnp.where(offset == cell, 1.0, 0.0).astype(jnp.bfloat16)
+
+
+def reorder(value):
+    row = lax.broadcasted_iota(jnp.int32, (HEADS, HEADS), 0)
+    col = lax.broadcasted_iota(jnp.int32, (HEADS, HEADS), 1)
+    moved = ((row >> 2) & 1) * 8 + (row >> 3) * 4 + (row & 3)
+    order = jnp.where(moved == col, 1.0, 0.0).astype(jnp.bfloat16)
+    return sum(dot_nn(order, piece) for piece in pieces_of(value))
+
+
+def pieces_of(value):
+    high = value.astype(jnp.bfloat16)
+    rest = value - high.astype(jnp.float32)
+    middle = rest.astype(jnp.bfloat16)
+    return high, middle, (rest - middle.astype(jnp.float32)).astype(jnp.bfloat16)
+
+
+def swap_halves(first, second):
+    low = lax.broadcasted_iota(jnp.int32, first.shape, 1) < QUERIES
+    return (
+        jnp.where(low, first, pltpu.roll(second, QUERIES, 1)),
+        jnp.where(low, pltpu.roll(first, QUERIES, 1), second),
+    )
+
+
+def table_sums(pairs, heads):
+    for tile in range(KEYS // 2):
+        upper, lower = swap_halves(
+            pairs[pl.ds(2 * tile, 8, stride=KEYS), :], pairs[pl.ds(2 * tile + 1, 8, stride=KEYS), :]
+        )
+        heads[0:8, tile * 128 : (tile + 1) * 128] = upper
+        heads[8:16, tile * 128 : (tile + 1) * 128] = lower
+    sums = dot_nt(jnp.concatenate(pieces_of(heads[...]), axis=0), offset_onehot())
+    return sums[0:16] + sums[16:32] + sums[32:48]
 
 
 def reduce_near_kernel(
-    parts, near_vec, far_vec, table_ref,
+    parts, near_vec, far_vec, pairs_ref,
     gj_ref, go_ref, table_out, jb_ref, eb_ref, *rest,
 ):
     owns, rest = rest[:6], rest[6:]
-    bias_scratch, spread, rest = rest[0], rest[1], rest[2:]
+    bias_scratch, spread, heads, rest = rest[0], rest[1], rest[2], rest[3:]
     bigs, rest = [rest[i * 10 : i * 10 + 10] for i in range(HALVES)], rest[10 * HALVES :]
     place = Place()
     place.greet()
     bigs = [Reduce(place, parts, scratch, i * HALF) for i, scratch in enumerate(bigs)]
     vec = Swap(place, rest[0:4])
     tab = Swap(place, rest[4:8])
+    vec.own[0, 0:8] = near_vec[...]
+    vec.own[0, 8:16] = far_vec[...]
+    vec.copies(0).start()
     for big in bigs:
         big.start()
-    vec.own[0, 0:8] = near_vec[...]
-    vec.own[0, 8:16] = far_vec[...]
-    tab.own[0] = table_ref[...]
-    vec.copies(0).start()
+    tab.own[0] = table_sums(pairs_ref, heads)
     tab.copies(0).start()
+    vec.hop(0)
     for big in bigs:
         big.cores()
-    vec.hop(0)
     tab.hop(0)
+    vec.hop(1)
     for big in bigs:
         big.sides()
-    vec.hop(1)
     tab.hop(1)
+    vec.hop(2)
     for big in bigs:
         big.corners()
-    vec.hop(2)
     tab.hop(2)
     for i, big in enumerate(bigs):
         total = big.finish()
@@ -303,7 +357,7 @@
             else:
                 go_ref[...] = rows
     sums = vec.finish()
-    table_out[...] = tab.finish()
+    table_out[...] = reorder(tab.finish())
     for tile in range(4):
         spread[tile] = sums[:, tile * 128 : (tile + 1) * 128]
     me = place.me
@@ -321,49 +375,74 @@
     tab.drain()
 
 
-def reduce_near(parts, near_vec, far_vec, table):
+def reduce_near(parts, near_vec, far_vec, pairs):
     one = jax.ShapeDtypeStruct((1, 16), jnp.float32)
     scratch = [pltpu.VMEM((8, 64), jnp.float32), pltpu.VMEM((4, 16, 128), jnp.float32)]
+    scratch += [pltpu.VMEM((HEADS, KEYS * QUERIES), jnp.float32)]
     for _ in range(HALVES):
         scratch += Reduce.scratch(HALF)
+    out_shape = [
+        jax.ShapeDtypeStruct((16, 3 * C), jnp.float32),
+        jax.ShapeDtypeStruct((16, C), jnp.float32),
+        jax.ShapeDtypeStruct((HEADS, CELLS), jnp.float32),
+        jax.ShapeDtypeStruct((2, 16), jnp.float32),
+        jax.ShapeDtypeStruct((1, 64), jnp.float32),
+    ] + [one] * 6
     return pl.pallas_call(
         reduce_near_kernel,
-        out_shape=[
-            jax.ShapeDtypeStruct((16, 3 * C), jnp.float32),
-            jax.ShapeDtypeStruct((16, C), jnp.float32),
-            jax.ShapeDtypeStruct(table.shape, jnp.float32),
-            jax.ShapeDtypeStruct((2, 16), jnp.float32),
-            jax.ShapeDtypeStruct((1, 64), jnp.float32),
-        ]
-        + [one] * 6,
-        in_specs=[pl.BlockSpec(memory_space=pl.ANY)] + [pl.BlockSpec(memory_space=pltpu.VMEM)] * 3,
-        out_specs=[pl.BlockSpec(memory_space=pltpu.VMEM)] * 11,
-        scratch_shapes=scratch + Swap.scratch((16, C)) + Swap.scratch(table.shape),
+        out_shape=out_shape,
+        grid=(1,),
+        in_specs=[pl.BlockSpec(memory_space=pl.ANY)] + [fixed(v.shape) for v in (near_vec, far_vec, pairs)],
+        out_specs=[fixed(v.shape) for v in out_shape],
+        scratch_shapes=scratch + Swap.scratch((16, C)) + Swap.scratch((HEADS, CELLS)),
         compiler_params=pltpu.CompilerParams(
-            collective_id=2, has_side_effects=True, vmem_limit_bytes=40 << 20
+            collective_id=2, has_side_effects=True, vmem_limit_bytes=62 << 20
         ),
         name="reduce_near",
-    )(parts.reshape(4, 2, 2, 2, 64, C), near_vec, far_vec, table)
-
-
-def settle_kernel(count, *refs):
-    for source, target in zip(refs[:count], refs[count:]):
-        target[...] = source[...]
+    )(parts.reshape(4, 2, 2, 2, 64, C), near_vec, far_vec, pairs)
+
+
+def fixed(shape):
+    return pl.BlockSpec(shape, lambda i: (0,) * len(shape), pipeline_mode=pl.Buffered(1))
+
+
+def settle_kernel(count, quarters, *refs):
+    sources, targets, rest = refs[:count], refs[count : 2 * count], refs[2 * count :]
+    held, come, go = rest[:count], rest[count], rest[count + 1]
+    cuts = [slice(None)] * (count - 1) + [pl.ds(2 * i, 2) for i in range(quarters)]
+    index = list(range(1, count)) + [0] * quarters
+    inward = [
+        pltpu.make_async_copy(sources[n].at[cut], held[n].at[cut], come.at[i])
+        for i, (n, cut) in enumerate(zip(index, cuts))
+    ]
+    outward = [
+        pltpu.make_async_copy(held[n].at[cut], targets[n].at[cut], go.at[i])
+        for i, (n, cut) in enumerate(zip(index, cuts))
+    ]
+    for copy in inward:
+        copy.start()
+    for first, then in zip(inward, outward):
+        first.wait()
+        then.start()
+    for copy in outward:
+        copy.wait()
 
 
 def settle(dx, others):
-    steps = SIDE // 2
-    block = pl.BlockSpec((2, SIDE, 16, C), lambda i: (i, 0, 0, 0))
-    whole = [pl.BlockSpec(v.shape, lambda i: (0, 0), pipeline_mode=pl.Buffered(1)) for v in others]
+    anywhere = pl.BlockSpec(memory_space=pl.ANY)
+    arrays = (dx, *others)
+    count, quarters = len(arrays), dx.shape[0] // 2
+    moves = count - 1 + quarters
     return pl.pallas_call(
-        functools.partial(settle_kernel, 1 + len(others)),
-        grid=(steps,),
-        in_specs=[block] + whole,
-        out_specs=[block] + whole,
-        out_shape=[jax.ShapeDtypeStruct(v.shape, v.dtype) for v in (dx, *others)],
-        compiler_params=pltpu.CompilerParams(dimension_semantics=("arbitrary",)),
+        functools.partial(settle_kernel, count, quarters),
+        in_specs=[anywhere] * count,
+        out_specs=[anywhere] * count,
+        out_shape=[jax.ShapeDtypeStruct(v.shape, v.dtype) for v in arrays],
+        scratch_shapes=[pltpu.VMEM(v.shape, v.dtype) for v in arrays]
+        + [pltpu.SemaphoreType.DMA((moves,)), pltpu.SemaphoreType.DMA((moves,))],
+        compiler_params=pltpu.CompilerParams(vmem_limit_bytes=62 << 20),
         name="settle",
-    )(dx, *others)
+    )(*arrays)
 
 ERFC_SLOPE = 0.4
 ERFC_TERMS = (
@@ -377,7 +456,7 @@
 
 
 def gelu_pair(v):
-    bell = jnp.exp(v * v * -0.5)
+    bell = jnp.exp2(v * v * -0.7213475204444817)
     t = 1.0 / (1.0 + jnp.abs(v) * (ERFC_SLOPE * 0.5**0.5))
     tail = ERFC_TERMS[5] * 0.5
     for term in ERFC_TERMS[4::-1]:
@@ -445,21 +524,27 @@
     low = upstream.astype(jnp.bfloat16)
     second_t = second.T
     low_t = low.T
-    for b in range(4):
-        cut = slice(b * C, (b + 1) * C)
-        we = far_ref[:, b * 16 : (b + 1) * 16, :].reshape(C, C)
-        hidden = dot_nn(second, we) + ebias_ref[:, cut]
-        active, slope = gelu_pair(hidden)
-        act[:, cut] = active.astype(jnp.bfloat16)
-        wr = far_ref[b * 8 : (b + 1) * 8, 64:128, :].reshape(C, C)
-        hg[:, cut] = (dot_nt(low, wr) * slope).astype(jnp.bfloat16)
-    reduced = dot_nn(act[...], far_ref[:, 64:128, :].reshape(EXPAND, C))
-    pulled = dot_nt(hg[...], jnp.concatenate([far_ref[:, b * 16 : (b + 1) * 16, :].reshape(C, C) for b in range(4)], axis=1))
-    for b in range(4):
+    we_of = lambda b: far_ref[:, b * 16 : (b + 1) * 16, :].reshape(C, C)
+
+    def weight_grads(b):
         cut = slice(b * C, (b + 1) * C)
         wr_acc[b] += dot_nn(low_t, act[:, cut])
         we_acc[b] += dot_nn(second_t, hg[:, cut])
         vec_ref[3 + b : 4 + b] += column_sum(hg[:, cut].astype(jnp.float32))
+
+    for b in range(8):
+        cut = slice(b * 256, (b + 1) * 256)
+        we = we_of(b // 2)[:, (b % 2) * 256 : (b % 2 + 1) * 256]
+        wr = far_ref[b * 4 : (b + 1) * 4, 64:128, :].reshape(256, C)
+        hidden = dot_nn(second, we) + ebias_ref[:, cut]
+        active, slope = gelu_pair(hidden)
+        act[:, cut] = active.astype(jnp.bfloat16)
+        hg[:, cut] = (dot_nt(low, wr) * slope).astype(jnp.bfloat16)
+        if b % 2 and b > 1:
+            weight_grads(b // 2 - 1)
+    weight_grads(3)
+    reduced = dot_nn(act[...], far_ref[:, 64:128, :].reshape(EXPAND, C))
+    pulled = dot_nt(hg[...], jnp.concatenate([we_of(b) for b in range(4)], axis=1))
     out_ref[...] = (res + reduced + bias_ref[7:8]).astype(jnp.bfloat16)
     rgrad_ref[...] = upstream + norm_pull(pulled, gain, xhat, rate)
     vec_ref[0:1] += column_sum(pulled * xhat)
@@ -566,6 +651,40 @@
     return jnp.broadcast_to(op(parts, axis=1, keepdims=True), parts.shape).reshape(value.shape)
 
 
+def build_bias(table_ref, pair_bias):
+    heads = dot_nn(table_ref[...], offset_onehot())
+    heads = reorder(heads)
+    for tile in range(KEY_ROWS // 2):
+        part = heads[:, tile * 128 : (tile + 1) * 128]
+        for key, value in enumerate(swap_halves(part[0:8], part[8:16]), 2 * tile):
+            if key >= SPOTS:
+                value = jnp.full(value.shape, -1e30, jnp.float32)
+            pair_bias[pl.ds(key, 8, stride=KEY_ROWS), :] = value
+
+
+def place_in(pane, spot):
+    down = seventh(spot)
+    y = (pane // 2) * WIN + down + SHIFT
+    x = lax.rem(pane, 2) * WIN + spot - WIN * down + SHIFT
+    return jnp.where(y >= SIDE, y - SIDE, y), jnp.where(x >= SIDE, x - SIDE, x)
+
+
+def pane_mask(pane, regions_ref):
+    labels = regions_ref[...].astype(jnp.float32).astype(jnp.bfloat16)
+    row = lax.broadcasted_iota(jnp.int32, (PAIR_SHAPE[0], SIDE), 0)
+    key = row - KEY_ROWS * ((row * 1171) >> 16)
+    y, x = place_in(pane, key)
+    col = lax.broadcasted_iota(jnp.int32, row.shape, 1)
+    lines = dot_nn(jnp.where(col == y, 1.0, 0.0).astype(jnp.bfloat16), labels)
+    keys = jnp.sum(jnp.where(col == x, lines, 0.0), axis=1, keepdims=True)
+    query = lax.broadcasted_iota(jnp.int32, (SIDE, PAIR_SHAPE[1]), 1) & (QUERY_ROWS - 1)
+    y, x = place_in(pane, query)
+    row = lax.broadcasted_iota(jnp.int32, query.shape, 0)
+    lines = dot_nn(labels, jnp.where(row == x, 1.0, 0.0).astype(jnp.bfloat16))
+    queries = jnp.sum(jnp.where(row == y, lines, 0.0), axis=0, keepdims=True)
+    return jnp.where(keys == queries, 0.0, -100.0)
+
+
 def bias_rows(rows, vec_ref, ebias_ref):
     values = rows[...].astype(jnp.float32)
 
@@ -583,7 +702,7 @@
 
 
 def attend_kernel(linked, *refs):
-    x_ref, bias_ref, mask_ref, *refs = refs
+    x_ref, table_ref, regions_ref, *refs = refs
     if linked:
         shards, refs = refs[:5], refs[5:]
     else:
@@ -591,20 +710,21 @@
     joint_ref, probs_ref, mixed_ref, res_ref, vec_ref, ebias_ref, *refs = refs
     if linked:
         near_out, output_out, far_out, *refs = refs
-    window, wide, blend, both, score_a, score_b, probs_a, probs_b, *refs = refs
+    window, wide, blend, both, score_a, score_b, probs_a, probs_b, pair_bias, *refs = refs
     pane = pl.program_id(0)
     last = pl.num_programs(0) - 1
     if linked:
         near, rows, output, far_own, local, *sems = refs
         place = Place()
-        close = Gather(place, near.at[place.me], near, *sems[0:2])
-        little = Gather(place, rows.at[place.me], rows, *sems[2:4])
-        middle = Gather(place, output.at[place.me], output, *sems[4:6])
-        distant = Gather(place, far_own, far_out, *sems[6:8])
         joint_w, output_w, expand_w, reduce_w, row_w = shards
-        pieces = [
-            (joint_w.at[:, b * C : (b + 1) * C], near.at[place.me].at[b * 16 : (b + 1) * 16]) for b in range(3)
+        blocks = [joint_w.at[:, b * C : (b + 1) * C] for b in range(3)]
+        close = [
+            Gather(place, blocks[b], near, *sems[2 * b : 2 * b + 2], 16 * b, 16) for b in range(3)
         ]
+        little = Gather(place, row_w, rows, *sems[6:8])
+        middle = Gather(place, output_w, output, *sems[8:10])
+        distant = Gather(place, far_own, far_out, *sems[10:12])
+        pieces = [(blocks[b], close[b].at(place.me)) for b in range(3)]
         pieces += [(row_w, rows.at[place.me]), (output_w, output.at[place.me])]
         pieces += [
             (expand_w.at[:, b * C : (b + 1) * C], far_own.at[b * 16 : (b + 1) * 16]) for b in range(4)
@@ -620,31 +740,31 @@
             for piece in pieces:
                 piece.start()
             place.greet()
-            for piece in pieces[:4]:
-                piece.wait()
-            close.start()
             little.start()
-            for piece in pieces[4:]:
-                piece.wait()
-            middle.start()
-            keep[2].start()
+            for group in close:
+                group.start()
+        build_bias(table_ref, pair_bias)
         wide[:, ROWS:, :] = jnp.zeros((12, QUERY_ROWS * 16 - ROWS, QUAD), jnp.float32)
         probs_b[...] = jnp.zeros_like(probs_b)
         if linked:
-            close.relay_columns()
             little.relay_columns()
-            close.relay_sides()
+            for group in close:
+                group.relay_columns()
+            middle.start()
             little.relay_sides()
-            middle.relay_columns()
-            distant.start()
-            close.relay_corners()
+            for group in close:
+                group.relay_sides()
             little.relay_corners()
+            for piece in pieces:
+                piece.wait()
             little.finish()
         bias_rows(rows, vec_ref, ebias_ref)
         if linked:
-            close.finish()
-            keep[0].start()
-            middle.relay_sides()
+            for group in close:
+                group.relay_corners()
+            middle.relay_columns()
+            distant.start()
+            keep[2].start()
 
     if linked:
         @pl.when(pane == 1)
@@ -665,6 +785,14 @@
     xhat, _ = norm_parts(source)
     normed = (xhat * vec_ref[0:1] + vec_ref[1:2]).astype(jnp.bfloat16)
     for b in range(3):
+        if linked:
+            @pl.when(pane == 0)
+            def _():
+                close[b].finish()
+                if b == 2:
+                    keep[0].start()
+                    middle.relay_sides()
+
         weight = near[:, b * 16 : (b + 1) * 16, :].reshape(C, C)
         block = dot_nn(normed, weight)
         if b != 1:
@@ -672,8 +800,9 @@
         block = block.astype(jnp.bfloat16)
         joint_ref[0, :, b * C : (b + 1) * C] = block
         put_tiles(wide, b * 4, block.astype(jnp.float32))
+    mask = pane_mask(pane, regions_ref)
     for pair in range(2):
-        both[pair] = bias_ref[pair] + mask_ref[0]
+        both[pair] = pair_bias[pair * PAIR_SHAPE[0] : (pair + 1) * PAIR_SHAPE[0]] + mask
 
     def rows_of(m):
         return pl.ds(m, QUERY_ROWS, stride=16), pl.ds(m, KEY_ROWS, stride=16)
@@ -732,7 +861,7 @@
         @pl.when(pane == last)
         def _():
             distant.finish()
-            for group in (close, little, middle, distant):
+            for group in (*close, little, middle, distant):
                 group.drain()
             for kept in keep:
                 kept.wait()
@@ -746,7 +875,7 @@
     return pl.BlockSpec((1,) + shape, lambda i: (i,) + (0,) * len(shape))
 
 
-def attend(x, bias, mask, weights, linked):
+def attend(x, table, regions, weights, linked):
     anywhere = pl.BlockSpec(memory_space=pl.ANY)
     out_specs = [stepped((ROWS, 3 * C)), stepped((16, 2) + PAIR_SHAPE), stepped((ROWS, C)),
                  fixed((SIDE, SIDE, 16, C)), fixed((8, C)), fixed((1, EXPAND))]
@@ -767,8 +896,9 @@
         pltpu.VMEM((2,) + PAIR_SHAPE, jnp.float32),
         pltpu.VMEM((2,) + PAIR_SHAPE, jnp.bfloat16),
         pltpu.VMEM((2,) + PAIR_SHAPE, jnp.bfloat16),
+        pltpu.VMEM((2 * PAIR_SHAPE[0], PAIR_SHAPE[1]), jnp.float32),
     ]
-    in_specs = [fixed((SIDE, SIDE, 16, C)), fixed((2,) + PAIR_SHAPE), stepped(PAIR_SHAPE)]
+    in_specs = [fixed((SIDE, SIDE, 16, C)), fixed(table.shape), fixed(regions.shape)]
     if linked:
         in_specs += [anywhere] * 5
         out_specs += [anywhere] * 3
@@ -783,7 +913,7 @@
             pltpu.VMEM((RANKS, 16, C), jnp.bfloat16),
             pltpu.VMEM((FAR, C), jnp.bfloat16),
             pltpu.SemaphoreType.DMA((13,)),
-        ] + [pltpu.SemaphoreType.DMA((31,))] * 8
+        ] + [pltpu.SemaphoreType.DMA((31,))] * 12
         extra = dict(collective_id=0, has_side_effects=True)
     else:
         in_specs += [fixed((RANKS, NEAR, C)), fixed((RANKS, 16, C)), fixed((RANKS, 16, 128))]
@@ -799,7 +929,7 @@
             vmem_limit_bytes=62 << 20, dimension_semantics=("arbitrary",), **extra
         ),
         name="attend",
-    )(x, bias, mask, *weights)
+    )(x, table, regions, *weights)
 
 
 def attend_back_kernel(linked, *refs):
@@ -974,34 +1104,6 @@
         ),
         name="attend_back",
     )(*operands)
-
-
-def pair_tables(bias_table, regions):
-    keys, queries = jnp.arange(KEY_ROWS), jnp.arange(QUERY_ROWS)
-    real = (keys < SPOTS)[:, None] & (queries < SPOTS)[None, :]
-    cells = (
-        (queries[None, :] // WIN - keys[:, None] // WIN + WIN - 1) * (2 * WIN - 1)
-        + queries[None, :] % WIN - keys[:, None] % WIN + WIN - 1
-    )
-    cells = jnp.where(real, cells, -1).reshape(-1)
-    onehot = (cells[None, :] == jnp.arange((2 * WIN - 1) ** 2)[:, None]).astype(jnp.bfloat16)
-    bias = dot_tn(bias_table, onehot).reshape(2, 2, 4, KEY_ROWS, QUERY_ROWS)
-    bias = jnp.where((keys < SPOTS)[:, None], bias, -1e30)
-    bias = bias.transpose(0, 2, 3, 1, 4).reshape((2,) + PAIR_SHAPE)
-    labels = jnp.roll(regions, (-SHIFT, -SHIFT), axis=(0, 1)).reshape(2, WIN, 2, WIN)
-    labels = labels.transpose(0, 2, 1, 3).reshape(PANES, SPOTS)
-    along = jnp.tile(jnp.pad(labels, ((0, 0), (0, KEY_ROWS - SPOTS))), (1, 4))
-    across = jnp.tile(jnp.pad(labels, ((0, 0), (0, QUERY_ROWS - SPOTS))), (1, 2))
-    mask = jnp.where(along[:, :, None] == across[:, None, :], 0.0, -100.0).astype(jnp.float32)
-    return bias, mask, onehot
-
-
-def table_sums(pairs, onehot):
-    heads = pairs.reshape(2, 4, KEY_ROWS, 2, QUERY_ROWS).transpose(0, 3, 1, 2, 4)
-    return lax.dot_general(
-        heads.reshape(HEADS, KEY_ROWS * QUERY_ROWS), onehot.astype(jnp.float32), (((1,), (1,)), ((), ())),
-        precision=exact_mode, preferred_element_type=jnp.float32,
-    )
 
 def regroup(packed, blocks, rows):
     count = packed.shape[0] // RANKS
@@ -1053,7 +1155,6 @@
     )
     x = images.transpose(1, 2, 0, 3)
     cot = cotangent.transpose(1, 2, 0, 3).reshape(-1, C)
-    bias, mask, onehot = pair_tables(bias_table, regions)
     if linked:
         row = jnp.zeros((16, 128), jnp.bfloat16)
         for first, vector in (
@@ -1064,7 +1165,7 @@
             height, width = vector.shape
             row += jnp.pad(vector, ((first, 16 - first - height), (0, 128 - width)))
         weights = (joint_weight, output_weight, expand_weight, reduce_weight, row)
-        joint, probs, mixed, res, vectors, ebias, near, output, far = attend(x, bias, mask, weights, True)
+        joint, probs, mixed, res, vectors, ebias, near, output, far = attend(x, bias_table.T, regions, weights, True)
     else:
         rows = C // ranks
         wide = lambda w: lax.all_gather(w, "dp", axis=0)
@@ -1077,7 +1178,7 @@
         row = jnp.pad(row, ((0, 0), (0, 7), (0, 0)))
         far = jnp.concatenate([wide(expand_weight[:, i * C : (i + 1) * C]) for i in range(4)], axis=1)
         far = jnp.concatenate([regroup(far, 4, rows), wide(reduce_weight).reshape(RANKS, 64, C)], axis=1)
-        joint, probs, mixed, res, vectors, ebias = attend(x, bias, mask, (near, output, row), False)
+        joint, probs, mixed, res, vectors, ebias = attend(x, bias_table.T, regions, (near, output, row), False)
     out, rgrad, far_part, far_vec = mlp_block(
         res.reshape(-1, C), cot, live_slots, far, vectors, ebias
     )
@@ -1085,10 +1186,10 @@
     dx, near_part, near_vec, pairs, *far_grads = attend_back(
         x, near, output, joint, probs, mixed, rgrad, vectors, far_part, linked
     )
-    table = table_sums(pairs, onehot)
+    pairs = pairs.reshape(-1, pairs.shape[-1])
     if linked:
         ge, gr = far_grads
-        reduced = reduce_near(near_part, near_vec, far_vec, table)
+        reduced = reduce_near(near_part, near_vec, far_vec, pairs)
         dx, ge, gr, gj, go, table, jb, eb, *own = settle(dx, (ge, gr, *reduced))
         own = [v.reshape(-1) for v in own]
         ob, gain1, shift1, gain2, shift2, rb = own
@@ -1103,6 +1204,11 @@
         ob, qb, vb, gain1, shift1 = [scatter(near_vec[i]) for i in range(5)]
         gain2, shift2, rb = [scatter(far_vec[i]) for i in range(3)]
         eb, jb = scatter(far_vec[3:7].reshape(-1)), jnp.stack([qb, vb])
+        heads = pairs.reshape(2, 4, KEY_ROWS, 2, QUERY_ROWS).transpose(0, 3, 1, 2, 4).reshape(HEADS, -1)
+        table = lax.dot_general(
+            heads, offset_onehot().astype(jnp.float32), (((1,), (1,)), ((), ())),
+            precision=exact_mode, preferred_element_type=jnp.float32,
+        )
         table = lax.psum(table, "dp")
     image_order = lambda v: v.reshape(SIDE, SIDE, count, C).transpose(2, 0, 1, 3)
     return (

time: 260 us -> 239 us (0.919)
  local copies, waits for them, and re-layouts: 12.5 us -> 0 us
  Pallas kernels: 240 us -> 236 us
  matrix products: 3.15 us -> 0 us
    unnamed x30 -> x0, local copies, waits for them, and re-layouts: 8.08 us -> none
    pallas_call x1, Pallas kernels: 68.7 us -> 64.9 us  [mlp_block(): pl.pallas_call(mlp_kernel, grid=(tokens // rows,), in_specs=[moving, movi...]
    dot_general x2 -> x0, matrix products: 3.15 us -> none  [the longest x1 1.95 us: table_sums(): lax.dot_general(heads.reshape(HEADS, KEY_ROWS * QUERY_ROWS), onehot.astyp...]
    reshape x8 -> x0, local copies, waits for them, and re-layouts: 2.78 us -> none  [the longest x2 1.39 us: table_sums(): pairs.reshape(2, 4, KEY_ROWS, 2, QUERY_ROWS).transpose(0, 3, 1, 2, 4)]
    pallas_call x2, Pallas kernels: 32.8 us -> 30.1 us  [the longest x1 26.5 us: reduce_near(): pl.pallas_call(reduce_near_kernel, out_shape=out_shape, grid=(1,), in_spe...]
where the time goes in v5:
time: 239 us
  Pallas kernels  236 us (99%)
    pallas_call x1, Pallas kernels, attend_back(): pl.pallas_call(functools.partial(attend_back_kernel, linked), grid=(PANES...  74 us
    pallas_call x1, Pallas kernels, attend(): pl.pallas_call(functools.partial(attend_kernel, linked), grid=(PANES,), i...  67.3 us
    pallas_call x1, Pallas kernels, mlp_block(): pl.pallas_call(mlp_kernel, grid=(tokens // rows,), in_specs=[moving, movi...  64.9 us
    pallas_call x1, Pallas kernels, reduce_near(): pl.pallas_call(reduce_near_kernel, out_shape=out_shape, grid=(1,), in_spe...  26.5 us

profile of v5, /device:TPU:0, one launch (start us, length us, event | category | flops | bytes accessed | tf_op | source)
XLA Modules:
  0.0 238.5 jit_solution(12196365409062153625)
XLA Ops:
  0.6 1.4 pad_add_fusion.refs_7_
  2.0 67.3 %attend.1 = (bf16[4,784,1536]{2,1,0:T(8,128)(2,1)}, bf16[4,16,2,224,128]{4,3,2,1,0:T(8,128)(2,1)}, bf16[4,784,512]{2,1,0:T(8,128)(2,1)}, f32[14,14,16,512]{3,2,1...) custom-call(bf16[14,14,16,512]{3,2,1,0:T(8,128)(2,1)} %bitcast.29, ...), custom_call_target="tpu_custom_call" | custom-call | tf_op jit(solution)/shard_map/attend/pallas_call | solution.py:921
  69.3 64.9 %mlp_block.1 = (bf16[3136,512]{1,0:T(8,128)(2,1)}, f32[3136,512]{1,0:T(8,128)}, bf16[32,128,512]{2,1,0:T(8,128)(2,1)}, f32[8,512]{1,0:T(8,128)}) custom-call(f32[3136,512]{1,0:T(8,128)} %bitcast.31, bf16[3136,512]{1,0:T(8,128)(2,1)} %bitcast.34, s32[16]{0:T(128)} %live_ref.1, bf16[32,128,512]{2,1,0:T(8,128)(2,1)} %get-tuple-element.60.far_ref, ...), custom_call_target="tpu_custom_call" | custom-call | tf_op jit(solution)/shard_map/mlp_block/pallas_call | solution.py:566
  134.2 74.0 %attend_back.1 = (bf16[14,14,16,512]{3,2,1,0:T(8,128)(2,1)}, bf16[32,64,512]{2,1,0:T(8,128)(2,1)}, f32[8,512]{1,0:T(8,128)}, f32[2,224,128]{2,1,0:T(8,128)}, f32[16,2048]{1,0:T(8,128)}, /*index=5*/f32[64,512]{1,0:T(8,128)}) custom-call(bf16[14,14,16,512]{3,2,1,0:T(8,128)(2,1)} %bitcast.30, bf16[32,48,512]{2,1,0:T(8,128)(2,1)} %get-tuple-element.64.refs_1_, ...), custom_call_target="tpu_custom_call" | custom-call | tf_op jit(solution)/shard_map/attend_back/pallas_call | solution.py:1095
  208.2 26.5 %reduce_near.1 = (f32[16,1536]{1,0:T(8,128)}, f32[16,512]{1,0:T(8,128)}, f32[16,169]{1,0:T(8,128)}, f32[2,16]{1,0:T(2,128)}, f32[1,64]{1,0:T(1,128)}, /*index=5*...) custom-call(bf16[4,2,2,2,64,512]{5,4,3,2,1,0:T(8,128)(2,1)} %bitcast, ...), custom_call_target="tpu_custom_call" | custom-call | tf_op jit(solution)/shard_map/reduce_near/pallas_call | solution.py:391
  234.8 3.6 %settle.1 = (bf16[14,14,16,512]{3,2,1,0:T(8,128)(2,1)}, f32[16,2048]{1,0:T(8,128)}, f32[64,512]{1,0:T(8,128)}, f32[16,1536]{1,0:T(8,128)}, f32[16,512]{1,0:T(8,1...) custom-call(bf16[14,14,16,512]{3,2,1,0:T(8,128)(2,1)} %get-tuple-ele, ...), custom_call_target="tpu_custom_call" | custom-call | tf_op jit(solution)/shard_map/settle/pallas_call | solution.py:436
